TPU v7x, 256 devices: a whole 4x4x8 slice. The times are simulated.
256 devices in a mesh: blocks: 64 (over x, z, core), gz: 4 (over y).
Axes of the slice: x: 4, y: 4, z: 8, core: 2. Of those that a mesh axis runs over, the one named last changes fastest.
Arguments:
- coarse_field: float32 [4, 1024, 3, 4096], P('gz', 'blocks'), may hold values from -6 to 6
- coarse_velocity: float32 [4, 1024, 3, 4096], P('gz', 'blocks'), may hold values from -15 to 15
- fine_field: float32 [4, 768, 3, 4096], P('gz', 'blocks'), may hold values from -6 to 6
- fine_velocity: float32 [4, 768, 3, 4096], P('gz', 'blocks'), may hold values from -15 to 15
- pairs: int32 [4, 2048, 6], P('gz', 'blocks'), may hold values from 0 to 63, as said below
Outputs:
- coarse_new: float32 [4, 1024, 3, 4096], P('gz', 'blocks')
- fine_new: float32 [4, 768, 3, 4096], P('gz', 'blocks')
- face_jump: float32 [4, 2048, 256], P('gz', 'blocks')
Inputs may be any that keep to these rules, and one draw needn't show every extreme that they name: `pairs`: Columns: fine slot below 12, face axis 0 to 2, owner device below 64, coarse slot below 16, quadrant row and column 0 or 1. No two rows of a device name the same fine slot and face axis, and no two rows of a group name the same coarse block, face axis and quadrant. The rows of one device name one owner device at most 2 times, and exactly 2 times for some owner; rows of one device that name the same owner differ in face axis; some owner is named 2 times by every device of its group. Each face axis stands in 10 to 11 of a device's rows.
All inputs are finite; a program needn't handle non-finite values.
Results may differ from a plain program's by a relative error of at most 0.0003.
Values sent between devices are 32-bit elements; how exact they have to be, the bound alone decides.
No kernel may reach another device: no remote copies, remote signals or barrier semaphores. Data moves between devices by JAX's collectives and lax.ppermute only.
A program may use at most 256 MiB of HBM per device.

v0:
```python
import jax
import jax.numpy as jnp
import numpy as np
from jax import lax
from jax.experimental import pallas as pl
from jax.experimental.pallas import tpu as pltpu
from jax.sharding import Mesh
from jax.sharding import PartitionSpec as P

EDGE = 16
HALF = 8
CB = 16
FB = 12
PAIRS = 32
PEERS = 64
WIDE = EDGE * EDGE
CELLS = EDGE**3
PITCH = 104
BLOCKS = ("blocks_0", "blocks_1", "blocks_2")
F32 = jnp.float32
BF16 = jnp.bfloat16
TANGENT = ((1, 2), (0, 2), (0, 1))


def _face_lane(row, col, flip):
    return col * EDGE + row if flip else row * EDGE + col


def _restrict_matrix(flip):
    out = np.zeros((2, WIDE, 128), np.float32)
    for m in range(HALF):
        for n in range(HALF):
            o = m * HALF + n
            out[0, _face_lane(2 * m, 2 * n, flip), o] = 0.5
            out[0, _face_lane(2 * m + 1, 2 * n, flip), o] = 0.5
            out[1, _face_lane(2 * m, 2 * n, flip), 64 + o] = 0.5
            out[1, _face_lane(2 * m, 2 * n + 1, flip), 64 + o] = 0.5
    return out.reshape(2 * WIDE, 128)


def _expand_matrix(flip):
    out = np.zeros((128, 256), np.float32)
    for m in range(HALF):
        for n in range(HALF):
            o = m * HALF + n
            out[o, _face_lane(m, n, flip)] = 1.0
            out[64 + o, 128 + _face_lane(m, n, flip)] = 1.0
    return out


def _quadrant_matrix(flip):
    out = np.zeros((WIDE, WIDE), np.float32)
    for row in range(EDGE):
        for col in range(EDGE):
            quad = (row // HALF) * 2 + col // HALF
            out[_face_lane(row, col, flip), quad * 64 + (row % HALF) * HALF + col % HALF] = 1.0
    return out


def _flip_matrix():
    out = np.zeros((WIDE, WIDE), np.float32)
    for row in range(EDGE):
        for col in range(EDGE):
            out[_face_lane(row, col, True), _face_lane(row, col, False)] = 1.0
    return out


def _prolong_matrix():
    out = np.zeros((128, WIDE), np.float32)
    for row in range(EDGE):
        for col in range(EDGE):
            o = (row // 2) * HALF + col // 2
            out[o, _face_lane(row, col, False)] = 1.0
            out[64 + o, _face_lane(row, col, False)] = 1.0
    return out


RESTRICT = np.stack([_restrict_matrix(False), _restrict_matrix(True)])
EXPAND = np.stack([_expand_matrix(False), _expand_matrix(True)])
QUADRANT = np.stack([_quadrant_matrix(False), _quadrant_matrix(True)])
FLIP = _flip_matrix()
PROLONG = _prolong_matrix()


def halves(value):
    high = value.astype(BF16)
    return high, (value - high.astype(F32)).astype(BF16)


def mm(a, b, dims=((1,), (0,))):
    return lax.dot_general(a, b, (dims, ((), ())), preferred_element_type=F32)


def mm_left(value, matrix, dims=((1,), (0,))):
    high, low = halves(value)
    return mm(high, matrix, dims) + mm(low, matrix, dims)


def mm_right(matrix, value, dims=((1,), (0,))):
    high, low = halves(value)
    return mm(matrix, high, dims) + mm(matrix, low, dims)


def lanes_of(value):
    return lax.broadcasted_iota(jnp.int32, value.shape, 1)


def y_prev(p):
    a, b = pltpu.roll(p[0], 16, 1), pltpu.roll(p[1], 16, 1)
    edge = lanes_of(a) < 16
    return jnp.where(edge, b, a), jnp.where(edge, a, b)


def y_next(p):
    a, b = pltpu.roll(p[0], 112, 1), pltpu.roll(p[1], 112, 1)
    edge = lanes_of(a) >= 112
    return jnp.where(edge, b, a), jnp.where(edge, a, b)


def z_prev(p):
    edge = (lanes_of(p[0]) & 15) == 0
    return tuple(jnp.where(edge, pltpu.roll(x, 113, 1), pltpu.roll(x, 1, 1)) for x in p)


def z_next(p):
    edge = (lanes_of(p[0]) & 15) == 15
    return tuple(jnp.where(edge, pltpu.roll(x, 15, 1), pltpu.roll(x, 127, 1)) for x in p)


def each(fn, *pairs):
    return tuple(fn(*(p[h] for p in pairs)) for h in range(2))


def slab(ref, comp, i, first, count):
    base = pl.multiple_of(i * WIDE, 128)
    return (
        ref[comp, first : first + count, pl.ds(base, 128)],
        ref[comp, first : first + count, pl.ds(pl.multiple_of(base + 128, 128), 128)],
    )


def put_slab(ref, comp, i, first, count, value):
    base = pl.multiple_of(i * WIDE, 128)
    ref[comp, first : first + count, pl.ds(base, 128)] = value[0]
    ref[comp, first : first + count, pl.ds(pl.multiple_of(base + 128, 128), 128)] = value[1]


def fine_slab(ref, comp, i):
    def one(half):
        start = comp * 32 + 2 * i + half
        return jnp.concatenate(
            [
                ref[pl.ds(start, 8, stride=PITCH), :],
                ref[pl.ds(start + 8 * PITCH, 8, stride=PITCH), :],
            ],
            axis=0,
        )

    return one(0), one(1)


def put_fine_slab(ref, comp, i, value):
    for half in range(2):
        start = comp * 32 + 2 * i + half
        ref[pl.ds(start, 8, stride=PITCH), :] = value[half][0:8]
        ref[pl.ds(start + 8 * PITCH, 8, stride=PITCH), :] = value[half][8:16]


def fetch_fine(source, target, sem):
    return [
        pltpu.make_async_copy(source.at[b], target.at[pl.ds(b * PITCH, 96)], sem)
        for b in range(FB)
    ]


def face_row_wise(load):
    def step(i, held):
        turned = pltpu.roll(load(i), (i % 8) * 16, 1)
        place = (lanes_of(turned) // 16) == i % 8
        upper = jnp.broadcast_to(i >= 8, turned.shape)
        return (
            jnp.where(place & ~upper, turned, held[0]),
            jnp.where(place & upper, turned, held[1]),
        )

    zero = jnp.zeros((CB, 128), F32)
    return lax.fori_loop(0, EDGE, step, (zero, zero))


def face_column_wise(load):
    def step(i, held):
        both = load(i)
        place = (lanes_of(both[0]) & 15) == i
        return each(lambda x, h: jnp.where(place, pltpu.roll(x, i, 1), h), both, held)

    zero = jnp.zeros((CB, 128), F32)
    return lax.fori_loop(0, EDGE, step, (zero, zero))


def routes(pairs_ref):
    slot, face, owner = pairs_ref[0], pairs_ref[1], pairs_ref[2]
    peer = lax.broadcasted_iota(jnp.int32, (PEERS, PAIRS), 0)
    named = (owner == peer).astype(F32)
    before = (
        lax.broadcasted_iota(jnp.int32, (PAIRS, PAIRS), 0)
        < lax.broadcasted_iota(jnp.int32, (PAIRS, PAIRS), 1)
    ).astype(F32)
    earlier = mm(named.astype(BF16), before.astype(BF16))
    rank = jnp.sum(named * earlier, axis=0, keepdims=True)
    first = jnp.where(rank < 0.5, named, 0.0)
    second = jnp.where(rank < 0.5, 0.0, named)
    at_row = lax.broadcasted_iota(jnp.int32, (3 * CB, PAIRS), 0)
    source = (face * CB + slot == at_row).astype(F32)
    return first, second, source


def first_kernel(
    cb, cv, fb, fv, pairs, restrict, send, speed, emf, scb, scv, sfb, sfv, cell, sems
):
    fine_copies = fetch_fine(fb, sfb, sems.at[0]) + fetch_fine(fv, sfv, sems.at[1])
    for copy in fine_copies:
        copy.start()
    coarse_copies = [
        pltpu.make_async_copy(cb, scb, sems.at[2]),
        pltpu.make_async_copy(cv, scv, sems.at[3]),
    ]
    for copy in coarse_copies:
        copy.start()
    idle = pl.ds(FB * PITCH, (CB - FB) * PITCH)
    sfb[idle, :] = jnp.zeros(((CB - FB) * PITCH, 128), F32)
    sfv[idle, :] = jnp.zeros(((CB - FB) * PITCH, 128), F32)

    def cells(load_b, load_v, first):
        def step(i, top):
            following = lax.rem(i + 1, EDGE)
            bx, by, bz = load_b(0, i), load_b(1, i), load_b(2, i)
            vx, vy, vz = load_v(0, i), load_v(1, i), load_v(2, i)
            mean = lambda a, b: 0.5 * (a + b)
            cx = each(mean, bx, load_b(0, following))
            cy = each(mean, by, y_next(by))
            cz = each(mean, bz, z_next(bz))
            put_slab(cell, 0, i, first, CB, each(lambda a, b, c, d: a * b - c * d, vz, cy, vy, cz))
            put_slab(cell, 1, i, first, CB, each(lambda a, b, c, d: a * b - c * d, vx, cz, vz, cx))
            put_slab(cell, 2, i, first, CB, each(lambda a, b, c, d: a * b - c * d, vy, cx, vx, cy))
            size = lambda a, b, c: jnp.sqrt(a * a + b * b + c * c)
            fast = each(lambda a, b: a + b, each(size, vx, vy, vz), each(size, cx, cy, cz))
            return jnp.maximum(top, jnp.maximum(fast[0], fast[1]))

        return lax.fori_loop(0, EDGE, step, jnp.zeros((CB, 128), F32))

    def edges(first):
        def step(i, carry):
            prior = lax.rem(i + EDGE - 1, EDGE)
            add = lambda a, b: a + b
            quarter = lambda a, b: 0.25 * (a + b)
            ex = slab(cell, 0, i, first, CB)
            sum_x = each(add, ex, y_prev(ex))
            put_slab(emf, 0, i, first, CB, each(quarter, sum_x, z_prev(sum_x)))
            sum_y = each(add, slab(cell, 1, i, first, CB), slab(cell, 1, prior, first, CB))
            put_slab(emf, 1, i, first, CB, each(quarter, sum_y, z_prev(sum_y)))
            sum_z = each(add, slab(cell, 2, i, first, CB), slab(cell, 2, prior, first, CB))
            put_slab(emf, 2, i, first, CB, each(quarter, sum_z, y_prev(sum_z)))
            return carry

        lax.fori_loop(0, EDGE, step, 0)

    for copy in fine_copies:
        copy.wait()
    top_fine = cells(lambda c, i: fine_slab(sfb, c, i), lambda c, i: fine_slab(sfv, c, i), CB)
    edges(CB)

    first, second, source = routes(pairs)
    rows = []
    for d in range(3):
        planes = []
        for along in TANGENT[d]:
            if d == 0:
                planes.append(slab(emf, along, 0, CB, CB))
            elif d == 1:
                planes.append(face_row_wise(lambda i: slab(emf, along, i, CB, CB)[0]))
            else:
                planes.append(face_column_wise(lambda i: slab(emf, along, i, CB, CB)))
        both = jnp.concatenate([*planes[0], *planes[1]], axis=1)
        rows.append(mm_left(both, restrict[1 if d == 2 else 0]))
    rows = jnp.concatenate(rows, axis=0)
    nt = ((1,), (1,))
    key = (pairs[1] * 64 + (pairs[4] * 2 + pairs[5]) * CB + pairs[3] + 1).astype(F32)
    lane = lax.broadcasted_iota(jnp.int32, (PEERS, 128), 1)
    meta = jnp.zeros((PEERS, 128), F32)
    for k, chosen in enumerate((first, second)):
        pick = mm(chosen.astype(BF16), source.astype(BF16), nt)
        send[:, 0, k * 128 : (k + 1) * 128] = mm_right(pick.astype(BF16), rows)
        meta = jnp.where(lane == k, jnp.sum(chosen * key, axis=1, keepdims=True), meta)
    send[:, 0, 256:384] = meta

    for copy in coarse_copies:
        copy.wait()
    top_coarse = cells(lambda c, i: slab(scb, c, i, 0, CB), lambda c, i: slab(scv, c, i, 0, CB), 0)
    edges(0)
    top = jnp.max(jnp.maximum(top_fine, top_coarse), axis=0, keepdims=True)
    speed[...] = jnp.broadcast_to(jnp.max(top, axis=1, keepdims=True), (1, 128))


def second_kernel(
    got, cb, fb, emf_in, expand, quadrant, new_c, new_f, back, normals, sfb, emf, out_f, sems
):
    copies = fetch_fine(fb, sfb, sems.at[0])
    for copy in copies:
        copy.start()
    load_emf = pltpu.make_async_copy(emf_in, emf, sems.at[1])
    load_emf.start()
    idle = pl.ds(FB * PITCH, (CB - FB) * PITCH)
    sfb[idle, :] = jnp.zeros(((CB - FB) * PITCH, 128), F32)

    meta = got[:, 0, 256:384]
    top = jnp.max(jnp.max(meta[:, 2:3], axis=0, keepdims=True), axis=1, keepdims=True)
    time_step = 0.2 / top
    keys = [meta[:, k : k + 1].astype(jnp.int32) - 1 for k in range(2)]
    target = lax.broadcasted_iota(jnp.int32, (PEERS, 256), 1)
    hit = jnp.concatenate([(k == target).astype(F32) for k in keys], axis=0).astype(BF16)
    rows = jnp.concatenate([got[:, 0, 0:128], got[:, 0, 128:256]], axis=0)
    tn = ((0,), (0,))
    replaced = mm_right(hit, rows, tn)[0:192]
    counted = mm(hit, jnp.ones((2 * PEERS, 128), BF16), tn)[0:192]
    spread = jnp.concatenate(
        [mm_left(replaced[0:128], expand[0]), mm_left(replaced[128:192], expand[1])], axis=0
    )
    lane = lax.broadcasted_iota(jnp.int32, (CB, 128), 1)

    def faces(d):
        def at(quad):
            return slice(d * 64 + quad * CB, d * 64 + (quad + 1) * CB)

        planes, masks = ([], []), []
        for h in range(2):
            near, far = (h, h + 2) if d == 2 else (2 * h, 2 * h + 1)
            for t in range(2):
                part = slice(t * 128, (t + 1) * 128)
                planes[t].append(spread[at(near), part] + pltpu.roll(spread[at(far), part], 8, 1))
            masks.append(jnp.where((lane & 15) < 8, counted[at(near)], counted[at(far)]))
        return planes, masks

    load_emf.wait()
    for t, along in enumerate(TANGENT[0]):
        planes, masks = faces(0)
        now = slab(emf, along, 0, 0, CB)
        put_slab(emf, along, 0, 0, CB, each(lambda m, p, e: jnp.where(m > 0.5, p, e), masks, planes[t], now))
    planes_1, masks_1 = faces(1)
    planes_2, masks_2 = faces(2)

    def correct(i, carry):
        turn = lax.rem(8 - i % 8, 8) * 16
        upper = jnp.broadcast_to(i >= 8, (CB, 128))
        there = pltpu.roll(jnp.where(upper, masks_1[1], masks_1[0]), turn, 1)
        for t, along in enumerate(TANGENT[1]):
            value = pltpu.roll(jnp.where(upper, planes_1[t][1], planes_1[t][0]), turn, 1)
            base = pl.multiple_of(i * WIDE, 128)
            now = emf[along, 0:CB, pl.ds(base, 128)]
            emf[along, 0:CB, pl.ds(base, 128)] = jnp.where((lane < 16) & (there > 0.5), value, now)
        turn = lax.rem(128 - i, 128)
        column = (lane & 15) == 0
        there = [column & (pltpu.roll(m, turn, 1) > 0.5) for m in masks_2]
        for t, along in enumerate(TANGENT[2]):
            value = [pltpu.roll(p, turn, 1) for p in planes_2[t]]
            now = slab(emf, along, i, 0, CB)
            put_slab(emf, along, i, 0, CB, each(jnp.where, there, value, now))
        return carry

    lax.fori_loop(0, EDGE, correct, 0)
    for copy in copies:
        copy.wait()

    def update(first, factor, load_b, store):
        def step(i, carry):
            following = lax.rem(i + 1, EDGE)
            ex, ey, ez = (slab(emf, c, i, first, CB) for c in range(3))
            ey_far, ez_far = (slab(emf, c, following, first, CB) for c in (1, 2))
            curl = lambda b, p, q, r, s: b - factor * ((p - q) - (r - s))
            store(0, i, each(curl, load_b(0, i), y_next(ez), ez, z_next(ey), ey))
            store(1, i, each(curl, load_b(1, i), z_next(ex), ex, ez_far, ez))
            store(2, i, each(curl, load_b(2, i), ey_far, ey, y_next(ex), ex))
            return carry

        lax.fori_loop(0, EDGE, step, 0)

    update(
        0,
        time_step,
        lambda c, i: slab(cb, c, i, 0, CB),
        lambda c, i, value: put_slab(new_c, c, i, 0, CB, value),
    )
    update(
        CB,
        time_step / 0.5,
        lambda c, i: fine_slab(sfb, c, i),
        lambda c, i, value: put_fine_slab(out_f, c, i, value),
    )
    results = [
        pltpu.make_async_copy(out_f.at[pl.ds(b * PITCH, 96)], new_f.at[b], sems.at[2])
        for b in range(FB)
    ]
    for copy in results:
        copy.start()
    quads = []
    faces_c = (
        slab(new_c, 0, 0, 0, CB),
        face_row_wise(lambda i: slab(new_c, 1, i, 0, CB)[0]),
        face_column_wise(lambda i: slab(new_c, 2, i, 0, CB)),
    )
    for d in range(3):
        quads.append(mm_left(jnp.concatenate(faces_c[d], axis=1), quadrant[1 if d == 2 else 0]))
    quads = jnp.concatenate([*quads, jnp.zeros((CB, WIDE), F32)], axis=0)
    wide_lane = lax.broadcasted_iota(jnp.int32, (PEERS, 64), 1)
    out_lane = lax.broadcasted_iota(jnp.int32, (PEERS, 128), 1)
    answers = []
    for k in range(2):
        key = keys[k]
        row = jnp.where(key >= 0, (key >> 6) * CB + (key & 15), -1)
        pick = (row == wide_lane).astype(F32).astype(BF16)
        both = mm_right(pick, quads)
        quad = (key >> 4) & 3
        value = jnp.where(quad >= 2, both[:, 128:256], both[:, 0:128])
        answers.append(jnp.where((quad & 1) == k, value, pltpu.roll(value, 64, 1)))
    back[:, 0, :] = jnp.where(out_lane < 64, answers[0], answers[1])

    faces_f = (
        fine_slab(out_f, 0, 0),
        face_row_wise(lambda i: fine_slab(out_f, 1, i)[0]),
        face_column_wise(lambda i: fine_slab(out_f, 2, i)),
    )
    for d in range(3):
        normals[d * CB : (d + 1) * CB, 0:128] = faces_f[d][0]
        normals[d * CB : (d + 1) * CB, 128:256] = faces_f[d][1]
    for copy in results:
        copy.wait()


def third_kernel(got, normals, pairs, flip, prolong, jump):
    first, second, source = routes(pairs)
    tn = ((0,), (0,))
    rows = got[:, 0, :]
    lane = lax.broadcasted_iota(jnp.int32, (PAIRS, 128), 1)
    own = jnp.where(
        lane < 64,
        mm_right(first.astype(BF16), rows, tn),
        mm_right(second.astype(BF16), rows, tn),
    )
    coarse = mm_left(own, prolong[...])
    source = source.astype(BF16)
    straight = mm_right(source[0 : 2 * CB], normals[0 : 2 * CB], tn)
    flipped = mm_left(mm_right(source[2 * CB :], normals[2 * CB :], tn), flip[...])
    jump[...] = straight + flipped - coarse


VMEM = pl.BlockSpec(memory_space=pltpu.VMEM)
ANY = pl.BlockSpec(memory_space=pl.ANY)


def on_device(coarse_field, coarse_velocity, fine_field, fine_velocity, pairs):
    cb = coarse_field[0].transpose(1, 0, 2)
    cv = coarse_velocity[0].transpose(1, 0, 2)
    fb = fine_field[0].reshape(FB, 96, 128)
    fv = fine_velocity[0].reshape(FB, 96, 128)
    rows = pairs[0].T.reshape(6, 1, PAIRS)
    field = pltpu.VMEM((3, CB, CELLS), F32)
    pitched = pltpu.VMEM((CB * PITCH, 128), F32)
    limit = pltpu.CompilerParams(vmem_limit_bytes=32 * 1024 * 1024)
    send, speed, emf = pl.pallas_call(
        first_kernel,
        out_shape=(
            jax.ShapeDtypeStruct((PEERS, 1, 384), F32),
            jax.ShapeDtypeStruct((1, 128), F32),
            jax.ShapeDtypeStruct((3, 2 * CB, CELLS), F32),
        ),
        in_specs=[ANY, ANY, ANY, ANY, VMEM, VMEM],
        out_specs=(VMEM, VMEM, VMEM),
        scratch_shapes=[
            field,
            field,
            pitched,
            pitched,
            pltpu.VMEM((3, 2 * CB, CELLS), F32),
            pltpu.SemaphoreType.DMA((4,)),
        ],
        compiler_params=limit,
        name="edges_and_rows",
    )(cb, cv, fb, fv, rows, jnp.asarray(RESTRICT, BF16))
    count = lax.axis_size("gz")
    others = [
        lax.ppermute(speed, "gz", [(i, (i + k) % count) for i in range(count)])
        for k in range(1, count)
    ]
    for other in others:
        speed = jnp.maximum(speed, other)
    lane = lax.broadcasted_iota(jnp.int32, send.shape, 2)
    send = jnp.where(lane == 258, speed[0, 0], send)
    got = lax.all_to_all(send, BLOCKS, 0, 0, tiled=True)
    new_c, new_f, back, normals = pl.pallas_call(
        second_kernel,
        out_shape=(
            jax.ShapeDtypeStruct((3, CB, CELLS), F32),
            jax.ShapeDtypeStruct((FB, 96, 128), F32),
            jax.ShapeDtypeStruct((PEERS, 1, 128), F32),
            jax.ShapeDtypeStruct((3 * CB, WIDE), F32),
        ),
        in_specs=[VMEM, VMEM, ANY, ANY, VMEM, VMEM],
        out_specs=(VMEM, ANY, VMEM, VMEM),
        scratch_shapes=[
            pitched,
            pltpu.VMEM((3, 2 * CB, CELLS), F32),
            pitched,
            pltpu.SemaphoreType.DMA((3,)),
        ],
        compiler_params=limit,
        name="corrected_updates",
    )(got, cb, fb, emf, jnp.asarray(EXPAND, BF16), jnp.asarray(QUADRANT, BF16))
    returned = lax.all_to_all(back, BLOCKS, 0, 0, tiled=True)
    jump = pl.pallas_call(
        third_kernel,
        out_shape=jax.ShapeDtypeStruct((PAIRS, WIDE), F32),
        in_specs=[VMEM] * 5,
        out_specs=VMEM,
        compiler_params=limit,
        name="face_jumps",
    )(returned, normals, rows, jnp.asarray(FLIP, BF16), jnp.asarray(PROLONG, BF16))
    return (
        new_c.transpose(1, 0, 2)[None],
        new_f.reshape(1, FB, 3, CELLS),
        jump[None],
    )


def solution(mesh):
    split = Mesh(
        mesh.devices.reshape(4, 8, 2, mesh.shape["gz"]), ("blocks_0", "blocks_1", "blocks_2", "gz")
    )
    in_specs = (
        P("gz", BLOCKS, None, None),
        P("gz", BLOCKS, None, None),
        P("gz", BLOCKS, None, None),
        P("gz", BLOCKS, None, None),
        P("gz", BLOCKS, None),
    )
    out_specs = (P("gz", BLOCKS, None, None), P("gz", BLOCKS, None, None), P("gz", BLOCKS, None))
    return jax.shard_map(
        on_device, mesh=split, in_specs=in_specs, out_specs=out_specs, check_vma=False
    )
```

profile of v0, /device:TPU:1, one launch (start us, length us, event | category | flops | bytes accessed | tf_op | source)
XLA Modules:
  0.0 80.7 jit_solution(2884980100084607639)
XLA Ops:
  0.6 0.7 copy.17
  1.3 0.0 copy-start
  1.3 1.1 %copy-done = f32[1,16,3,4096]{3,1,2,0:T(8,128)S(1)} copy-done((f32[1,16,3,4096]{3,1,2,0:T(8,128)S(1)}, f32[1,16,3,4096]{3,1,2,0:T(8,128)}, u32[]{:S(2)}) %copy-start) | copy-done | bytes 786456
  2.5 0.0 copy-start.1
  2.5 1.1 %copy-done.1 = f32[1,12,3,4096]{3,0,2,1:T(1,128)S(1)} copy-done((f32[1,12,3,4096]{3,0,2,1:T(1,128)S(1)}, f32[1,12,3,4096]{3,0,2,1:T(1,128)}, u32[]{:S(2)}) %copy-start.1) | copy-done | bytes 589848
  3.5 0.0 copy-start.3
  3.5 1.1 %copy-done.3 = f32[1,16,3,4096]{3,1,2,0:T(8,128)S(1)} copy-done((f32[1,16,3,4096]{3,1,2,0:T(8,128)S(1)}, f32[1,16,3,4096]{3,1,2,0:T(8,128)}, u32[]{:S(2)}) %copy-start.3) | copy-done | bytes 786456
  4.7 0.0 copy-start.4
  4.7 1.1 %copy-done.4 = f32[1,12,3,4096]{3,0,2,1:T(1,128)S(1)} copy-done((f32[1,12,3,4096]{3,0,2,1:T(1,128)S(1)}, f32[1,12,3,4096]{3,0,2,1:T(1,128)}, u32[]{:S(2)}) %copy-start.4) | copy-done | bytes 589848
  5.7 0.0 copy-start.5
  5.7 0.9 %copy-done.5 = bf16[2,512,128]{2,1,0:T(8,128)(2,1)S(1)} copy-done((bf16[2,512,128]{2,1,0:T(8,128)(2,1)S(1)}, bf16[2,512,128]{2,1,0:T(8,128)(2,1)}, u32[]{:S(2)}) %copy-start.5) | copy-done | bytes 262168
  6.7 0.0 copy-start.2
  6.7 0.0 copy-start.6
  6.7 15.1 %edges_and_rows.1 = (f32[64,1,384]{2,1,0:T(1,128)S(1)}, f32[1,128]{1,0:T(1,128)S(1)}, f32[3,32,4096]{2,1,0:T(8,128)S(1)}) custom-call(f32[3,16,4096]{2,1,0:T(8,128)S(1)} %bitcast.20, f32[3,16,4096]{2,1,0:T(8,128)S(1)} %bitcast.24, f32[12,96,128]{2,1,0:T(8,128)S(1)} %bitcast.22, f32[12,96,128]{2,1,0:T(8,128)S(1)} %bitcast.25, s32[6,1,32]{2,1,0:T(1,128)S(1)} %reshape.12.pairs, ...), custom_call_target="tpu_custom_call" | custom-call | tf_op jit(solution)/shard_map/edges_and_rows/pallas_call | solution.py:468
  21.8 3.6 %collective-permute-start.2 = (f32[1,128]{1,0:T(1,128)S(1)}, f32[1,128]{1,0:T(1,128)S(1)}, u32[]{:S(2)}, u32[]{:S(2)}) collective-permute-start(f32[1,128]{1,0:T(1,128)S(1)} %get-tuple-element.10), channel_id=1, source_target_pairs={{0,3},{1,0},{2,1},{3,2},{4,7},{5,4},{6,5},{7,6},{8,11},{9,8},{10,9... | collective-permute-start | bytes 1544 | tf_op jit(solution)/shard_map/ppermute | solution.py:490
  25.4 0.3 collective-permute-start.1
  25.8 0.7 collective-permute-start
  26.5 0.0 collective-permute-done.2
  26.5 2.9 %collective-permute-done.1 = f32[1,128]{1,0:T(1,128)S(1)} collective-permute-done((f32[1,128]{1,0:T(1,128)S(1)}, f32[1,128]{1,0:T(1,128)S(1)}, u32[]{:S(2)}, u32[]{:S(2)}) %collective-permute-start.1) | collective-permute-done | bytes 544 | tf_op jit(solution)/shard_map/ppermute | solution.py:490
  29.4 0.1 collective-permute-done
  29.4 0.1 broadcast_select_fusion
  29.5 23.8 %all_to_all.10.got = f32[64,1,384]{2,1,0:T(1,128)S(1)} all-to-all(f32[64,1,384]{2,1,0:T(1,128)S(1)} %broadcast_select_fusion), channel_id=1, replica_groups=mesh['blocks_0'=4,'blocks_1'=8,'blocks_2'=2,'gz'=4] {'blocks_0','blocks_..., dimensions={0} | all-to-all | bytes 196608 | tf_op jit(solution)/shard_map/all_to_all | solution.py:497
  53.4 0.0 copy-done.2
  53.4 0.0 copy-done.6
  53.4 0.0 copy-done.8
  53.4 0.0 copy-start.7
  53.4 0.0 copy-start.9
  53.4 12.7 %corrected_updates.1 = (f32[3,16,4096]{2,1,0:T(8,128)}, f32[12,96,128]{2,1,0:T(8,128)}, f32[64,1,128]{2,1,0:T(1,128)S(1)}, f32[48,256]{1,0:T(8,128)S(1)}) custom-call(f32[64,1,384]{2,1,0:T(1,128)S(1)} %all_to_all.10.got, f32[3,16,4096]{2,1,0:T(8,128)S(1)} %bitcast.21, f32[12,96,128]{2,1,0:T(8,128)S(1)} %bitcast.23, ...), custom_call_target="tpu_custom_call" | custom-call | tf_op jit(solution)/shard_map/corrected_updates/pallas_call | solution.py:498
  66.1 13.5 %all_to_all.11.got = f32[64,1,128]{2,1,0:T(1,128)S(1)} all-to-all(f32[64,1,128]{2,1,0:T(1,128)S(1)} %get-tuple-element.15), channel_id=1, replica_groups=mesh['blocks_0'=4,'blocks_1'=8,'blocks_2'=2,'gz'=4] {'blocks_0','blocks_..., dimensions={0} | all-to-all | bytes 65536 | tf_op jit(solution)/shard_map/all_to_all | solution.py:517
  79.6 0.0 copy-done.7
  79.6 0.0 copy-done.9
  79.6 1.1 %face_jumps.1 = f32[32,256]{1,0:T(8,128)} custom-call(f32[64,1,128]{2,1,0:T(1,128)S(1)} %all_to_all.11.got, f32[48,256]{1,0:T(8,128)S(1)} %get-tuple-element.16.normals, s32[6,1,32]{2,1,0:T(1,128)S(1)} %reshape.12.pairs, bf16[256,256]{1,0:T(8,128)(2,1)S(1)} %copy-done.7, bf16[128,256]{1,0:T(8,128)(2,1)S(1)} %copy-done.9), custom_call_target="tpu_custom_call" | custom-call | tf_op jit(solution)/shard_map/face_jumps/pallas_call | solution.py:518
  (4 shorter events, 0.0 us)
Async XLA Ops:
  1.3 1.1 %copy-start = (f32[1,16,3,4096]{3,1,2,0:T(8,128)S(1)}, f32[1,16,3,4096]{3,1,2,0:T(8,128)}, u32[]{:S(2)}) copy-start(f32[1,16,3,4096]{3,1,2,0:T(8,128)} %param.10) | copy-start | bytes 2359300
  2.5 1.1 %copy-start.1 = (f32[1,12,3,4096]{3,0,2,1:T(1,128)S(1)}, f32[1,12,3,4096]{3,0,2,1:T(1,128)}, u32[]{:S(2)}) copy-start(f32[1,12,3,4096]{3,0,2,1:T(1,128)} %param.12) | copy-start | bytes 1769476
  3.5 1.1 %copy-start.3 = (f32[1,16,3,4096]{3,1,2,0:T(8,128)S(1)}, f32[1,16,3,4096]{3,1,2,0:T(8,128)}, u32[]{:S(2)}) copy-start(f32[1,16,3,4096]{3,1,2,0:T(8,128)} %param.11) | copy-start | bytes 2359300
  4.7 1.1 %copy-start.4 = (f32[1,12,3,4096]{3,0,2,1:T(1,128)S(1)}, f32[1,12,3,4096]{3,0,2,1:T(1,128)}, u32[]{:S(2)}) copy-start(f32[1,12,3,4096]{3,0,2,1:T(1,128)} %param.13) | copy-start | bytes 1769476
  5.7 0.9 %copy-start.5 = (bf16[2,512,128]{2,1,0:T(8,128)(2,1)S(1)}, bf16[2,512,128]{2,1,0:T(8,128)(2,1)}, u32[]{:S(2)}) copy-start(bf16[2,512,128]{2,1,0:T(8,128)(2,1)} %constant.12.clone.restrict) | copy-start | bytes 786436
  6.7 46.7 %copy-start.2 = (f32[1,12,3,4096]{3,0,2,1:T(1,128)S(1)}, f32[1,12,3,4096]{3,0,2,1:T(1,128)}, u32[]{:S(2)}) copy-start(f32[1,12,3,4096]{3,0,2,1:T(1,128)} %param.12) | copy-start | bytes 1769476
  6.7 46.7 %copy-start.6 = (bf16[2,256,256]{2,1,0:T(8,128)(2,1)S(1)}, bf16[2,256,256]{2,1,0:T(8,128)(2,1)}, u32[]{:S(2)}) copy-start(bf16[2,256,256]{2,1,0:T(8,128)(2,1)} %constant.14.clone.quadrant) | copy-start | bytes 786436
  6.7 46.7 %copy-start.8 = (bf16[2,128,256]{2,1,0:T(8,128)(2,1)S(1)}, bf16[2,128,256]{2,1,0:T(8,128)(2,1)}, u32[]{:S(2)}) copy-start(bf16[2,128,256]{2,1,0:T(8,128)(2,1)} %constant.13.clone.expand) | copy-start | bytes 393220
  21.8 4.7 %collective-permute-start.2 = (f32[1,128]{1,0:T(1,128)S(1)}, f32[1,128]{1,0:T(1,128)S(1)}, u32[]{:S(2)}, u32[]{:S(2)}) collective-permute-start(f32[1,128]{1,0:T(1,128)S(1)} %get-tuple-element.10), channel_id=1, source_target_pairs={{0,3},{1,0},{2,1},{3,2},{4,7},{5,4},{6,5},{7,6},{8,11},{9,8},{10,9... | collective-permute-start | bytes 1544 | tf_op jit(solution)/shard_map/ppermute | solution.py:490
  25.4 3.9 %collective-permute-start.1 = (f32[1,128]{1,0:T(1,128)S(1)}, f32[1,128]{1,0:T(1,128)S(1)}, u32[]{:S(2)}, u32[]{:S(2)}) collective-permute-start(f32[1,128]{1,0:T(1,128)S(1)} %get-tuple-element.10), channel_id=1, source_target_pairs={{0,2},{1,3},{2,0},{3,1},{4,6},{5,7},{6,4},{7,5},{8,10},{9,11},{10,... | collective-permute-start | bytes 1544 | tf_op jit(solution)/shard_map/ppermute | solution.py:490
  25.8 3.6 %collective-permute-start = (f32[1,128]{1,0:T(1,128)S(1)}, f32[1,128]{1,0:T(1,128)S(1)}, u32[]{:S(2)}, u32[]{:S(2)}) collective-permute-start(f32[1,128]{1,0:T(1,128)S(1)} %get-tuple-element.10), channel_id=1, source_target_pairs={{0,1},{1,2},{2,3},{3,0},{4,5},{5,6},{6,7},{7,4},{8,9},{9,10},{10,1... | collective-permute-start | bytes 1544 | tf_op jit(solution)/shard_map/ppermute | solution.py:490
  53.4 26.2 %copy-start.7 = (bf16[256,256]{1,0:T(8,128)(2,1)S(1)}, bf16[256,256]{1,0:T(8,128)(2,1)}, u32[]{:S(2)}) copy-start(bf16[256,256]{1,0:T(8,128)(2,1)} %constant.15.clone.flip) | copy-start | bytes 393220
  53.4 26.2 %copy-start.9 = (bf16[128,256]{1,0:T(8,128)(2,1)S(1)}, bf16[128,256]{1,0:T(8,128)(2,1)}, u32[]{:S(2)}) copy-start(bf16[128,256]{1,0:T(8,128)(2,1)} %constant.16.clone.prolong) | copy-start | bytes 196612
where the time goes:
time: 81.1 us; the launch traced here: 80.7 us
  blocking collectives  37.3 us (46%)
  Pallas kernels  29 us (36%)
  local copies, waits for them, and re-layouts  6.06 us (7%)
  starting transfers between devices  4.67 us (6%)
  waiting for transfers between devices  2.93 us (4%)
    all_to_all x1, blocking collectives, on_device(): got = lax.all_to_all(send, BLOCKS, 0, 0, tiled=True)  23.8 us
    pallas_call x1, Pallas kernels, on_device(): pl.pallas_call(first_kernel, out_shape=(jax.ShapeDtypeStruct((PEERS, 1, 3...  15.1 us
    all_to_all x1, blocking collectives, on_device(): returned = lax.all_to_all(back, BLOCKS, 0, 0, tiled=True)  13.5 us
    pallas_call x1, Pallas kernels, on_device(): pl.pallas_call(second_kernel, out_shape=(jax.ShapeDtypeStruct((3, CB, CEL...  12.7 us
    unnamed x21, local copies, waits for them, and re-layouts  6.05 us
    ppermute x3, starting transfers between devices, on_device(): lax.ppermute(speed, 'gz', [(i, (i + k) % count) for i in range(count)])  4.67 us
    ppermute x3, waiting for transfers between devices, on_device(): lax.ppermute(speed, 'gz', [(i, (i + k) % count) for i in range(count)])  2.93 us
  transfers between devices with their start and end apart: 3, of which 2 were waited for; matrix products, arithmetic and copies ran while one was open for 0% of the time, Pallas kernels for 0%

commit v1 on v0

v1 whole, which is shorter than its diff:
```python
import jax
import jax.numpy as jnp
import numpy as np
from jax import lax
from jax.experimental import pallas as pl
from jax.experimental.pallas import tpu as pltpu
from jax.sharding import Mesh
from jax.sharding import PartitionSpec as P

EDGE = 16
HALF = 8
CB = 16
FB = 12
PAIRS = 32
PEERS = 64
WIDE = EDGE * EDGE
CELLS = EDGE**3
PITCH = 104
BLOCKS = ("blocks_0", "blocks_1", "blocks_2")
F32 = jnp.float32
BF16 = jnp.bfloat16
TANGENT = ((1, 2), (0, 2), (0, 1))
UNROLL = 16


def _face_lane(row, col, flip):
    return col * EDGE + row if flip else row * EDGE + col


def _restrict_matrix(flip):
    out = np.zeros((2, WIDE, 128), np.float32)
    for m in range(HALF):
        for n in range(HALF):
            o = m * HALF + n
            out[0, _face_lane(2 * m, 2 * n, flip), o] = 0.5
            out[0, _face_lane(2 * m + 1, 2 * n, flip), o] = 0.5
            out[1, _face_lane(2 * m, 2 * n, flip), 64 + o] = 0.5
            out[1, _face_lane(2 * m, 2 * n + 1, flip), 64 + o] = 0.5
    return out.reshape(2 * WIDE, 128)


def _expand_matrix(flip):
    out = np.zeros((128, 256), np.float32)
    for m in range(HALF):
        for n in range(HALF):
            o = m * HALF + n
            out[o, _face_lane(m, n, flip)] = 1.0
            out[64 + o, 128 + _face_lane(m, n, flip)] = 1.0
    return out


def _quadrant_matrix(flip):
    out = np.zeros((WIDE, WIDE), np.float32)
    for row in range(EDGE):
        for col in range(EDGE):
            quad = (row // HALF) * 2 + col // HALF
            out[_face_lane(row, col, flip), quad * 64 + (row % HALF) * HALF + col % HALF] = 1.0
    return out


def _flip_matrix():
    out = np.zeros((WIDE, WIDE), np.float32)
    for row in range(EDGE):
        for col in range(EDGE):
            out[_face_lane(row, col, True), _face_lane(row, col, False)] = 1.0
    return out


def _prolong_matrix():
    out = np.zeros((128, WIDE), np.float32)
    for row in range(EDGE):
        for col in range(EDGE):
            o = (row // 2) * HALF + col // 2
            out[o, _face_lane(row, col, False)] = 1.0
            out[64 + o, _face_lane(row, col, False)] = 1.0
    return out


RESTRICT = np.stack([_restrict_matrix(False), _restrict_matrix(True)])
EXPAND = np.stack([_expand_matrix(False), _expand_matrix(True)])
QUADRANT = np.stack([_quadrant_matrix(False), _quadrant_matrix(True)])
FLIP = _flip_matrix()
PROLONG = _prolong_matrix()


def halves(value):
    high = value.astype(BF16)
    return high, (value - high.astype(F32)).astype(BF16)


def mm(a, b, dims=((1,), (0,))):
    return lax.dot_general(a, b, (dims, ((), ())), preferred_element_type=F32)


def mm_left(value, matrix, dims=((1,), (0,))):
    high, low = halves(value)
    return mm(high, matrix, dims) + mm(low, matrix, dims)


def mm_right(matrix, value, dims=((1,), (0,))):
    high, low = halves(value)
    return mm(matrix, high, dims) + mm(matrix, low, dims)


def lanes_of(value):
    return lax.broadcasted_iota(jnp.int32, value.shape, 1)


def y_prev(p):
    a, b = pltpu.roll(p[0], 16, 1), pltpu.roll(p[1], 16, 1)
    edge = lanes_of(a) < 16
    return jnp.where(edge, b, a), jnp.where(edge, a, b)


def y_next(p):
    a, b = pltpu.roll(p[0], 112, 1), pltpu.roll(p[1], 112, 1)
    edge = lanes_of(a) >= 112
    return jnp.where(edge, b, a), jnp.where(edge, a, b)


def z_prev(p):
    edge = (lanes_of(p[0]) & 15) == 0
    return tuple(jnp.where(edge, pltpu.roll(x, 113, 1), pltpu.roll(x, 1, 1)) for x in p)


def z_next(p):
    edge = (lanes_of(p[0]) & 15) == 15
    return tuple(jnp.where(edge, pltpu.roll(x, 15, 1), pltpu.roll(x, 127, 1)) for x in p)


def each(fn, *pairs):
    return tuple(fn(*(p[h] for p in pairs)) for h in range(2))


def span(i, half):
    start = i * WIDE + half * 128
    return pl.ds(start if isinstance(start, int) else pl.multiple_of(start, 128), 128)


def slab(ref, comp, i, first, count):
    return tuple(ref[comp, first : first + count, span(i, half)] for half in range(2))


def put_slab(ref, comp, i, first, count, value):
    for half in range(2):
        ref[comp, first : first + count, span(i, half)] = value[half]


def fine_slab(ref, comp, i):
    def one(half):
        start = comp * 32 + 2 * i + half
        return jnp.concatenate(
            [
                ref[pl.ds(start, 8, stride=PITCH), :],
                ref[pl.ds(start + 8 * PITCH, 8, stride=PITCH), :],
            ],
            axis=0,
        )

    return one(0), one(1)


def put_fine_slab(ref, comp, i, value):
    for half in range(2):
        start = comp * 32 + 2 * i + half
        ref[pl.ds(start, 8, stride=PITCH), :] = value[half][0:8]
        ref[pl.ds(start + 8 * PITCH, 8, stride=PITCH), :] = value[half][8:16]


def fetch_fine(source, target, sem):
    return [
        pltpu.make_async_copy(source.at[b], target.at[pl.ds(b * PITCH, 96)], sem)
        for b in range(FB)
    ]


def face_row_wise(load):
    out = [jnp.zeros((CB, 128), F32)] * 2
    group = lax.broadcasted_iota(jnp.int32, (CB, 128), 1) // 16
    for i in range(EDGE):
        turned = pltpu.roll(load(i), i % 8 * 16, 1)
        out[i // 8] = jnp.where(group == i % 8, turned, out[i // 8])
    return tuple(out)


def face_column_wise(load):
    out = (jnp.zeros((CB, 128), F32),) * 2
    column = lax.broadcasted_iota(jnp.int32, (CB, 128), 1) & 15
    for i in range(EDGE):
        out = each(lambda x, h: jnp.where(column == i, pltpu.roll(x, i, 1), h), load(i), out)
    return out


def routes(pairs_ref):
    slot, face, owner = pairs_ref[0], pairs_ref[1], pairs_ref[2]
    peer = lax.broadcasted_iota(jnp.int32, (PEERS, PAIRS), 0)
    named = (owner == peer).astype(F32)
    before = (
        lax.broadcasted_iota(jnp.int32, (PAIRS, PAIRS), 0)
        < lax.broadcasted_iota(jnp.int32, (PAIRS, PAIRS), 1)
    ).astype(F32)
    earlier = mm(named.astype(BF16), before.astype(BF16))
    rank = jnp.sum(named * earlier, axis=0, keepdims=True)
    first = jnp.where(rank < 0.5, named, 0.0)
    second = jnp.where(rank < 0.5, 0.0, named)
    at_row = lax.broadcasted_iota(jnp.int32, (3 * CB, PAIRS), 0)
    source = (face * CB + slot == at_row).astype(F32)
    return first, second, source


def cells_kernel(cb, cv, fb, fv, cell_c, cell_f, b_c, b_f, speed, v_c, v_f, sems):
    fine_copies = fetch_fine(fb, b_f, sems.at[0]) + fetch_fine(fv, v_f, sems.at[1])
    coarse_copies = [
        pltpu.make_async_copy(cb, b_c, sems.at[2]),
        pltpu.make_async_copy(cv, v_c, sems.at[3]),
    ]
    for copy in fine_copies + coarse_copies:
        copy.start()
    idle = pl.ds(FB * PITCH, (CB - FB) * PITCH)
    b_f[idle, :] = jnp.zeros(((CB - FB) * PITCH, 128), F32)
    v_f[idle, :] = jnp.zeros(((CB - FB) * PITCH, 128), F32)

    def cells(load_b, load_v, cell):
        def step(i, top):
            following = lax.rem(i + 1, EDGE)
            bx, by, bz = load_b(0, i), load_b(1, i), load_b(2, i)
            vx, vy, vz = load_v(0, i), load_v(1, i), load_v(2, i)
            mean = lambda a, b: 0.5 * (a + b)
            cx = each(mean, bx, load_b(0, following))
            cy = each(mean, by, y_next(by))
            cz = each(mean, bz, z_next(bz))
            cross = lambda a, b, c, d: a * b - c * d
            put_slab(cell, 0, i, 0, CB, each(cross, vz, cy, vy, cz))
            put_slab(cell, 1, i, 0, CB, each(cross, vx, cz, vz, cx))
            put_slab(cell, 2, i, 0, CB, each(cross, vy, cx, vx, cy))
            size = lambda a, b, c: jnp.sqrt(a * a + b * b + c * c)
            fast = each(lambda a, b: a + b, each(size, vx, vy, vz), each(size, cx, cy, cz))
            return jnp.maximum(top, jnp.maximum(fast[0], fast[1]))

        return lax.fori_loop(0, EDGE, step, jnp.zeros((CB, 128), F32), unroll=UNROLL)

    for copy in fine_copies:
        copy.wait()
    top_fine = cells(lambda c, i: fine_slab(b_f, c, i), lambda c, i: fine_slab(v_f, c, i), cell_f)
    for copy in coarse_copies:
        copy.wait()
    top_coarse = cells(
        lambda c, i: slab(b_c, c, i, 0, CB), lambda c, i: slab(v_c, c, i, 0, CB), cell_c
    )
    top = jnp.max(jnp.maximum(top_fine, top_coarse), axis=0, keepdims=True)
    speed[...] = jnp.broadcast_to(jnp.max(top, axis=1, keepdims=True), (1, 128))


def edges(cell, emf):
    def step(i, carry):
        prior = lax.rem(i + EDGE - 1, EDGE)
        add = lambda a, b: a + b
        quarter = lambda a, b: 0.25 * (a + b)
        ex = slab(cell, 0, i, 0, CB)
        sum_x = each(add, ex, y_prev(ex))
        put_slab(emf, 0, i, 0, CB, each(quarter, sum_x, z_prev(sum_x)))
        sum_y = each(add, slab(cell, 1, i, 0, CB), slab(cell, 1, prior, 0, CB))
        put_slab(emf, 1, i, 0, CB, each(quarter, sum_y, z_prev(sum_y)))
        sum_z = each(add, slab(cell, 2, i, 0, CB), slab(cell, 2, prior, 0, CB))
        put_slab(emf, 2, i, 0, CB, each(quarter, sum_z, y_prev(sum_z)))
        return carry

    lax.fori_loop(0, EDGE, step, 0, unroll=UNROLL)


def face_of(ref, along, d):
    if d == 0:
        return slab(ref, along, 0, 0, CB)
    if d == 1:
        return face_row_wise(lambda i: slab(ref, along, i, 0, CB)[0])
    return face_column_wise(lambda i: slab(ref, along, i, 0, CB))


def rows_kernel(cell, pairs, restrict, send, emf):
    edges(cell, emf)
    first, second, source = routes(pairs)
    rows = []
    for d in range(3):
        planes = [face_of(emf, along, d) for along in TANGENT[d]]
        both = jnp.concatenate([*planes[0], *planes[1]], axis=1)
        rows.append(mm_left(both, restrict[1 if d == 2 else 0]))
    rows = jnp.concatenate(rows, axis=0)
    nt = ((1,), (1,))
    key = (pairs[1] * 64 + (pairs[4] * 2 + pairs[5]) * CB + pairs[3] + 1).astype(F32)
    lane = lax.broadcasted_iota(jnp.int32, (PEERS, 128), 1)
    meta = jnp.zeros((PEERS, 128), F32)
    for k, chosen in enumerate((first, second)):
        pick = mm(chosen.astype(BF16), source.astype(BF16), nt)
        send[:, 0, k * 128 : (k + 1) * 128] = mm_right(pick.astype(BF16), rows)
        meta = jnp.where(lane == k, jnp.sum(chosen * key, axis=1, keepdims=True), meta)
    send[:, 0, 256:384] = meta


def coarse_kernel(cell, b_c, quadrant, emf, planes, quads):
    edges(cell, emf)
    for d in range(3):
        for t in range(2):
            at = (d * 2 + t) * CB
            face = face_of(emf, TANGENT[d][t], d)
            planes[at : at + CB, 0:128] = face[0]
            planes[at : at + CB, 128:256] = face[1]
        normal = jnp.concatenate(face_of(b_c, d, d), axis=1)
        quads[d * CB : (d + 1) * CB, :] = mm_left(normal, quadrant[1 if d == 2 else 0])


def answer_kernel(got, planes, quads_b, expand, quadrant, rows_b, rows_c, patch, masks):
    meta = got[:, 0, 256:384]
    keys = [meta[:, k : k + 1].astype(jnp.int32) - 1 for k in range(2)]
    target = lax.broadcasted_iota(jnp.int32, (PEERS, 256), 1)
    hit = jnp.concatenate([(k == target).astype(F32) for k in keys], axis=0).astype(BF16)
    rows = jnp.concatenate([got[:, 0, 0:128], got[:, 0, 128:256]], axis=0)
    tn = ((0,), (0,))
    replaced = mm_right(hit, rows, tn)[0:192]
    counted = mm(hit, jnp.ones((2 * PEERS, 128), BF16), tn)[0:192]
    spread = (mm_left(replaced, expand[0]), mm_left(replaced, expand[1]))
    lane = lax.broadcasted_iota(jnp.int32, (CB, 128), 1)

    def at(d, quad):
        return slice(d * 64 + quad * CB, d * 64 + (quad + 1) * CB)

    def value(d, t, flip):
        part = slice(t * 128, (t + 1) * 128)
        out = []
        for h in range(2):
            near, far = (h, h + 2) if flip else (2 * h, 2 * h + 1)
            x = spread[flip]
            out.append(x[at(d, near), part] + pltpu.roll(x[at(d, far), part], 8, 1))
        return tuple(out)

    def mask(d, flip):
        out = []
        for h in range(2):
            near, far = (h, h + 2) if flip else (2 * h, 2 * h + 1)
            out.append(jnp.where((lane & 15) < 8, counted[at(d, near)], counted[at(d, far)]) > 0.5)
        return tuple(out)

    value = {
        (d, t): value(d, t, int(d == 2)) for d in range(3) for t in range(2)
    } | {"1x": value(1, 0, 1), "2x": value(2, 0, 0)}
    hits = {d: mask(d, int(d == 2)) for d in range(3)} | {"1x": mask(1, 1), "2x": mask(2, 0)}
    for d in range(3):
        for h in range(2):
            side = slice(h * 128, (h + 1) * 128)
            masks[d * CB : (d + 1) * CB, side] = hits[d][h].astype(F32)
            for t in range(2):
                first = (d * 2 + t) * CB
                patch[first : first + CB, side] = value[d, t][h]

    def face(d, t):
        first = (d * 2 + t) * CB
        return planes[first : first + CB, 0:128], planes[first : first + CB, 128:256]

    both = lambda a, b: a & b
    column = ((lane & 15) == 0,) * 2
    row = (lane < 16, lane < 0)
    put = lambda m, new, old: each(jnp.where, m, new, old)
    ey_0 = put(hits[0], value[0, 0], face(0, 0))
    ez_0 = put(hits[0], value[0, 1], face(0, 1))
    ez_1 = put(each(both, row, hits[0]), value[0, 1], face(1, 1))
    ey_2 = put(each(both, column, hits[0]), value[0, 0], face(2, 1))
    ex_1 = put(hits[1], value[1, 0], face(1, 0))
    ez_1 = put(hits[1], value[1, 1], ez_1)
    ez_0 = put(each(both, row, hits[1]), value[1, 1], ez_0)
    ex_2 = put(each(both, row, hits["1x"]), value["1x"], face(2, 0))
    ex_2 = put(hits[2], value[2, 0], ex_2)
    ey_2 = put(hits[2], value[2, 1], ey_2)
    ex_1 = put(each(both, column, hits["2x"]), value["2x"], ex_1)
    ey_0 = put(each(both, column, hits[2]), value[2, 1], ey_0)
    curl = lambda p, q, r, s: (p - q) - (r - s)
    curls = (
        each(curl, y_next(ez_0), ez_0, z_next(ey_0), ey_0),
        each(curl, z_next(ex_1), ex_1, y_next(ez_1), ez_1),
        each(curl, z_next(ey_2), ey_2, y_next(ex_2), ex_2),
    )
    straight = jnp.concatenate(
        [jnp.concatenate(curls[0], axis=1), jnp.concatenate(curls[1], axis=1)], axis=0
    )
    quads_c = jnp.concatenate(
        [
            mm_left(straight, quadrant[0]),
            mm_left(jnp.concatenate(curls[2], axis=1), quadrant[1]),
        ],
        axis=0,
    )
    wide_lane = lax.broadcasted_iota(jnp.int32, (PEERS, 3 * CB), 1)
    out_lane = lax.broadcasted_iota(jnp.int32, (PEERS, 128), 1)
    for out, quads in ((rows_b, quads_b[...]), (rows_c, quads_c)):
        answers = []
        for k in range(2):
            key = keys[k]
            place = jnp.where(key >= 0, (key >> 6) * CB + (key & 15), -1)
            pick = (place == wide_lane).astype(F32).astype(BF16)
            found = mm_right(pick, quads)
            quad = (key >> 4) & 3
            side = jnp.where(quad >= 2, found[:, 128:256], found[:, 0:128])
            answers.append(jnp.where((quad & 1) == k, side, pltpu.roll(side, 64, 1)))
        out[:, 0, :] = jnp.where(out_lane < 64, answers[0], answers[1])


def update_kernel(
    top, emf_c, patch, masks, emf_f, b_c, b_f, new_c, new_f, normals, emf, out_c, out_f, sems
):
    time_step = 0.2 / top[0:1, 2:3]
    lane = lax.broadcasted_iota(jnp.int32, (CB, 128), 1)

    def pair(ref, first):
        return ref[first : first + CB, 0:128], ref[first : first + CB, 128:256]

    def update(emf, factor, load_b, store, done):
        for i in range(EDGE):
            following = (i + 1) % EDGE
            ex, ey, ez = (slab(emf, c, i, 0, CB) for c in range(3))
            ey_far, ez_far = (slab(emf, c, following, 0, CB) for c in (1, 2))
            curl = lambda b, p, q, r, s: b - factor * ((p - q) - (r - s))
            store(0, i, each(curl, load_b(0, i), y_next(ez), ez, z_next(ey), ey))
            store(1, i, each(curl, load_b(1, i), z_next(ex), ex, ez_far, ez))
            store(2, i, each(curl, load_b(2, i), ey_far, ey, y_next(ex), ex))
            done(i)

    update(
        emf_f,
        time_step / 0.5,
        lambda c, i: fine_slab(b_f, c, i),
        lambda c, i, value: put_fine_slab(out_f, c, i, value),
        lambda i: None,
    )
    results = [
        pltpu.make_async_copy(out_f.at[pl.ds(b * PITCH, 96)], new_f.at[b], sems.at[0])
        for b in range(FB)
    ]
    for copy in results:
        copy.start()

    planes = {(d, t): pair(patch, (d * 2 + t) * CB) for d in range(3) for t in range(2)}
    hits = [pair(masks, d * CB) for d in range(3)]
    for i in range(EDGE):
        now = {c: slab(emf_c, c, i, 0, CB) for c in range(3)}
        if i == 0:
            for t, c in enumerate(TANGENT[0]):
                now[c] = each(lambda m, p, e: jnp.where(m > 0.5, p, e), hits[0], planes[0, t], now[c])
        turn, h = (8 - i % 8) % 8 * 16, i // 8
        there = (lane < 16) & (pltpu.roll(hits[1][h], turn, 1) > 0.5)
        for t, c in enumerate(TANGENT[1]):
            now[c] = (jnp.where(there, pltpu.roll(planes[1, t][h], turn, 1), now[c][0]), now[c][1])
        turn = (128 - i) % 128
        there = [((lane & 15) == 0) & (pltpu.roll(m, turn, 1) > 0.5) for m in hits[2]]
        for t, c in enumerate(TANGENT[2]):
            value = [pltpu.roll(p, turn, 1) for p in planes[2, t]]
            now[c] = each(jnp.where, there, value, now[c])
        for c in range(3):
            put_slab(emf, c, i, 0, CB, now[c])

    def send_chunk(i):
        if i % 4 == 3:
            part = pl.ds((i - 3) * WIDE, 4 * WIDE)
            copy = pltpu.make_async_copy(out_c.at[:, :, part], new_c.at[:, :, part], sems.at[1])
            copy.start()
            results.append(copy)

    update(
        emf,
        time_step,
        lambda c, i: slab(b_c, c, i, 0, CB),
        lambda c, i, value: put_slab(out_c, c, i, 0, CB, value),
        send_chunk,
    )
    faces = (
        fine_slab(out_f, 0, 0),
        face_row_wise(lambda i: fine_slab(out_f, 1, i)[0]),
        face_column_wise(lambda i: fine_slab(out_f, 2, i)),
    )
    for d in range(3):
        normals[d * CB : (d + 1) * CB, 0:128] = faces[d][0]
        normals[d * CB : (d + 1) * CB, 128:256] = faces[d][1]
    for copy in results:
        copy.wait()


def third_kernel(got, normals, pairs, flip, prolong, jump):
    first, second, source = routes(pairs)
    tn = ((0,), (0,))
    rows = got[:, 0, :]
    lane = lax.broadcasted_iota(jnp.int32, (PAIRS, 128), 1)
    own = jnp.where(
        lane < 64,
        mm_right(first.astype(BF16), rows, tn),
        mm_right(second.astype(BF16), rows, tn),
    )
    coarse = mm_left(own, prolong[...])
    source = source.astype(BF16)
    straight = mm_right(source[0 : 2 * CB], normals[0 : 2 * CB], tn)
    flipped = mm_left(mm_right(source[2 * CB :], normals[2 * CB :], tn), flip[...])
    jump[...] = straight + flipped - coarse


VMEM = pl.BlockSpec(memory_space=pltpu.VMEM)
HBM = pl.BlockSpec(memory_space=pltpu.HBM)
FIELD = (3, CB, CELLS)
PITCHED = (CB * PITCH, 128)


def call(kernel, name, outs, args, scratch=()):
    far = [isinstance(out, tuple) and out[0] == "hbm" for out in outs]
    return pl.pallas_call(
        kernel,
        out_shape=[
            pltpu.HBM(out[1], F32) if is_far else pltpu.VMEM(out, F32)
            for out, is_far in zip(outs, far)
        ],
        in_specs=[HBM if is_far else VMEM for _, is_far in args],
        out_specs=[HBM if is_far else VMEM for is_far in far],
        scratch_shapes=list(scratch),
        compiler_params=pltpu.CompilerParams(vmem_limit_bytes=24 * 1024 * 1024),
        name=name,
    )(
        *(
            pltpu.with_memory_space_constraint(a, pltpu.HBM if is_far else pltpu.VMEM)
            for a, is_far in args
        )
    )


def on_device(coarse_field, coarse_velocity, fine_field, fine_velocity, pairs):
    cb = coarse_field[0].transpose(1, 0, 2)
    cv = coarse_velocity[0].transpose(1, 0, 2)
    fb = fine_field[0].reshape(FB, 96, 128)
    fv = fine_velocity[0].reshape(FB, 96, 128)
    rows = pairs.transpose(2, 0, 1)
    restrict, expand, quadrant, flip, prolong = (
        jnp.asarray(x, BF16) for x in (RESTRICT, EXPAND, QUADRANT, FLIP, PROLONG)
    )
    near = lambda *arrays: [(a, False) for a in arrays]
    far = lambda *arrays: [(a, True) for a in arrays]
    count = lax.axis_size("gz")

    cell_c, cell_f, b_c, b_f, speed = call(
        cells_kernel,
        "cells",
        [FIELD, FIELD, FIELD, PITCHED, (1, 128)],
        far(cb, cv, fb, fv),
        [pltpu.VMEM(FIELD, F32), pltpu.VMEM(PITCHED, F32), pltpu.SemaphoreType.DMA((4,))],
    )
    other = lax.ppermute(speed, "gz", [(i, i ^ 1) for i in range(count)])
    send, emf_f = call(
        rows_kernel, "rows", [(PEERS, 1, 384), FIELD], near(cell_f, rows, restrict)
    )
    speed = jnp.maximum(speed, other)
    lane = lax.broadcasted_iota(jnp.int32, send.shape, 2)
    send = jnp.where(lane == 258, speed[0, 0], send)
    got = lax.all_to_all(send, BLOCKS, 0, 0, tiled=True)
    emf_c, planes, quads = call(
        coarse_kernel,
        "coarse_edges",
        [FIELD, (6 * CB, WIDE), (3 * CB, WIDE)],
        near(cell_c, b_c, quadrant),
    )
    top = jnp.max(got[:, :, 256:384], axis=0)
    other = lax.ppermute(top, "gz", [(i, i ^ 2) for i in range(count)])
    rows_b, rows_c, patch, masks = call(
        answer_kernel,
        "answers",
        [(PEERS, 1, 128), (PEERS, 1, 128), (6 * CB, WIDE), (3 * CB, WIDE)],
        near(got, planes, quads, expand, quadrant),
    )
    top = jnp.maximum(top, other)
    back = rows_b - (0.2 / top[0, 2]) * rows_c
    returned = lax.all_to_all(back, BLOCKS, 0, 0, tiled=True)
    new_c, new_f, normals = call(
        update_kernel,
        "updates",
        [("hbm", FIELD), ("hbm", (FB, 96, 128)), (3 * CB, WIDE)],
        near(top, emf_c, patch, masks, emf_f, b_c, b_f),
        [
            pltpu.VMEM(FIELD, F32),
            pltpu.VMEM(FIELD, F32),
            pltpu.VMEM(PITCHED, F32),
            pltpu.SemaphoreType.DMA((2,)),
        ],
    )
    (jump,) = call(
        third_kernel,
        "face_jumps",
        [(PAIRS, WIDE)],
        near(returned, normals, rows, flip, prolong),
    )
    return (
        new_c.transpose(1, 0, 2)[None],
        new_f.reshape(1, FB, 3, CELLS),
        jump[None],
    )


def solution(mesh):
    split = Mesh(
        mesh.devices.reshape(4, 8, 2, mesh.shape["gz"]), ("blocks_0", "blocks_1", "blocks_2", "gz")
    )
    in_specs = (
        P("gz", BLOCKS, None, None),
        P("gz", BLOCKS, None, None),
        P("gz", BLOCKS, None, None),
        P("gz", BLOCKS, None, None),
        P("gz", BLOCKS, None),
    )
    out_specs = (P("gz", BLOCKS, None, None), P("gz", BLOCKS, None, None), P("gz", BLOCKS, None))
    return jax.shard_map(
        on_device, mesh=split, in_specs=in_specs, out_specs=out_specs, check_vma=False
    )
```

time: 81.1 us -> 54.4 us (0.67)
  Pallas kernels: 29 us -> 9.34 us
  blocking collectives: 37.3 us -> 23 us
  starting transfers between devices: 4.67 us -> 9.89 us
  waiting for transfers between devices: 2.93 us -> 6.07 us
  local copies, waits for them, and re-layouts: 6.06 us -> 3.43 us
    pallas_call x3 -> x6, Pallas kernels: 29 us -> 9.34 us  [call(): pl.pallas_call(kernel, out_shape=[pltpu.HBM(out[1], F32) if is_far else p...]
    all_to_all x1 -> x0, blocking collectives: 13.5 us -> none  [on_device(): returned = lax.all_to_all(back, BLOCKS, 0, 0, tiled=True)]
    all_to_all x0 -> x1, waiting for transfers between devices: none -> 6.07 us  [on_device(): returned = lax.all_to_all(back, BLOCKS, 0, 0, tiled=True)]
    all_to_all x0 -> x1, starting transfers between devices: none -> 4.7 us  [on_device(): returned = lax.all_to_all(back, BLOCKS, 0, 0, tiled=True)]
    unnamed x21, local copies, waits for them, and re-layouts: 6.05 us -> 2.85 us
    ppermute x3 -> x2, waiting for transfers between devices: 2.93 us -> 0.01 us  [the longest x1 0.01 us: on_device(): other = lax.ppermute(speed, 'gz', [(i, i ^ 1) for i in range(count)])]
    ppermute x3 -> x2, starting transfers between devices: 4.67 us -> 5.19 us  [the longest x1 2.99 us: on_device(): other = lax.ppermute(top, 'gz', [(i, i ^ 2) for i in range(count)])]
  transfers between devices with their start and end apart: 3 -> 3, of which waited for: 2 -> 1; matrix products, arithmetic and copies ran while one was open for 0% -> 0% of each run, Pallas kernels for 0% -> 12%
where the time goes in v1:
time: 54.4 us; the launch traced here: 54 us
  blocking collectives  23 us (42%)
  starting transfers between devices  9.89 us (18%)
  Pallas kernels  9.34 us (17%)
  waiting for transfers between devices  6.07 us (11%)
  local copies, waits for them, and re-layouts  3.43 us (6%)
  between operations  1.47 us (3%)
  other arithmetic  0.82 us (2%)
    all_to_all x1, blocking collectives, on_device(): got = lax.all_to_all(send, BLOCKS, 0, 0, tiled=True)  23 us
    pallas_call x6, Pallas kernels, call(): pl.pallas_call(kernel, out_shape=[pltpu.HBM(out[1], F32) if is_far else p...  9.34 us
    all_to_all x1, waiting for transfers between devices, on_device(): returned = lax.all_to_all(back, BLOCKS, 0, 0, tiled=True)  6.07 us
    all_to_all x1, starting transfers between devices, on_device(): returned = lax.all_to_all(back, BLOCKS, 0, 0, tiled=True)  4.7 us
    ppermute x1, starting transfers between devices, on_device(): other = lax.ppermute(top, 'gz', [(i, i ^ 2) for i in range(count)])  2.99 us
    unnamed x21, local copies, waits for them, and re-layouts  2.85 us
    ppermute x1, starting transfers between devices, on_device(): other = lax.ppermute(speed, 'gz', [(i, i ^ 1) for i in range(count)])  2.2 us
  transfers between devices with their start and end apart: 3, of which 1 were waited for; matrix products, arithmetic and copies ran while one was open for 0% of the time, Pallas kernels for 12%

profile of v1, /device:TPU:1, one launch (start us, length us, event | category | flops | bytes accessed | tf_op | source)
XLA Modules:
  0.0 54.0 jit_solution(16385377653426000868)
XLA Ops:
  0.6 0.0 copy-start.1
  0.6 2.4 %cells.1 = (f32[3,16,4096]{2,1,0:T(8,128)S(1)}, f32[3,16,4096]{2,1,0:T(8,128)S(1)}, f32[3,16,4096]{2,1,0:T(8,128)S(1)}, f32[1664,128]{1,0:T(8,128)S(1)}, f32[1,128]{1,0:T(1,128)S(1)}) custom-call(f32[3,16,4096]{2,1,0:T(8,128)} %bitcast.27, f32[3,16,4096]{2,1,0:T(8,128)} %bitcast.28, f32[12,96,128]{2,1,0:T(8,128)} %bitcast.29, f32[12,96,128]{2,1,0:T(8,128)} %bitcast.30), custom_call_target="tpu_custom_call" | custom-call | tf_op jit(solution)/shard_map/cells/pallas_call | solution.py:509
  3.1 0.0 copy-start.9
  3.1 2.2 %collective-permute-start = (f32[1,128]{1,0:T(1,128)S(1)}, f32[1,128]{1,0:T(1,128)S(1)}, u32[]{:S(2)}, u32[]{:S(2)}) collective-permute-start(f32[1,128]{1,0:T(1,128)S(1)} %get-tuple-element.20), channel_id=1, source_target_pairs={{0,1},{1,0},{2,3},{3,2},{4,5},{5,4},{6,7},{7,6},{8,9},{9,8},{10,11... | collective-permute-start | bytes 1544 | tf_op jit(solution)/shard_map/ppermute | solution.py:548
  5.3 0.0 copy-done.1
  5.3 0.0 copy-done.9
  5.3 1.3 %rows.1 = (f32[64,1,384]{2,1,0:T(1,128)S(1)}, f32[3,16,4096]{2,1,0:T(8,128)S(1)}) custom-call(f32[3,16,4096]{2,1,0:T(8,128)S(1)} %get-tuple-element.21.cell, s32[6,1,32]{2,1,0:T(1,128)S(1)} %bitcast.25, bf16[2,512,128]{2,1,0:T(8,128)(2,1)S(1)} %copy-done.1), custom_call_target="tpu_custom_call" | custom-call | tf_op jit(solution)/shard_map/rows/pallas_call | solution.py:509
  6.6 0.0 copy-start
  6.6 0.0 collective-permute-done
  6.7 0.1 broadcast_select_fusion
  6.8 23.0 %all_to_all.10.got = f32[64,1,384]{2,1,0:T(1,128)S(1)} all-to-all(f32[64,1,384]{2,1,0:T(1,128)S(1)} %broadcast_select_fusion), channel_id=1, replica_groups=mesh['blocks_0'=4,'blocks_1'=8,'blocks_2'=2,'gz'=4] {'blocks_0','blocks_..., dimensions={0} | all-to-all | bytes 196608 | tf_op jit(solution)/shard_map/all_to_all | solution.py:555
  29.8 0.1 slice_reduce_fusion
  29.9 3.0 %collective-permute-start.1 = (f32[1,128]{1,0:T(1,128)S(1)}, f32[1,128]{1,0:T(1,128)S(1)}, u32[]{:S(2)}, u32[]{:S(2)}) collective-permute-start(f32[1,128]{1,0:T(1,128)S(1)} %bitcast.31), channel_id=1, source_target_pairs={{0,2},{1,3},{2,0},{3,1},{4,6},{5,7},{6,4},{7,5},{8,10},{9,11},{10,... | collective-permute-start | bytes 1544 | tf_op jit(solution)/shard_map/ppermute | solution.py:563
  32.9 0.0 copy-done
  32.9 1.7 %coarse_edges.1 = (f32[3,16,4096]{2,1,0:T(8,128)S(1)}, f32[96,256]{1,0:T(8,128)S(1)}, f32[48,256]{1,0:T(8,128)S(1)}) custom-call(f32[3,16,4096]{2,1,0:T(8,128)S(1)} %get-tuple-element.23.cell, f32[3,16,4096]{2,1,0:T(8,128)S(1)} %get-tuple-element.24.b_c, bf16[2,256,256]{2,1,0:T(8,128)(2,1)S(1)} %copy-done), custom_call_target="tpu_custom_call" | custom-call | tf_op jit(solution)/shard_map/coarse_edges/pallas_call | solution.py:509
  34.6 0.0 copy-done.2
  34.6 1.5 %answers.1 = (f32[64,1,128]{2,1,0:T(1,128)S(1)}, f32[64,1,128]{2,1,0:T(1,128)S(1)}, f32[96,256]{1,0:T(8,128)S(1)}, f32[48,256]{1,0:T(8,128)S(1)}) custom-call(f32[64,1,384]{2,1,0:T(1,128)S(1)} %all_to_all.10.got, f32[96,256]{1,0:T(8,128)S(1)} %get-tuple-element.26.planes, f32[48,256]{1,0:T(8,128)S(1)} %get-tuple-element.27.quads_b, ...), custom_call_target="tpu_custom_call" | custom-call | tf_op jit(solution)/shard_map/answers/pallas_call | solution.py:509
  36.1 0.0 copy-start.7
  36.1 0.0 collective-permute-done.1
  36.2 0.6 %slice.11 = f32[1,1]{1,0:T(1,128)} slice(f32[1,128]{1,0:T(1,128)S(1)} %bitcast_maximum_fusion.top), slice={[0:1], [2:3]} | slice | bytes 8 | tf_op jit(solution)/shard_map/slice | solution.py:571
  37.4 0.6 %multiply_subtract_fusion = f32[8,8,128]{2,1,0:T(8,128)} fusion(f32[8,8,128]{2,1,0:T(8,128)S(1)} %bitcast.23, f32[8,8,128]{2,1,0:T(8,128)S(1)} %bitcast.24, f32[]{:T(128)} %bitcast.12), kind=kLoop, calls=%fused_computation.2 | loop fusion | flops 16384 | bytes 98308 | tf_op jit(solution)/shard_map/sub | solution.py:571
  38.1 0.0 copy-done.7
  38.1 4.7 %all-to-all-start.1 = ((f32[64,1,128]{2,1,0:T(1,128)}), f32[64,1,128]{2,1,0:T(1,128)S(1)}, u32[]{:S(2)}, u32[]{:S(2)}) async-start(f32[64,1,128]{2,1,0:T(1,128)} %bitcast.20), calls=%async_computation.1 | async-start | bytes 65536 | tf_op jit(solution)/shard_map/all_to_all | solution.py:572
  42.8 0.0 copy-start.8
  42.8 0.8 %copy-done.8 = f32[48,256]{1,0:T(8,128)S(1)} copy-done((f32[48,256]{1,0:T(8,128)S(1)}, f32[48,256]{1,0:T(8,128)}, u32[]{:S(2)}) %copy-start.8) | copy-done | bytes 49176
  43.6 1.9 %updates.1 = (f32[3,16,4096]{2,1,0:T(8,128)}, f32[12,96,128]{2,1,0:T(8,128)}, f32[48,256]{1,0:T(8,128)S(1)}) custom-call(f32[1,128]{1,0:T(1,128)S(1)} %bitcast_maximum_fusion.top, f32[3,16,4096]{2,1,0:T(8,128)S(1)} %get-tuple-element.25.emf_c, f32[96,256]{1,0:T(8,128)S(1)} %get-tuple-element.28.patch, f32[48,256]{1,0:T(8,128)S(1)} %copy-done.8, ...), custom_call_target="tpu_custom_call" | custom-call | tf_op jit(solution)/shard_map/updates/pallas_call | solution.py:509
  45.4 0.0 copy-start.5
  45.5 0.6 %copy-done.5 = f32[48,256]{1,0:T(8,128)} copy-done((f32[48,256]{1,0:T(8,128)}, f32[48,256]{1,0:T(8,128)S(1)}, u32[]{:S(2)}) %copy-start.5) | copy-done | bytes 49176
  46.0 6.1 %all-to-all-done.1.got = f32[64,1,128]{2,1,0:T(1,128)S(1)} async-done(((f32[64,1,128]{2,1,0:T(1,128)}), f32[64,1,128]{2,1,0:T(1,128)S(1)}, u32[]{:S(2)}, u32[]{:S(2)}) %all-to-all-start.1) | async-done | bytes 32800 | tf_op jit(solution)/shard_map/all_to_all | solution.py:572
  52.1 0.8 %copy-done.6 = f32[48,256]{1,0:T(8,128)S(1)} copy-done((f32[48,256]{1,0:T(8,128)S(1)}, f32[48,256]{1,0:T(8,128)}, u32[]{:S(2)}) %copy-start.6) | copy-done | bytes 49176
  52.9 0.5 face_jumps.1
  53.4 0.6 %copy.15 = f32[1,32,256]{2,1,0:T(8,128)} copy(f32[1,32,256]{2,1,0:T(8,128)S(1)} %bitcast.22) | data formatting | bytes 65536
  (9 shorter events, 0.0 us)
Async XLA Ops:
  0.6 4.7 %copy-start.1 = (bf16[2,512,128]{2,1,0:T(8,128)(2,1)S(1)}, bf16[2,512,128]{2,1,0:T(8,128)(2,1)}, u32[]{:S(2)}) copy-start(bf16[2,512,128]{2,1,0:T(8,128)(2,1)} %constant.17.clone.restrict) | copy-start | bytes 786436
  3.1 2.2 %copy-start.9 = (s32[1,32,6]{1,0,2:T(1,128)S(1)}, s32[1,32,6]{1,0,2:T(1,128)}, u32[]{:S(2)}) copy-start(s32[1,32,6]{1,0,2:T(1,128)} %param.14) | copy-start | bytes 2308
  3.1 3.6 %collective-permute-start = (f32[1,128]{1,0:T(1,128)S(1)}, f32[1,128]{1,0:T(1,128)S(1)}, u32[]{:S(2)}, u32[]{:S(2)}) collective-permute-start(f32[1,128]{1,0:T(1,128)S(1)} %get-tuple-element.20), channel_id=1, source_target_pairs={{0,1},{1,0},{2,3},{3,2},{4,5},{5,4},{6,7},{7,6},{8,9},{9,8},{10,11... | collective-permute-start | bytes 1544 | tf_op jit(solution)/shard_map/ppermute | solution.py:548
  6.6 26.3 %copy-start = (bf16[2,256,256]{2,1,0:T(8,128)(2,1)S(1)}, bf16[2,256,256]{2,1,0:T(8,128)(2,1)}, u32[]{:S(2)}) copy-start(bf16[2,256,256]{2,1,0:T(8,128)(2,1)} %constant.19.clone.quadrant) | copy-start | bytes 786436
  29.9 6.3 %collective-permute-start.1 = (f32[1,128]{1,0:T(1,128)S(1)}, f32[1,128]{1,0:T(1,128)S(1)}, u32[]{:S(2)}, u32[]{:S(2)}) collective-permute-start(f32[1,128]{1,0:T(1,128)S(1)} %bitcast.31), channel_id=1, source_target_pairs={{0,2},{1,3},{2,0},{3,1},{4,6},{5,7},{6,4},{7,5},{8,10},{9,11},{10,... | collective-permute-start | bytes 1544 | tf_op jit(solution)/shard_map/ppermute | solution.py:563
  32.9 1.7 %copy-start.2 = (bf16[2,128,256]{2,1,0:T(8,128)(2,1)S(1)}, bf16[2,128,256]{2,1,0:T(8,128)(2,1)}, u32[]{:S(2)}) copy-start(bf16[2,128,256]{2,1,0:T(8,128)(2,1)} %constant.18.clone.expand) | copy-start | bytes 393220
  36.1 1.9 %copy-start.7 = (f32[48,256]{1,0:T(8,128)}, f32[48,256]{1,0:T(8,128)S(1)}, u32[]{:S(2)}) copy-start(f32[48,256]{1,0:T(8,128)S(1)} %get-tuple-element.29.masks) | copy-start | bytes 147460
  38.1 14.1 %all-to-all-start.1 = ((f32[64,1,128]{2,1,0:T(1,128)}), f32[64,1,128]{2,1,0:T(1,128)S(1)}, u32[]{:S(2)}, u32[]{:S(2)}) async-start(f32[64,1,128]{2,1,0:T(1,128)} %bitcast.20), calls=%async_computation.1 | async-start | bytes 65536 | tf_op jit(solution)/shard_map/all_to_all | solution.py:572
  42.8 0.8 %copy-start.8 = (f32[48,256]{1,0:T(8,128)S(1)}, f32[48,256]{1,0:T(8,128)}, u32[]{:S(2)}) copy-start(f32[48,256]{1,0:T(8,128)} %copy-done.7) | copy-start | bytes 147460
  43.6 8.6 %copy-start.3 = (bf16[256,256]{1,0:T(8,128)(2,1)S(1)}, bf16[256,256]{1,0:T(8,128)(2,1)}, u32[]{:S(2)}) copy-start(bf16[256,256]{1,0:T(8,128)(2,1)} %constant.20.clone.flip) | copy-start | bytes 393220
  43.6 8.6 %copy-start.4 = (bf16[128,256]{1,0:T(8,128)(2,1)S(1)}, bf16[128,256]{1,0:T(8,128)(2,1)}, u32[]{:S(2)}) copy-start(bf16[128,256]{1,0:T(8,128)(2,1)} %constant.21.clone.prolong) | copy-start | bytes 196612
  45.4 0.6 %copy-start.5 = (f32[48,256]{1,0:T(8,128)}, f32[48,256]{1,0:T(8,128)S(1)}, u32[]{:S(2)}) copy-start(f32[48,256]{1,0:T(8,128)S(1)} %get-tuple-element.36.normals) | copy-start | bytes 147460
  52.1 0.8 %copy-start.6 = (f32[48,256]{1,0:T(8,128)S(1)}, f32[48,256]{1,0:T(8,128)}, u32[]{:S(2)}) copy-start(f32[48,256]{1,0:T(8,128)} %copy-done.5) | copy-start | bytes 147460

commit v2 on v1

--- a/solution.py
+++ b/solution.py
@@ -1,6 +1,5 @@
 import jax
 import jax.numpy as jnp
-import numpy as np
 from jax import lax
 from jax.experimental import pallas as pl
 from jax.experimental.pallas import tpu as pltpu
@@ -23,64 +22,51 @@
 UNROLL = 16
 
 
-def _face_lane(row, col, flip):
+def grid_of(rows, cols):
+    return (
+        lax.broadcasted_iota(jnp.int32, (rows, cols), 0),
+        lax.broadcasted_iota(jnp.int32, (1, cols), 1),
+    )
+
+
+def face_lane(row, col, flip):
     return col * EDGE + row if flip else row * EDGE + col
 
 
-def _restrict_matrix(flip):
-    out = np.zeros((2, WIDE, 128), np.float32)
-    for m in range(HALF):
-        for n in range(HALF):
-            o = m * HALF + n
-            out[0, _face_lane(2 * m, 2 * n, flip), o] = 0.5
-            out[0, _face_lane(2 * m + 1, 2 * n, flip), o] = 0.5
-            out[1, _face_lane(2 * m, 2 * n, flip), 64 + o] = 0.5
-            out[1, _face_lane(2 * m, 2 * n + 1, flip), 64 + o] = 0.5
-    return out.reshape(2 * WIDE, 128)
-
-
-def _expand_matrix(flip):
-    out = np.zeros((128, 256), np.float32)
-    for m in range(HALF):
-        for n in range(HALF):
-            o = m * HALF + n
-            out[o, _face_lane(m, n, flip)] = 1.0
-            out[64 + o, 128 + _face_lane(m, n, flip)] = 1.0
-    return out
-
-
-def _quadrant_matrix(flip):
-    out = np.zeros((WIDE, WIDE), np.float32)
-    for row in range(EDGE):
-        for col in range(EDGE):
-            quad = (row // HALF) * 2 + col // HALF
-            out[_face_lane(row, col, flip), quad * 64 + (row % HALF) * HALF + col % HALF] = 1.0
-    return out
-
-
-def _flip_matrix():
-    out = np.zeros((WIDE, WIDE), np.float32)
-    for row in range(EDGE):
-        for col in range(EDGE):
-            out[_face_lane(row, col, True), _face_lane(row, col, False)] = 1.0
-    return out
-
-
-def _prolong_matrix():
-    out = np.zeros((128, WIDE), np.float32)
-    for row in range(EDGE):
-        for col in range(EDGE):
-            o = (row // 2) * HALF + col // 2
-            out[o, _face_lane(row, col, False)] = 1.0
-            out[64 + o, _face_lane(row, col, False)] = 1.0
-    return out
-
-
-RESTRICT = np.stack([_restrict_matrix(False), _restrict_matrix(True)])
-EXPAND = np.stack([_expand_matrix(False), _expand_matrix(True)])
-QUADRANT = np.stack([_quadrant_matrix(False), _quadrant_matrix(True)])
-FLIP = _flip_matrix()
-PROLONG = _prolong_matrix()
+def as_matrix(where, value=1.0):
+    return jnp.where(where, value, 0.0).astype(BF16)
+
+
+def restrict_matrix(flip):
+    at, to = grid_of(WIDE, 128)
+    m, n = (to >> 3) & 7, to & 7
+    base = face_lane(2 * m, 2 * n, flip)
+    firsts = (to < 64) & ((at == base) | (at == base + face_lane(1, 0, flip)))
+    seconds = (to >= 64) & ((at == base) | (at == base + face_lane(0, 1, flip)))
+    return jnp.concatenate([as_matrix(firsts, 0.5), as_matrix(seconds, 0.5)], axis=0)
+
+
+def expand_matrix(flip):
+    at, _ = grid_of(128, 256)
+    to = lax.broadcasted_iota(jnp.int32, (128, 256), 1)
+    place = face_lane((at >> 3) & 7, at & 7, flip)
+    return as_matrix(((at >> 6) == (to >> 7)) & (place == (to & 127)))
+
+
+def quadrant_matrix(flip):
+    at, to = grid_of(WIDE, WIDE)
+    row, col = (to >> 7) * HALF + ((to >> 3) & 7), ((to >> 6) & 1) * HALF + (to & 7)
+    return as_matrix(at == face_lane(row, col, flip))
+
+
+def flip_matrix():
+    at, to = grid_of(WIDE, WIDE)
+    return as_matrix(at == (to & 15) * EDGE + (to >> 4))
+
+
+def prolong_matrix():
+    at, to = grid_of(128, WIDE)
+    return as_matrix((at & 63) == (to >> 5) * HALF + ((to & 15) >> 1))
 
 
 def halves(value):
@@ -208,25 +194,68 @@
     return first, second, source
 
 
-def cells_kernel(cb, cv, fb, fv, cell_c, cell_f, b_c, b_f, speed, v_c, v_f, sems):
-    fine_copies = fetch_fine(fb, b_f, sems.at[0]) + fetch_fine(fv, v_f, sems.at[1])
+def edges(cell, emf):
+    last = [slab(cell, c, EDGE - 1, 0, CB) for c in range(3)]
+    now = last
+    add = lambda a, b: a + b
+    quarter = lambda a, b: 0.25 * (a + b)
+    for i in reversed(range(EDGE)):
+        prior = [slab(cell, c, i - 1, 0, CB) for c in range(3)] if i else last
+        sum_x = each(add, now[0], y_prev(now[0]))
+        sum_y = each(add, now[1], prior[1])
+        sum_z = each(add, now[2], prior[2])
+        put_slab(emf, 0, i, 0, CB, each(quarter, sum_x, z_prev(sum_x)))
+        put_slab(emf, 1, i, 0, CB, each(quarter, sum_y, z_prev(sum_y)))
+        put_slab(emf, 2, i, 0, CB, each(quarter, sum_z, y_prev(sum_z)))
+        now = prior
+
+
+def face_of(ref, along, d):
+    if d == 0:
+        return slab(ref, along, 0, 0, CB)
+    if d == 1:
+        return face_row_wise(lambda i: slab(ref, along, i, 0, CB)[0])
+    return face_column_wise(lambda i: slab(ref, along, i, 0, CB))
+
+
+def first_kernel(
+    cb, cv, fb, fv, far_pairs,
+    send, cell_c, emf_f, b_f,
+    b_c, v_c, pitched_b, v_f, pairs, out, sems,
+):
+    fine_copies = fetch_fine(fb, pitched_b, sems.at[0]) + fetch_fine(fv, v_f, sems.at[1])
     coarse_copies = [
-        pltpu.make_async_copy(cb, b_c, sems.at[2]),
-        pltpu.make_async_copy(cv, v_c, sems.at[3]),
+        [
+            pltpu.make_async_copy(far.at[:, :, part], near.at[:, :, part], sems.at[2 + q])
+            for far, near in ((cb, b_c), (cv, v_c))
+        ]
+        for q, part in enumerate(pl.ds(q * 4 * WIDE, 4 * WIDE) for q in range(4))
     ]
-    for copy in fine_copies + coarse_copies:
+    pairs_copy = pltpu.make_async_copy(far_pairs, pairs, sems.at[6])
+    for copy in [pairs_copy, *fine_copies, *sum(coarse_copies, [])]:
         copy.start()
     idle = pl.ds(FB * PITCH, (CB - FB) * PITCH)
-    b_f[idle, :] = jnp.zeros(((CB - FB) * PITCH, 128), F32)
+    pitched_b[idle, :] = jnp.zeros(((CB - FB) * PITCH, 128), F32)
     v_f[idle, :] = jnp.zeros(((CB - FB) * PITCH, 128), F32)
-
-    def cells(load_b, load_v, cell):
-        def step(i, top):
-            following = lax.rem(i + 1, EDGE)
+    pairs_copy.wait()
+    first, second, source = routes(pairs)
+    nt = ((1,), (1,))
+    key = (pairs[1] * 64 + (pairs[4] * 2 + pairs[5]) * CB + pairs[3] + 1).astype(F32)
+    lane = lax.broadcasted_iota(jnp.int32, (PEERS, 128), 1)
+    meta = jnp.zeros((PEERS, 128), F32)
+    picks = []
+    for k, chosen in enumerate((first, second)):
+        picks.append(mm(chosen.astype(BF16), source.astype(BF16), nt).astype(BF16))
+        meta = jnp.where(lane == k, jnp.sum(chosen * key, axis=1, keepdims=True), meta)
+
+    def cells(load_b, load_v, cell, ready):
+        top = jnp.zeros((CB, 128), F32)
+        for i in range(EDGE):
+            ready(i)
             bx, by, bz = load_b(0, i), load_b(1, i), load_b(2, i)
             vx, vy, vz = load_v(0, i), load_v(1, i), load_v(2, i)
             mean = lambda a, b: 0.5 * (a + b)
-            cx = each(mean, bx, load_b(0, following))
+            cx = each(mean, bx, load_b(0, (i + 1) % EDGE))
             cy = each(mean, by, y_next(by))
             cz = each(mean, bz, z_next(bz))
             cross = lambda a, b, c, d: a * b - c * d
@@ -235,68 +264,61 @@
             put_slab(cell, 2, i, 0, CB, each(cross, vy, cx, vx, cy))
             size = lambda a, b, c: jnp.sqrt(a * a + b * b + c * c)
             fast = each(lambda a, b: a + b, each(size, vx, vy, vz), each(size, cx, cy, cz))
-            return jnp.maximum(top, jnp.maximum(fast[0], fast[1]))
-
-        return lax.fori_loop(0, EDGE, step, jnp.zeros((CB, 128), F32), unroll=UNROLL)
+            top = jnp.maximum(top, jnp.maximum(fast[0], fast[1]))
+        return top
 
     for copy in fine_copies:
         copy.wait()
-    top_fine = cells(lambda c, i: fine_slab(b_f, c, i), lambda c, i: fine_slab(v_f, c, i), cell_f)
-    for copy in coarse_copies:
-        copy.wait()
-    top_coarse = cells(
-        lambda c, i: slab(b_c, c, i, 0, CB), lambda c, i: slab(v_c, c, i, 0, CB), cell_c
-    )
-    top = jnp.max(jnp.maximum(top_fine, top_coarse), axis=0, keepdims=True)
-    speed[...] = jnp.broadcast_to(jnp.max(top, axis=1, keepdims=True), (1, 128))
-
-
-def edges(cell, emf):
-    def step(i, carry):
-        prior = lax.rem(i + EDGE - 1, EDGE)
-        add = lambda a, b: a + b
-        quarter = lambda a, b: 0.25 * (a + b)
-        ex = slab(cell, 0, i, 0, CB)
-        sum_x = each(add, ex, y_prev(ex))
-        put_slab(emf, 0, i, 0, CB, each(quarter, sum_x, z_prev(sum_x)))
-        sum_y = each(add, slab(cell, 1, i, 0, CB), slab(cell, 1, prior, 0, CB))
-        put_slab(emf, 1, i, 0, CB, each(quarter, sum_y, z_prev(sum_y)))
-        sum_z = each(add, slab(cell, 2, i, 0, CB), slab(cell, 2, prior, 0, CB))
-        put_slab(emf, 2, i, 0, CB, each(quarter, sum_z, y_prev(sum_z)))
-        return carry
-
-    lax.fori_loop(0, EDGE, step, 0, unroll=UNROLL)
-
-
-def face_of(ref, along, d):
-    if d == 0:
-        return slab(ref, along, 0, 0, CB)
-    if d == 1:
-        return face_row_wise(lambda i: slab(ref, along, i, 0, CB)[0])
-    return face_column_wise(lambda i: slab(ref, along, i, 0, CB))
-
-
-def rows_kernel(cell, pairs, restrict, send, emf):
-    edges(cell, emf)
-    first, second, source = routes(pairs)
+    held = {}
+
+    def fine_b(c, i):
+        if (c, i) not in held:
+            held[c, i] = fine_slab(pitched_b, c, i)
+            put_slab(b_f, c, i, 0, CB, held[c, i])
+        return held[c, i]
+
+    top_fine = cells(fine_b, lambda c, i: fine_slab(v_f, c, i), emf_f, lambda i: None)
+    edges(emf_f, emf_f)
+    restrict = [restrict_matrix(False), restrict_matrix(True)]
     rows = []
     for d in range(3):
-        planes = [face_of(emf, along, d) for along in TANGENT[d]]
+        planes = [face_of(emf_f, along, d) for along in TANGENT[d]]
         both = jnp.concatenate([*planes[0], *planes[1]], axis=1)
         rows.append(mm_left(both, restrict[1 if d == 2 else 0]))
     rows = jnp.concatenate(rows, axis=0)
-    nt = ((1,), (1,))
-    key = (pairs[1] * 64 + (pairs[4] * 2 + pairs[5]) * CB + pairs[3] + 1).astype(F32)
-    lane = lax.broadcasted_iota(jnp.int32, (PEERS, 128), 1)
-    meta = jnp.zeros((PEERS, 128), F32)
-    for k, chosen in enumerate((first, second)):
-        pick = mm(chosen.astype(BF16), source.astype(BF16), nt)
-        send[:, 0, k * 128 : (k + 1) * 128] = mm_right(pick.astype(BF16), rows)
-        meta = jnp.where(lane == k, jnp.sum(chosen * key, axis=1, keepdims=True), meta)
-    send[:, 0, 256:384] = meta
-
-
-def coarse_kernel(cell, b_c, quadrant, emf, planes, quads):
+    for k in range(2):
+        out[:, 0, k * 128 : (k + 1) * 128] = mm_right(picks[k], rows)
+    rows_copy = pltpu.make_async_copy(
+        out.at[:, :, pl.ds(0, 256)], send.at[:, :, pl.ds(0, 256)], sems.at[7]
+    )
+    rows_copy.start()
+
+    def coarse_ready(i):
+        for q in range(4):
+            if i == max(4 * q - 1, 0):
+                for copy in coarse_copies[q]:
+                    copy.wait()
+
+    top_coarse = cells(
+        lambda c, i: slab(b_c, c, i, 0, CB),
+        lambda c, i: slab(v_c, c, i, 0, CB),
+        cell_c,
+        coarse_ready,
+    )
+    top = jnp.max(jnp.maximum(top_fine, top_coarse), axis=0, keepdims=True)
+    top = jnp.broadcast_to(jnp.max(top, axis=1, keepdims=True), (PEERS, 128))
+    out[:, 0, 256:384] = jnp.where(lane < 2, meta, top)
+    meta_copy = pltpu.make_async_copy(
+        out.at[:, :, pl.ds(256, 128)], send.at[:, :, pl.ds(256, 128)], sems.at[8]
+    )
+    meta_copy.start()
+    rows_copy.wait()
+    meta_copy.wait()
+
+
+def coarse_kernel(cell, cb, emf, far_planes, quads, b_c, planes, sems):
+    load = pltpu.make_async_copy(cb, b_c, sems.at[0])
+    load.start()
     edges(cell, emf)
     for d in range(3):
         for t in range(2):
@@ -304,11 +326,25 @@
             face = face_of(emf, TANGENT[d][t], d)
             planes[at : at + CB, 0:128] = face[0]
             planes[at : at + CB, 128:256] = face[1]
+    store = pltpu.make_async_copy(planes, far_planes, sems.at[1])
+    store.start()
+    quadrant = [quadrant_matrix(False), quadrant_matrix(True)]
+    load.wait()
+    for d in range(3):
         normal = jnp.concatenate(face_of(b_c, d, d), axis=1)
         quads[d * CB : (d + 1) * CB, :] = mm_left(normal, quadrant[1 if d == 2 else 0])
-
-
-def answer_kernel(got, planes, quads_b, expand, quadrant, rows_b, rows_c, patch, masks):
+    store.wait()
+
+
+def answer_kernel(
+    got, far_planes, quads_b, cb, back, far_patch, masks, b_c, planes, patch, out, sems
+):
+    load = pltpu.make_async_copy(cb, b_c, sems.at[0])
+    load_planes = pltpu.make_async_copy(far_planes, planes, sems.at[1])
+    load_planes.start()
+    load.start()
+    expand = [expand_matrix(False), expand_matrix(True)]
+    quadrant = [quadrant_matrix(False), quadrant_matrix(True)]
     meta = got[:, 0, 256:384]
     keys = [meta[:, k : k + 1].astype(jnp.int32) - 1 for k in range(2)]
     target = lax.broadcasted_iota(jnp.int32, (PEERS, 256), 1)
@@ -343,13 +379,17 @@
         (d, t): value(d, t, int(d == 2)) for d in range(3) for t in range(2)
     } | {"1x": value(1, 0, 1), "2x": value(2, 0, 0)}
     hits = {d: mask(d, int(d == 2)) for d in range(3)} | {"1x": mask(1, 1), "2x": mask(2, 0)}
-    for d in range(3):
-        for h in range(2):
-            side = slice(h * 128, (h + 1) * 128)
-            masks[d * CB : (d + 1) * CB, side] = hits[d][h].astype(F32)
+    for h in range(2):
+        side = slice(h * 128, (h + 1) * 128)
+        masks[:, side] = sum(hits[d][h].astype(F32) * 2.0**d for d in range(3))
+        for d in range(3):
             for t in range(2):
                 first = (d * 2 + t) * CB
                 patch[first : first + CB, side] = value[d, t][h]
+
+    store = pltpu.make_async_copy(patch, far_patch, sems.at[2])
+    store.start()
+    load_planes.wait()
 
     def face(d, t):
         first = (d * 2 + t) * CB
@@ -389,7 +429,7 @@
     )
     wide_lane = lax.broadcasted_iota(jnp.int32, (PEERS, 3 * CB), 1)
     out_lane = lax.broadcasted_iota(jnp.int32, (PEERS, 128), 1)
-    for out, quads in ((rows_b, quads_b[...]), (rows_c, quads_c)):
+    for part, quads in enumerate((quads_b[...], quads_c)):
         answers = []
         for k in range(2):
             key = keys[k]
@@ -399,12 +439,23 @@
             quad = (key >> 4) & 3
             side = jnp.where(quad >= 2, found[:, 128:256], found[:, 0:128])
             answers.append(jnp.where((quad & 1) == k, side, pltpu.roll(side, 64, 1)))
-        out[:, 0, :] = jnp.where(out_lane < 64, answers[0], answers[1])
+        side = slice(part * 128, (part + 1) * 128)
+        out[:, 0, side] = jnp.where(out_lane < 64, answers[0], answers[1])
+    send = pltpu.make_async_copy(out, back, sems.at[3])
+    send.start()
+    for copy in (load, store, send):
+        copy.wait()
 
 
 def update_kernel(
-    top, emf_c, patch, masks, emf_f, b_c, b_f, new_c, new_f, normals, emf, out_c, out_f, sems
+    top, emf_c, far_patch, masks, emf_f, b_c, b_f, far_pairs,
+    new_c, new_f, picked, chosen,
+    emf, out_c, out_f, pairs, patch, sems,
 ):
+    load = pltpu.make_async_copy(far_pairs, pairs, sems.at[2])
+    load_patch = pltpu.make_async_copy(far_patch, patch, sems.at[3])
+    load_patch.start()
+    load.start()
     time_step = 0.2 / top[0:1, 2:3]
     lane = lax.broadcasted_iota(jnp.int32, (CB, 128), 1)
 
@@ -425,7 +476,7 @@
     update(
         emf_f,
         time_step / 0.5,
-        lambda c, i: fine_slab(b_f, c, i),
+        lambda c, i: slab(b_f, c, i, 0, CB),
         lambda c, i, value: put_fine_slab(out_f, c, i, value),
         lambda i: None,
     )
@@ -436,8 +487,10 @@
     for copy in results:
         copy.start()
 
+    load_patch.wait()
     planes = {(d, t): pair(patch, (d * 2 + t) * CB) for d in range(3) for t in range(2)}
-    hits = [pair(masks, d * CB) for d in range(3)]
+    bits = [m.astype(jnp.int32) for m in pair(masks, 0)]
+    hits = [[((m >> d) & 1).astype(F32) for m in bits] for d in range(3)]
     for i in range(EDGE):
         now = {c: slab(emf_c, c, i, 0, CB) for c in range(3)}
         if i == 0:
@@ -474,37 +527,46 @@
         face_row_wise(lambda i: fine_slab(out_f, 1, i)[0]),
         face_column_wise(lambda i: fine_slab(out_f, 2, i)),
     )
-    for d in range(3):
-        normals[d * CB : (d + 1) * CB, 0:128] = faces[d][0]
-        normals[d * CB : (d + 1) * CB, 128:256] = faces[d][1]
+    load.wait()
+    first, second, source = routes(pairs)
+    tn = ((0,), (0,))
+    same = (
+        lax.broadcasted_iota(jnp.int32, (PEERS, PEERS), 0)
+        == lax.broadcasted_iota(jnp.int32, (PEERS, PEERS), 1)
+    ).astype(F32).astype(BF16)
+    chosen[...] = jnp.concatenate(
+        [mm(first.astype(BF16), same, tn), mm(second.astype(BF16), same, tn)], axis=1
+    )
+    source = source.astype(BF16)
+    flip = flip_matrix()
+    normals = [jnp.concatenate(face, axis=1) for face in faces]
+    straight = mm_right(source[0 : 2 * CB], jnp.concatenate(normals[0:2], axis=0), tn)
+    flipped = mm_left(mm_right(source[2 * CB :], normals[2], tn), flip)
+    picked[...] = straight + flipped
     for copy in results:
         copy.wait()
 
 
-def third_kernel(got, normals, pairs, flip, prolong, jump):
-    first, second, source = routes(pairs)
-    tn = ((0,), (0,))
-    rows = got[:, 0, :]
+def third_kernel(got, top, picked, chosen, jump, held, sems):
+    rows = got[:, 0, 0:128] - (0.2 / top[0:1, 2:3]) * got[:, 0, 128:256]
     lane = lax.broadcasted_iota(jnp.int32, (PAIRS, 128), 1)
-    own = jnp.where(
-        lane < 64,
-        mm_right(first.astype(BF16), rows, tn),
-        mm_right(second.astype(BF16), rows, tn),
-    )
-    coarse = mm_left(own, prolong[...])
-    source = source.astype(BF16)
-    straight = mm_right(source[0 : 2 * CB], normals[0 : 2 * CB], tn)
-    flipped = mm_left(mm_right(source[2 * CB :], normals[2 * CB :], tn), flip[...])
-    jump[...] = straight + flipped - coarse
+    picks = chosen[...].astype(BF16)
+    sides = [mm_right(picks[:, k * PEERS : (k + 1) * PEERS], rows) for k in range(2)]
+    own = jnp.where(lane < 64, sides[0], sides[1])
+    held[...] = picked[...] - mm_left(own, prolong_matrix())
+    copy = pltpu.make_async_copy(held, jump, sems.at[0])
+    copy.start()
+    copy.wait()
 
 
 VMEM = pl.BlockSpec(memory_space=pltpu.VMEM)
 HBM = pl.BlockSpec(memory_space=pltpu.HBM)
 FIELD = (3, CB, CELLS)
 PITCHED = (CB * PITCH, 128)
-
-
-def call(kernel, name, outs, args, scratch=()):
+FACES = (6 * CB, WIDE)
+
+
+def call(kernel, name, outs, args, scratch=(), aliases=None):
     far = [isinstance(out, tuple) and out[0] == "hbm" for out in outs]
     return pl.pallas_call(
         kernel,
@@ -515,6 +577,7 @@
         in_specs=[HBM if is_far else VMEM for _, is_far in args],
         out_specs=[HBM if is_far else VMEM for is_far in far],
         scratch_shapes=list(scratch),
+        input_output_aliases=aliases or {},
         compiler_params=pltpu.CompilerParams(vmem_limit_bytes=24 * 1024 * 1024),
         name=name,
     )(
@@ -531,62 +594,61 @@
     fb = fine_field[0].reshape(FB, 96, 128)
     fv = fine_velocity[0].reshape(FB, 96, 128)
     rows = pairs.transpose(2, 0, 1)
-    restrict, expand, quadrant, flip, prolong = (
-        jnp.asarray(x, BF16) for x in (RESTRICT, EXPAND, QUADRANT, FLIP, PROLONG)
-    )
     near = lambda *arrays: [(a, False) for a in arrays]
     far = lambda *arrays: [(a, True) for a in arrays]
     count = lax.axis_size("gz")
 
-    cell_c, cell_f, b_c, b_f, speed = call(
-        cells_kernel,
-        "cells",
-        [FIELD, FIELD, FIELD, PITCHED, (1, 128)],
-        far(cb, cv, fb, fv),
-        [pltpu.VMEM(FIELD, F32), pltpu.VMEM(PITCHED, F32), pltpu.SemaphoreType.DMA((4,))],
-    )
-    other = lax.ppermute(speed, "gz", [(i, i ^ 1) for i in range(count)])
-    send, emf_f = call(
-        rows_kernel, "rows", [(PEERS, 1, 384), FIELD], near(cell_f, rows, restrict)
-    )
-    speed = jnp.maximum(speed, other)
-    lane = lax.broadcasted_iota(jnp.int32, send.shape, 2)
-    send = jnp.where(lane == 258, speed[0, 0], send)
+    field = pltpu.VMEM(FIELD, F32)
+    pitched = pltpu.VMEM(PITCHED, F32)
+    small = pltpu.VMEM((6, 1, PAIRS), jnp.int32)
+    sems = pltpu.SemaphoreType.DMA
+    send, cell_c, emf_f, b_f = call(
+        first_kernel,
+        "speeds_and_rows",
+        [("hbm", (PEERS, 1, 384)), FIELD, FIELD, FIELD],
+        far(cb, cv, fb, fv, rows),
+        [field, field, pitched, pitched, small, pltpu.VMEM((PEERS, 1, 384), F32), sems((9,))],
+    )
     got = lax.all_to_all(send, BLOCKS, 0, 0, tiled=True)
     emf_c, planes, quads = call(
         coarse_kernel,
         "coarse_edges",
-        [FIELD, (6 * CB, WIDE), (3 * CB, WIDE)],
-        near(cell_c, b_c, quadrant),
-    )
+        [FIELD, ("hbm", FACES), (3 * CB, WIDE)],
+        near(cell_c) + far(cb),
+        [field, pltpu.VMEM(FACES, F32), sems((2,))],
+        {0: 0},
+    )
+    got, emf_c, planes, quads = lax.optimization_barrier((got, emf_c, planes, quads))
     top = jnp.max(got[:, :, 256:384], axis=0)
-    other = lax.ppermute(top, "gz", [(i, i ^ 2) for i in range(count)])
-    rows_b, rows_c, patch, masks = call(
+    top = jnp.maximum(top, lax.ppermute(top, "gz", [(i, i ^ 1) for i in range(count)]))
+    back, patch, masks, b_c = call(
         answer_kernel,
         "answers",
-        [(PEERS, 1, 128), (PEERS, 1, 128), (6 * CB, WIDE), (3 * CB, WIDE)],
-        near(got, planes, quads, expand, quadrant),
-    )
-    top = jnp.maximum(top, other)
-    back = rows_b - (0.2 / top[0, 2]) * rows_c
+        [("hbm", (PEERS, 1, 256)), ("hbm", FACES), (CB, WIDE), FIELD],
+        near(got) + far(planes) + near(quads) + far(cb),
+        [
+            pltpu.VMEM(FACES, F32),
+            pltpu.VMEM(FACES, F32),
+            pltpu.VMEM((PEERS, 1, 256), F32),
+            sems((4,)),
+        ],
+    )
+    back, top = lax.optimization_barrier((back, top))
+    top = jnp.maximum(top, lax.ppermute(top, "gz", [(i, i ^ 2) for i in range(count)]))
     returned = lax.all_to_all(back, BLOCKS, 0, 0, tiled=True)
-    new_c, new_f, normals = call(
+    new_c, new_f, picked, chosen = call(
         update_kernel,
         "updates",
-        [("hbm", FIELD), ("hbm", (FB, 96, 128)), (3 * CB, WIDE)],
-        near(top, emf_c, patch, masks, emf_f, b_c, b_f),
-        [
-            pltpu.VMEM(FIELD, F32),
-            pltpu.VMEM(FIELD, F32),
-            pltpu.VMEM(PITCHED, F32),
-            pltpu.SemaphoreType.DMA((2,)),
-        ],
+        [("hbm", FIELD), ("hbm", (FB, 96, 128)), (PAIRS, WIDE), (PAIRS, 128)],
+        near(top, emf_c) + far(patch) + near(masks, emf_f, b_c, b_f) + far(rows),
+        [field, field, pitched, small, pltpu.VMEM(FACES, F32), sems((4,))],
     )
     (jump,) = call(
         third_kernel,
         "face_jumps",
-        [(PAIRS, WIDE)],
-        near(returned, normals, rows, flip, prolong),
+        [("hbm", (PAIRS, WIDE))],
+        near(returned, top, picked, chosen),
+        [pltpu.VMEM((PAIRS, WIDE), F32), sems((1,))],
     )
     return (
         new_c.transpose(1, 0, 2)[None],

time: 54.4 us -> 48.5 us (0.89)
  blocking collectives: 23 us -> 0 us
  starting transfers between devices: 9.89 us -> 21.8 us
  waiting for transfers between devices: 6.07 us -> 12 us
  Pallas kernels: 9.34 us -> 13.6 us
  local copies, waits for them, and re-layouts: 3.43 us -> 0 us
  between operations: 1.47 us -> 0.7 us
  other arithmetic: 0.82 us -> 0.09 us
    all_to_all x1 -> x0, blocking collectives: 23 us -> none  [on_device(): got = lax.all_to_all(send, BLOCKS, 0, 0, tiled=True)]
    all_to_all x0 -> x1, starting transfers between devices: none -> 13 us  [on_device(): got = lax.all_to_all(send, BLOCKS, 0, 0, tiled=True)]
    all_to_all x0 -> x1, waiting for transfers between devices: none -> 7.25 us  [on_device(): got = lax.all_to_all(send, BLOCKS, 0, 0, tiled=True)]
    pallas_call x6 -> x5, Pallas kernels: 9.34 us -> 13.6 us  [call(): pl.pallas_call(kernel, out_shape=[pltpu.HBM(out[1], F32) if is_far else p...]
    unnamed x21 -> x0, local copies, waits for them, and re-layouts: 2.85 us -> none
    all_to_all x1, waiting for transfers between devices: 6.07 us -> 3.5 us  [on_device(): returned = lax.all_to_all(back, BLOCKS, 0, 0, tiled=True)]
    ppermute x2, waiting for transfers between devices: 0.01 us -> 1.3 us  [the longest x1 1.3 us: on_device(): lax.ppermute(top, 'gz', [(i, i ^ 2) for i in range(count)])]
    ppermute x2, starting transfers between devices: 5.19 us -> 4.08 us  [the longest x1 2.71 us: on_device(): lax.ppermute(top, 'gz', [(i, i ^ 2) for i in range(count)])]
  transfers between devices with their start and end apart: 3 -> 4, of which waited for: 1 -> 3; matrix products, arithmetic and copies ran while one was open for 0% -> 0% of each run, Pallas kernels for 12% -> 16%
where the time goes in v2:
time: 48.5 us; the launch traced here: 48.2 us
  starting transfers between devices  21.8 us (45%)
  Pallas kernels  13.6 us (28%)
  waiting for transfers between devices  12 us (25%)
  between operations  0.7 us (1%)
    pallas_call x5, Pallas kernels, call(): pl.pallas_call(kernel, out_shape=[pltpu.HBM(out[1], F32) if is_far else p...  13.6 us
    all_to_all x1, starting transfers between devices, on_device(): got = lax.all_to_all(send, BLOCKS, 0, 0, tiled=True)  13 us
    all_to_all x1, waiting for transfers between devices, on_device(): got = lax.all_to_all(send, BLOCKS, 0, 0, tiled=True)  7.25 us
    all_to_all x1, starting transfers between devices, on_device(): returned = lax.all_to_all(back, BLOCKS, 0, 0, tiled=True)  4.68 us
    all_to_all x1, waiting for transfers between devices, on_device(): returned = lax.all_to_all(back, BLOCKS, 0, 0, tiled=True)  3.5 us
    ppermute x1, starting transfers between devices, on_device(): lax.ppermute(top, 'gz', [(i, i ^ 2) for i in range(count)])  2.71 us
    ppermute x1, starting transfers between devices, on_device(): lax.ppermute(top, 'gz', [(i, i ^ 1) for i in range(count)])  1.37 us
    ppermute x1, waiting for transfers between devices, on_device(): lax.ppermute(top, 'gz', [(i, i ^ 2) for i in range(count)])  1.3 us
  transfers between devices with their start and end apart: 4, of which 3 were waited for; matrix products, arithmetic and copies ran while one was open for 0% of the time, Pallas kernels for 16%

profile of v2, /device:TPU:1, one launch (start us, length us, event | category | flops | bytes accessed | tf_op | source)
XLA Modules:
  0.0 48.2 jit_solution(10199290532474682628)
XLA Ops:
  0.6 4.6 %speeds_and_rows.1 = (f32[64,1,384]{2,1,0:T(1,128)}, f32[3,16,4096]{2,1,0:T(8,128)S(1)}, f32[3,16,4096]{2,1,0:T(8,128)S(1)}, f32[3,16,4096]{2,1,0:T(8,128)S(1)}) custom-call(f32[3,16,4096]{2,1,0:T(8,128)} %bitcast.16, f32[3,16,4096]{2,1,0:T(8,128)} %bitcast.19, f32[12,96,128]{2,1,0:T(8,128)} %bitcast.20, f32[12,96,128]{2,1,0:T(8,128)} %bitcast.21, ...), custom_call_target="tpu_custom_call" | custom-call | tf_op jit(solution)/shard_map/speeds_and_rows/pallas_call | solution.py:571
  5.2 13.0 %all-to-all-start = ((f32[64,1,384]{2,1,0:T(1,128)}), f32[64,1,384]{2,1,0:T(1,128)S(1)}, u32[]{:S(2)}, u32[]{:S(2)}) async-start(f32[64,1,384]{2,1,0:T(1,128)} %get-tuple-element.24), calls=%async_computation | async-start | bytes 196608 | tf_op jit(solution)/shard_map/all_to_all | solution.py:612
  18.2 2.9 %coarse_edges.1 = (f32[3,16,4096]{2,1,0:T(8,128)S(1)}, f32[96,256]{1,0:T(8,128)}, f32[48,256]{1,0:T(8,128)S(1)}) custom-call(f32[3,16,4096]{2,1,0:T(8,128)S(1)} %get-tuple-element.25.cell, f32[3,16,4096]{2,1,0:T(8,128)} %bitcast.17), custom_call_target="tpu_custom_call", output_to_operand_aliasing={{0}: (0, {})} | custom-call | tf_op jit(solution)/shard_map/coarse_edges/pallas_call | solution.py:571
  21.2 7.2 %all-to-all-done.got = f32[64,1,384]{2,1,0:T(1,128)S(1)} async-done(((f32[64,1,384]{2,1,0:T(1,128)}), f32[64,1,384]{2,1,0:T(1,128)S(1)}, u32[]{:S(2)}, u32[]{:S(2)}) %all-to-all-start) | async-done | bytes 98336 | tf_op jit(solution)/shard_map/all_to_all | solution.py:612
  28.4 0.1 slice_reduce_fusion
  28.5 1.4 %collective-permute-start = (f32[1,128]{1,0:T(1,128)S(1)}, f32[1,128]{1,0:T(1,128)S(1)}, u32[]{:S(2)}, u32[]{:S(2)}) collective-permute-start(f32[1,128]{1,0:T(1,128)S(1)} %bitcast.25), channel_id=1, source_target_pairs={{0,1},{1,0},{2,3},{3,2},{4,5},{5,4},{6,7},{7,6},{8,9},{9,8},{10,11... | collective-permute-start | bytes 1544 | tf_op jit(solution)/shard_map/ppermute | solution.py:623
  29.9 2.7 %answers.1 = (f32[64,1,256]{2,1,0:T(1,128)}, f32[96,256]{1,0:T(8,128)}, f32[16,256]{1,0:T(8,128)S(1)}, f32[3,16,4096]{2,1,0:T(8,128)S(1)}) custom-call(f32[64,1,384]{2,1,0:T(1,128)S(1)} %all-to-all-done.got, f32[96,256]{1,0:T(8,128)} %get-tuple-element.30.far_planes, f32[48,256]{1,0:T(8,128)S(1)} %get-tuple-element.31.quads_b, f32[3,16,4096]{2,1,0:T(8,128)} %bitcast.18), custom_call_target="tpu_custom_call" | custom-call | tf_op jit(solution)/shard_map/answers/pallas_call | solution.py:571
  32.5 0.0 collective-permute-done
  32.5 4.7 %all-to-all-start.1 = ((f32[64,1,256]{2,1,0:T(1,128)}), f32[64,1,256]{2,1,0:T(1,128)S(1)}, u32[]{:S(2)}, u32[]{:S(2)}) async-start(f32[64,1,256]{2,1,0:T(1,128)} %get-tuple-element.42), calls=%async_computation.1 | async-start | bytes 131072 | tf_op jit(solution)/shard_map/all_to_all | solution.py:638
  37.2 2.7 %collective-permute-start.1 = (f32[1,128]{1,0:T(1,128)S(1)}, f32[1,128]{1,0:T(1,128)S(1)}, u32[]{:S(2)}, u32[]{:S(2)}) collective-permute-start(f32[1,128]{1,0:T(1,128)S(1)} %bitcast_maximum_fusion), channel_id=1, source_target_pairs={{0,2},{1,3},{2,0},{3,1},{4,6},{5,7},{6,4},{7,5},{8,10},{9,11},{10,... | collective-permute-start | bytes 1544 | tf_op jit(solution)/shard_map/ppermute | solution.py:637
  40.0 1.3 %collective-permute-done.1 = f32[1,128]{1,0:T(1,128)S(1)} collective-permute-done((f32[1,128]{1,0:T(1,128)S(1)}, f32[1,128]{1,0:T(1,128)S(1)}, u32[]{:S(2)}, u32[]{:S(2)}) %collective-permute-start.1) | collective-permute-done | bytes 544 | tf_op jit(solution)/shard_map/ppermute | solution.py:637
  41.3 2.4 %updates.1 = (f32[3,16,4096]{2,1,0:T(8,128)}, f32[12,96,128]{2,1,0:T(8,128)}, f32[32,256]{1,0:T(8,128)S(1)}, f32[32,128]{1,0:T(8,128)S(1)}) custom-call(f32[1,128]{1,0:T(1,128)S(1)} %max.7.top, f32[3,16,4096]{2,1,0:T(8,128)S(1)} %get-tuple-element.34.emf_c, f32[96,256]{1,0:T(8,128)} %get-tuple-element.35.far_patch, f32[16,256]{1,0:T(8,128)S(1)} %get-tuple-element.36.masks, ...), custom_call_target="tpu_custom_call" | custom-call | tf_op jit(solution)/shard_map/updates/pallas_call | solution.py:571
  43.6 3.5 %all-to-all-done.1.got = f32[64,1,256]{2,1,0:T(1,128)S(1)} async-done(((f32[64,1,256]{2,1,0:T(1,128)}), f32[64,1,256]{2,1,0:T(1,128)S(1)}, u32[]{:S(2)}, u32[]{:S(2)}) %all-to-all-start.1) | async-done | bytes 65568 | tf_op jit(solution)/shard_map/all_to_all | solution.py:638
  47.1 1.0 %face_jumps.1 = f32[32,256]{1,0:T(8,128)} custom-call(f32[64,1,256]{2,1,0:T(1,128)S(1)} %all-to-all-done.1.got, f32[1,128]{1,0:T(1,128)S(1)} %max.7.top, f32[32,256]{1,0:T(8,128)S(1)} %get-tuple-element.43.picked, f32[32,128]{1,0:T(8,128)S(1)} %get-tuple-element.44.chosen), custom_call_target="tpu_custom_call" | custom-call | tf_op jit(solution)/shard_map/face_jumps/pallas_call | solution.py:571
  (2 shorter events, 0.0 us)
Async XLA Ops:
  5.2 23.2 %all-to-all-start = ((f32[64,1,384]{2,1,0:T(1,128)}), f32[64,1,384]{2,1,0:T(1,128)S(1)}, u32[]{:S(2)}, u32[]{:S(2)}) async-start(f32[64,1,384]{2,1,0:T(1,128)} %get-tuple-element.24), calls=%async_computation | async-start | bytes 196608 | tf_op jit(solution)/shard_map/all_to_all | solution.py:612
  28.5 4.0 %collective-permute-start = (f32[1,128]{1,0:T(1,128)S(1)}, f32[1,128]{1,0:T(1,128)S(1)}, u32[]{:S(2)}, u32[]{:S(2)}) collective-permute-start(f32[1,128]{1,0:T(1,128)S(1)} %bitcast.25), channel_id=1, source_target_pairs={{0,1},{1,0},{2,3},{3,2},{4,5},{5,4},{6,7},{7,6},{8,9},{9,8},{10,11... | collective-permute-start | bytes 1544 | tf_op jit(solution)/shard_map/ppermute | solution.py:623
  32.5 14.6 %all-to-all-start.1 = ((f32[64,1,256]{2,1,0:T(1,128)}), f32[64,1,256]{2,1,0:T(1,128)S(1)}, u32[]{:S(2)}, u32[]{:S(2)}) async-start(f32[64,1,256]{2,1,0:T(1,128)} %get-tuple-element.42), calls=%async_computation.1 | async-start | bytes 131072 | tf_op jit(solution)/shard_map/all_to_all | solution.py:638
  37.2 4.0 %collective-permute-start.1 = (f32[1,128]{1,0:T(1,128)S(1)}, f32[1,128]{1,0:T(1,128)S(1)}, u32[]{:S(2)}, u32[]{:S(2)}) collective-permute-start(f32[1,128]{1,0:T(1,128)S(1)} %bitcast_maximum_fusion), channel_id=1, source_target_pairs={{0,2},{1,3},{2,0},{3,1},{4,6},{5,7},{6,4},{7,5},{8,10},{9,11},{10,... | collective-permute-start | bytes 1544 | tf_op jit(solution)/shard_map/ppermute | solution.py:637

commit v3 on v2

--- a/solution.py
+++ b/solution.py
@@ -19,7 +19,6 @@
 F32 = jnp.float32
 BF16 = jnp.bfloat16
 TANGENT = ((1, 2), (0, 2), (0, 1))
-UNROLL = 16
 
 
 def grid_of(rows, cols):
@@ -218,19 +217,54 @@
     return face_column_wise(lambda i: slab(ref, along, i, 0, CB))
 
 
-def first_kernel(
-    cb, cv, fb, fv, far_pairs,
-    send, cell_c, emf_f, b_f,
-    b_c, v_c, pitched_b, v_f, pairs, out, sems,
-):
-    fine_copies = fetch_fine(fb, pitched_b, sems.at[0]) + fetch_fine(fv, v_f, sems.at[1])
-    coarse_copies = [
+def coarse_parts(cb, cv, b_c, v_c, sems):
+    return [
         [
-            pltpu.make_async_copy(far.at[:, :, part], near.at[:, :, part], sems.at[2 + q])
+            pltpu.make_async_copy(far.at[:, :, part], near.at[:, :, part], sems.at[q])
             for far, near in ((cb, b_c), (cv, v_c))
         ]
         for q, part in enumerate(pl.ds(q * 4 * WIDE, 4 * WIDE) for q in range(4))
     ]
+
+
+def wait_part(copies, i):
+    for q in range(4):
+        if i == max(4 * q - 1, 0):
+            for copy in copies[q]:
+                copy.wait()
+
+
+def centres(load_b, i):
+    bx, by, bz = (load_b(c, i) for c in range(3))
+    mean = lambda a, b: 0.5 * (a + b)
+    return (
+        each(mean, bx, load_b(0, (i + 1) % EDGE)),
+        each(mean, by, y_next(by)),
+        each(mean, bz, z_next(bz)),
+    )
+
+
+def speeds(centre, velocity):
+    size = lambda a, b, c: jnp.sqrt(a * a + b * b + c * c)
+    fast = each(lambda a, b: a + b, each(size, *velocity), each(size, *centre))
+    return jnp.maximum(fast[0], fast[1])
+
+
+def put_cell(cell, i, centre, velocity):
+    cross = lambda a, b, c, d: a * b - c * d
+    (cx, cy, cz), (vx, vy, vz) = centre, velocity
+    put_slab(cell, 0, i, 0, CB, each(cross, vz, cy, vy, cz))
+    put_slab(cell, 1, i, 0, CB, each(cross, vx, cz, vz, cx))
+    put_slab(cell, 2, i, 0, CB, each(cross, vy, cx, vx, cy))
+
+
+def first_kernel(
+    cb, cv, fb, fv, far_pairs,
+    send, emf_f, b_f,
+    b_c, v_c, pitched_b, v_f, pairs, out, sems,
+):
+    fine_copies = fetch_fine(fb, pitched_b, sems.at[0]) + fetch_fine(fv, v_f, sems.at[1])
+    coarse_copies = coarse_parts(cb, cv, b_c, v_c, sems.at[pl.ds(2, 4)])
     pairs_copy = pltpu.make_async_copy(far_pairs, pairs, sems.at[6])
     for copy in [pairs_copy, *fine_copies, *sum(coarse_copies, [])]:
         copy.start()
@@ -248,25 +282,6 @@
         picks.append(mm(chosen.astype(BF16), source.astype(BF16), nt).astype(BF16))
         meta = jnp.where(lane == k, jnp.sum(chosen * key, axis=1, keepdims=True), meta)
 
-    def cells(load_b, load_v, cell, ready):
-        top = jnp.zeros((CB, 128), F32)
-        for i in range(EDGE):
-            ready(i)
-            bx, by, bz = load_b(0, i), load_b(1, i), load_b(2, i)
-            vx, vy, vz = load_v(0, i), load_v(1, i), load_v(2, i)
-            mean = lambda a, b: 0.5 * (a + b)
-            cx = each(mean, bx, load_b(0, (i + 1) % EDGE))
-            cy = each(mean, by, y_next(by))
-            cz = each(mean, bz, z_next(bz))
-            cross = lambda a, b, c, d: a * b - c * d
-            put_slab(cell, 0, i, 0, CB, each(cross, vz, cy, vy, cz))
-            put_slab(cell, 1, i, 0, CB, each(cross, vx, cz, vz, cx))
-            put_slab(cell, 2, i, 0, CB, each(cross, vy, cx, vx, cy))
-            size = lambda a, b, c: jnp.sqrt(a * a + b * b + c * c)
-            fast = each(lambda a, b: a + b, each(size, vx, vy, vz), each(size, cx, cy, cz))
-            top = jnp.maximum(top, jnp.maximum(fast[0], fast[1]))
-        return top
-
     for copy in fine_copies:
         copy.wait()
     held = {}
@@ -277,7 +292,11 @@
             put_slab(b_f, c, i, 0, CB, held[c, i])
         return held[c, i]
 
-    top_fine = cells(fine_b, lambda c, i: fine_slab(v_f, c, i), emf_f, lambda i: None)
+    top_fine = top_coarse = jnp.zeros((CB, 128), F32)
+    for i in range(EDGE):
+        centre, velocity = centres(fine_b, i), [fine_slab(v_f, c, i) for c in range(3)]
+        put_cell(emf_f, i, centre, velocity)
+        top_fine = jnp.maximum(top_fine, speeds(centre, velocity))
     edges(emf_f, emf_f)
     restrict = [restrict_matrix(False), restrict_matrix(True)]
     rows = []
@@ -293,18 +312,10 @@
     )
     rows_copy.start()
 
-    def coarse_ready(i):
-        for q in range(4):
-            if i == max(4 * q - 1, 0):
-                for copy in coarse_copies[q]:
-                    copy.wait()
-
-    top_coarse = cells(
-        lambda c, i: slab(b_c, c, i, 0, CB),
-        lambda c, i: slab(v_c, c, i, 0, CB),
-        cell_c,
-        coarse_ready,
-    )
+    for i in range(EDGE):
+        wait_part(coarse_copies, i)
+        centre = centres(lambda c, k: slab(b_c, c, k, 0, CB), i)
+        top_coarse = jnp.maximum(top_coarse, speeds(centre, [slab(v_c, c, i, 0, CB) for c in range(3)]))
     top = jnp.max(jnp.maximum(top_fine, top_coarse), axis=0, keepdims=True)
     top = jnp.broadcast_to(jnp.max(top, axis=1, keepdims=True), (PEERS, 128))
     out[:, 0, 256:384] = jnp.where(lane < 2, meta, top)
@@ -316,36 +327,35 @@
     meta_copy.wait()
 
 
-def coarse_kernel(cell, cb, emf, far_planes, quads, b_c, planes, sems):
-    load = pltpu.make_async_copy(cb, b_c, sems.at[0])
-    load.start()
-    edges(cell, emf)
+def coarse_kernel(cb, cv, emf, planes, quads, b_c, v_c, sems):
+    copies = coarse_parts(cb, cv, b_c, v_c, sems)
+    for copy in sum(copies, []):
+        copy.start()
+    load_b, load_v = (lambda c, i, ref=ref: slab(ref, c, i, 0, CB) for ref in (b_c, v_c))
+    for i in range(EDGE):
+        wait_part(copies, i)
+        centre = centres(load_b, i)
+        put_cell(emf, i, centre, [load_v(c, i) for c in range(3)])
+    edges(emf, emf)
     for d in range(3):
         for t in range(2):
             at = (d * 2 + t) * CB
             face = face_of(emf, TANGENT[d][t], d)
             planes[at : at + CB, 0:128] = face[0]
             planes[at : at + CB, 128:256] = face[1]
-    store = pltpu.make_async_copy(planes, far_planes, sems.at[1])
-    store.start()
     quadrant = [quadrant_matrix(False), quadrant_matrix(True)]
-    load.wait()
     for d in range(3):
         normal = jnp.concatenate(face_of(b_c, d, d), axis=1)
         quads[d * CB : (d + 1) * CB, :] = mm_left(normal, quadrant[1 if d == 2 else 0])
-    store.wait()
 
 
 def answer_kernel(
-    got, far_planes, quads_b, cb, back, far_patch, masks, b_c, planes, patch, out, sems
+    got, planes, quads_b, back, far_patch, masks, top, patch, out, sems
 ):
-    load = pltpu.make_async_copy(cb, b_c, sems.at[0])
-    load_planes = pltpu.make_async_copy(far_planes, planes, sems.at[1])
-    load_planes.start()
-    load.start()
     expand = [expand_matrix(False), expand_matrix(True)]
     quadrant = [quadrant_matrix(False), quadrant_matrix(True)]
     meta = got[:, 0, 256:384]
+    top[...] = jnp.max(meta, axis=0, keepdims=True)
     keys = [meta[:, k : k + 1].astype(jnp.int32) - 1 for k in range(2)]
     target = lax.broadcasted_iota(jnp.int32, (PEERS, 256), 1)
     hit = jnp.concatenate([(k == target).astype(F32) for k in keys], axis=0).astype(BF16)
@@ -387,9 +397,8 @@
                 first = (d * 2 + t) * CB
                 patch[first : first + CB, side] = value[d, t][h]
 
-    store = pltpu.make_async_copy(patch, far_patch, sems.at[2])
+    store = pltpu.make_async_copy(patch, far_patch, sems.at[0])
     store.start()
-    load_planes.wait()
 
     def face(d, t):
         first = (d * 2 + t) * CB
@@ -441,9 +450,9 @@
             answers.append(jnp.where((quad & 1) == k, side, pltpu.roll(side, 64, 1)))
         side = slice(part * 128, (part + 1) * 128)
         out[:, 0, side] = jnp.where(out_lane < 64, answers[0], answers[1])
-    send = pltpu.make_async_copy(out, back, sems.at[3])
+    send = pltpu.make_async_copy(out, back, sems.at[1])
     send.start()
-    for copy in (load, store, send):
+    for copy in (store, send):
         copy.wait()
 
 
@@ -566,7 +575,7 @@
 FACES = (6 * CB, WIDE)
 
 
-def call(kernel, name, outs, args, scratch=(), aliases=None):
+def call(kernel, outs, args, scratch=(), aliases=None):
     far = [isinstance(out, tuple) and out[0] == "hbm" for out in outs]
     return pl.pallas_call(
         kernel,
@@ -579,7 +588,6 @@
         scratch_shapes=list(scratch),
         input_output_aliases=aliases or {},
         compiler_params=pltpu.CompilerParams(vmem_limit_bytes=24 * 1024 * 1024),
-        name=name,
     )(
         *(
             pltpu.with_memory_space_constraint(a, pltpu.HBM if is_far else pltpu.VMEM)
@@ -602,50 +610,37 @@
     pitched = pltpu.VMEM(PITCHED, F32)
     small = pltpu.VMEM((6, 1, PAIRS), jnp.int32)
     sems = pltpu.SemaphoreType.DMA
-    send, cell_c, emf_f, b_f = call(
+    send, emf_f, b_f = call(
         first_kernel,
-        "speeds_and_rows",
-        [("hbm", (PEERS, 1, 384)), FIELD, FIELD, FIELD],
+        [("hbm", (PEERS, 1, 384)), FIELD, FIELD],
         far(cb, cv, fb, fv, rows),
         [field, field, pitched, pitched, small, pltpu.VMEM((PEERS, 1, 384), F32), sems((9,))],
     )
     got = lax.all_to_all(send, BLOCKS, 0, 0, tiled=True)
-    emf_c, planes, quads = call(
-        coarse_kernel,
-        "coarse_edges",
-        [FIELD, ("hbm", FACES), (3 * CB, WIDE)],
-        near(cell_c) + far(cb),
-        [field, pltpu.VMEM(FACES, F32), sems((2,))],
-        {0: 0},
-    )
-    got, emf_c, planes, quads = lax.optimization_barrier((got, emf_c, planes, quads))
-    top = jnp.max(got[:, :, 256:384], axis=0)
-    top = jnp.maximum(top, lax.ppermute(top, "gz", [(i, i ^ 1) for i in range(count)]))
-    back, patch, masks, b_c = call(
+    emf_c, planes, quads, b_c = call(
+        coarse_kernel, [FIELD, FACES, (3 * CB, WIDE), FIELD], far(cb, cv), [field, sems((4,))]
+    )
+    got, emf_c, planes, quads, b_c = lax.optimization_barrier((got, emf_c, planes, quads, b_c))
+    back, patch, masks, top = call(
         answer_kernel,
-        "answers",
-        [("hbm", (PEERS, 1, 256)), ("hbm", FACES), (CB, WIDE), FIELD],
-        near(got) + far(planes) + near(quads) + far(cb),
-        [
-            pltpu.VMEM(FACES, F32),
-            pltpu.VMEM(FACES, F32),
-            pltpu.VMEM((PEERS, 1, 256), F32),
-            sems((4,)),
-        ],
-    )
-    back, top = lax.optimization_barrier((back, top))
-    top = jnp.maximum(top, lax.ppermute(top, "gz", [(i, i ^ 2) for i in range(count)]))
+        [("hbm", (PEERS, 1, 256)), ("hbm", FACES), (CB, WIDE), (1, 128)],
+        near(got, planes, quads),
+        [pltpu.VMEM(FACES, F32), pltpu.VMEM((PEERS, 1, 256), F32), sems((2,))],
+    )
+    others = []
+    for k in range(1, count):
+        others.append(lax.ppermute(top, "gz", [(i, (i + k) % count) for i in range(count)]))
+    for other in others:
+        top = jnp.maximum(top, other)
     returned = lax.all_to_all(back, BLOCKS, 0, 0, tiled=True)
     new_c, new_f, picked, chosen = call(
         update_kernel,
-        "updates",
         [("hbm", FIELD), ("hbm", (FB, 96, 128)), (PAIRS, WIDE), (PAIRS, 128)],
         near(top, emf_c) + far(patch) + near(masks, emf_f, b_c, b_f) + far(rows),
         [field, field, pitched, small, pltpu.VMEM(FACES, F32), sems((4,))],
     )
     (jump,) = call(
         third_kernel,
-        "face_jumps",
         [("hbm", (PAIRS, WIDE))],
         near(returned, top, picked, chosen),
         [pltpu.VMEM((PAIRS, WIDE), F32), sems((1,))],
@@ -669,6 +664,5 @@
         P("gz", BLOCKS, None),
     )
     out_specs = (P("gz", BLOCKS, None, None), P("gz", BLOCKS, None, None), P("gz", BLOCKS, None))
-    return jax.shard_map(
-        on_device, mesh=split, in_specs=in_specs, out_specs=out_specs, check_vma=False
-    )
+
+    return jax.shard_map(on_device, mesh=split, in_specs=in_specs, out_specs=out_specs, check_vma=False)

time: 48.5 us -> 51 us (1.052)
  waiting for transfers between devices: 12 us -> 14.3 us
    all_to_all x1, waiting for transfers between devices: 3.5 us -> 7.46 us  [on_device(): returned = lax.all_to_all(back, BLOCKS, 0, 0, tiled=True)]
    ppermute x2 -> x3, waiting for transfers between devices: 1.3 us -> 0.01 us  [on_device(): lax.ppermute(top, 'gz', [(i, (i + k) % count) for i in range(count)])]
    all_to_all x1, starting transfers between devices: 4.68 us -> 5.27 us  [on_device(): returned = lax.all_to_all(back, BLOCKS, 0, 0, tiled=True)]
    ppermute x2 -> x3, starting transfers between devices: 4.08 us -> 3.85 us  [on_device(): lax.ppermute(top, 'gz', [(i, (i + k) % count) for i in range(count)])]
  transfers between devices with their start and end apart: 4 -> 5, of which waited for: 3 -> 2; matrix products, arithmetic and copies ran while one was open for 0% -> 0% of each run, Pallas kernels for 16% -> 11%
where the time goes in v3:
time: 51 us; the launch traced here: 50.7 us
  starting transfers between devices  22.1 us (43%)
  waiting for transfers between devices  14.3 us (28%)
  Pallas kernels  13.5 us (26%)
  between operations  0.71 us (1%)
    pallas_call x5, Pallas kernels, call(): pl.pallas_call(kernel, out_shape=[pltpu.HBM(out[1], F32) if is_far else p...  13.5 us
    all_to_all x1, starting transfers between devices, on_device(): got = lax.all_to_all(send, BLOCKS, 0, 0, tiled=True)  13 us
    all_to_all x1, waiting for transfers between devices, on_device(): returned = lax.all_to_all(back, BLOCKS, 0, 0, tiled=True)  7.46 us
    all_to_all x1, waiting for transfers between devices, on_device(): got = lax.all_to_all(send, BLOCKS, 0, 0, tiled=True)  6.86 us
    all_to_all x1, starting transfers between devices, on_device(): returned = lax.all_to_all(back, BLOCKS, 0, 0, tiled=True)  5.27 us
    ppermute x3, starting transfers between devices, on_device(): lax.ppermute(top, 'gz', [(i, (i + k) % count) for i in range(count)])  3.85 us
  transfers between devices with their start and end apart: 5, of which 2 were waited for; matrix products, arithmetic and copies ran while one was open for 0% of the time, Pallas kernels for 11%

profile of v3, /device:TPU:1, one launch (start us, length us, event | category | flops | bytes accessed | tf_op | source)
XLA Modules:
  0.0 50.7 jit_solution(11641940453502697939)
XLA Ops:
  0.6 4.6 %shard_map.76 = (f32[64,1,384]{2,1,0:T(1,128)}, f32[3,16,4096]{2,1,0:T(8,128)S(1)}, f32[3,16,4096]{2,1,0:T(8,128)S(1)}) custom-call(f32[3,16,4096]{2,1,0:T(8,128)} %bitcast.14, f32[3,16,4096]{2,1,0:T(8,128)} %bitcast.16, f32[12,96,128]{2,1,0:T(8,128)} %bitcast.18, f32[12,96,128]{2,1,0:T(8,128)} %bitcast.19, s32[6,1,32]{2,1,0:T(1,128)} %bitcast.21), custom_call_target="tpu_custom_call" | custom-call | tf_op jit(solution)/shard_map/pallas_call | solution.py:580
  5.2 13.0 %all-to-all-start = ((f32[64,1,384]{2,1,0:T(1,128)}), f32[64,1,384]{2,1,0:T(1,128)S(1)}, u32[]{:S(2)}, u32[]{:S(2)}) async-start(f32[64,1,384]{2,1,0:T(1,128)} %get-tuple-element.23), calls=%async_computation | async-start | bytes 196608 | tf_op jit(solution)/shard_map/all_to_all | solution.py:619
  18.2 3.3 %shard_map.77 = (f32[3,16,4096]{2,1,0:T(8,128)S(1)}, f32[96,256]{1,0:T(8,128)S(1)}, f32[48,256]{1,0:T(8,128)S(1)}, f32[3,16,4096]{2,1,0:T(8,128)S(1)}) custom-call(f32[3,16,4096]{2,1,0:T(8,128)} %bitcast.15, f32[3,16,4096]{2,1,0:T(8,128)} %bitcast.17), custom_call_target="tpu_custom_call" | custom-call | tf_op jit(solution)/shard_map/pallas_call | solution.py:580
  21.5 6.9 %all-to-all-done.got = f32[64,1,384]{2,1,0:T(1,128)S(1)} async-done(((f32[64,1,384]{2,1,0:T(1,128)}), f32[64,1,384]{2,1,0:T(1,128)S(1)}, u32[]{:S(2)}, u32[]{:S(2)}) %all-to-all-start) | async-done | bytes 98336 | tf_op jit(solution)/shard_map/all_to_all | solution.py:619
  28.4 2.2 %shard_map.78 = (f32[64,1,256]{2,1,0:T(1,128)}, f32[96,256]{1,0:T(8,128)}, f32[16,256]{1,0:T(8,128)S(1)}, f32[1,128]{1,0:T(1,128)S(1)}) custom-call(f32[64,1,384]{2,1,0:T(1,128)S(1)} %all-to-all-done.got, f32[96,256]{1,0:T(8,128)S(1)} %get-tuple-element.29.planes, f32[48,256]{1,0:T(8,128)S(1)} %get-tuple-element.30.quads_b), custom_call_target="tpu_custom_call" | custom-call | tf_op jit(solution)/shard_map/pallas_call | solution.py:580
  30.6 2.8 %collective-permute-start.2 = (f32[1,128]{1,0:T(1,128)S(1)}, f32[1,128]{1,0:T(1,128)S(1)}, u32[]{:S(2)}, u32[]{:S(2)}) collective-permute-start(f32[1,128]{1,0:T(1,128)S(1)} %get-tuple-element.31), channel_id=1, source_target_pairs={{0,3},{1,0},{2,1},{3,2},{4,7},{5,4},{6,5},{7,6},{8,11},{9,8},{10,9... | collective-permute-start | bytes 1544 | tf_op jit(solution)/shard_map/ppermute | solution.py:632
  33.4 0.3 collective-permute-start.1
  33.8 0.7 %collective-permute-start = (f32[1,128]{1,0:T(1,128)S(1)}, f32[1,128]{1,0:T(1,128)S(1)}, u32[]{:S(2)}, u32[]{:S(2)}) collective-permute-start(f32[1,128]{1,0:T(1,128)S(1)} %get-tuple-element.31), channel_id=1, source_target_pairs={{0,1},{1,2},{2,3},{3,0},{4,5},{5,6},{6,7},{7,4},{8,9},{9,10},{10,1... | collective-permute-start | bytes 1544 | tf_op jit(solution)/shard_map/ppermute | solution.py:632
  34.5 5.3 %all-to-all-start.1 = ((f32[64,1,256]{2,1,0:T(1,128)}), f32[64,1,256]{2,1,0:T(1,128)S(1)}, u32[]{:S(2)}, u32[]{:S(2)}) async-start(f32[64,1,256]{2,1,0:T(1,128)} %get-tuple-element.40), calls=%async_computation.1 | async-start | bytes 131072 | tf_op jit(solution)/shard_map/all_to_all | solution.py:635
  39.7 0.0 collective-permute-done.2
  39.8 0.0 collective-permute-done.1
  39.8 0.0 collective-permute-done
  39.8 2.4 %shard_map.79 = (f32[3,16,4096]{2,1,0:T(8,128)}, f32[12,96,128]{2,1,0:T(8,128)}, f32[32,256]{1,0:T(8,128)S(1)}, f32[32,128]{1,0:T(8,128)S(1)}) custom-call(f32[1,128]{1,0:T(1,128)S(1)} %maximum_maximum_fusion.top, f32[3,16,4096]{2,1,0:T(8,128)S(1)} %get-tuple-element.32.emf_c, f32[96,256]{1,0:T(8,128)} %get-tuple-element.33.far_patch, ...), custom_call_target="tpu_custom_call" | custom-call | tf_op jit(solution)/shard_map/pallas_call | solution.py:580
  42.2 7.5 %all-to-all-done.1.got = f32[64,1,256]{2,1,0:T(1,128)S(1)} async-done(((f32[64,1,256]{2,1,0:T(1,128)}), f32[64,1,256]{2,1,0:T(1,128)S(1)}, u32[]{:S(2)}, u32[]{:S(2)}) %all-to-all-start.1) | async-done | bytes 65568 | tf_op jit(solution)/shard_map/all_to_all | solution.py:635
  49.6 1.0 %shard_map.80 = f32[32,256]{1,0:T(8,128)} custom-call(f32[64,1,256]{2,1,0:T(1,128)S(1)} %all-to-all-done.1.got, f32[1,128]{1,0:T(1,128)S(1)} %maximum_maximum_fusion.top, f32[32,256]{1,0:T(8,128)S(1)} %get-tuple-element.41.picked, f32[32,128]{1,0:T(8,128)S(1)} %get-tuple-element.42.chosen), custom_call_target="tpu_custom_call" | custom-call | tf_op jit(solution)/shard_map/pallas_call | solution.py:580
  (1 shorter events, 0.0 us)
Async XLA Ops:
  5.2 23.2 %all-to-all-start = ((f32[64,1,384]{2,1,0:T(1,128)}), f32[64,1,384]{2,1,0:T(1,128)S(1)}, u32[]{:S(2)}, u32[]{:S(2)}) async-start(f32[64,1,384]{2,1,0:T(1,128)} %get-tuple-element.23), calls=%async_computation | async-start | bytes 196608 | tf_op jit(solution)/shard_map/all_to_all | solution.py:619
  30.6 9.1 %collective-permute-start.2 = (f32[1,128]{1,0:T(1,128)S(1)}, f32[1,128]{1,0:T(1,128)S(1)}, u32[]{:S(2)}, u32[]{:S(2)}) collective-permute-start(f32[1,128]{1,0:T(1,128)S(1)} %get-tuple-element.31), channel_id=1, source_target_pairs={{0,3},{1,0},{2,1},{3,2},{4,7},{5,4},{6,5},{7,6},{8,11},{9,8},{10,9... | collective-permute-start | bytes 1544 | tf_op jit(solution)/shard_map/ppermute | solution.py:632
  33.4 6.3 %collective-permute-start.1 = (f32[1,128]{1,0:T(1,128)S(1)}, f32[1,128]{1,0:T(1,128)S(1)}, u32[]{:S(2)}, u32[]{:S(2)}) collective-permute-start(f32[1,128]{1,0:T(1,128)S(1)} %get-tuple-element.31), channel_id=1, source_target_pairs={{0,2},{1,3},{2,0},{3,1},{4,6},{5,7},{6,4},{7,5},{8,10},{9,11},{10,... | collective-permute-start | bytes 1544 | tf_op jit(solution)/shard_map/ppermute | solution.py:632
  33.8 6.0 %collective-permute-start = (f32[1,128]{1,0:T(1,128)S(1)}, f32[1,128]{1,0:T(1,128)S(1)}, u32[]{:S(2)}, u32[]{:S(2)}) collective-permute-start(f32[1,128]{1,0:T(1,128)S(1)} %get-tuple-element.31), channel_id=1, source_target_pairs={{0,1},{1,2},{2,3},{3,0},{4,5},{5,6},{6,7},{7,4},{8,9},{9,10},{10,1... | collective-permute-start | bytes 1544 | tf_op jit(solution)/shard_map/ppermute | solution.py:632
  34.5 15.2 %all-to-all-start.1 = ((f32[64,1,256]{2,1,0:T(1,128)}), f32[64,1,256]{2,1,0:T(1,128)S(1)}, u32[]{:S(2)}, u32[]{:S(2)}) async-start(f32[64,1,256]{2,1,0:T(1,128)} %get-tuple-element.40), calls=%async_computation.1 | async-start | bytes 131072 | tf_op jit(solution)/shard_map/all_to_all | solution.py:635

commit v4 on v3

--- a/solution.py
+++ b/solution.py
@@ -456,51 +456,35 @@
         copy.wait()
 
 
-def update_kernel(
-    top, emf_c, far_patch, masks, emf_f, b_c, b_f, far_pairs,
-    new_c, new_f, picked, chosen,
-    emf, out_c, out_f, pairs, patch, sems,
-):
-    load = pltpu.make_async_copy(far_pairs, pairs, sems.at[2])
-    load_patch = pltpu.make_async_copy(far_patch, patch, sems.at[3])
+def curls(load, curl):
+    first = [load(c, 0) for c in range(3)]
+    now = first
+    turn = lambda p, q, r, s: (p - q) - (r - s)
+    for i in range(EDGE):
+        far = [load(c, i + 1) for c in range(3)] if i + 1 < EDGE else first
+        ex, ey, ez = now
+        put_slab(curl, 0, i, 0, CB, each(turn, y_next(ez), ez, z_next(ey), ey))
+        put_slab(curl, 1, i, 0, CB, each(turn, z_next(ex), ex, far[2], ez))
+        put_slab(curl, 2, i, 0, CB, each(turn, far[1], ey, y_next(ex), ex))
+        now = far
+
+
+def curl_kernel(emf_c, far_patch, masks, emf_f, curl_c, curl_f, patch, sems):
+    load_patch = pltpu.make_async_copy(far_patch, patch, sems.at[0])
     load_patch.start()
-    load.start()
-    time_step = 0.2 / top[0:1, 2:3]
+    curls(lambda c, i: slab(emf_f, c, i, 0, CB), curl_f)
     lane = lax.broadcasted_iota(jnp.int32, (CB, 128), 1)
 
     def pair(ref, first):
         return ref[first : first + CB, 0:128], ref[first : first + CB, 128:256]
-
-    def update(emf, factor, load_b, store, done):
-        for i in range(EDGE):
-            following = (i + 1) % EDGE
-            ex, ey, ez = (slab(emf, c, i, 0, CB) for c in range(3))
-            ey_far, ez_far = (slab(emf, c, following, 0, CB) for c in (1, 2))
-            curl = lambda b, p, q, r, s: b - factor * ((p - q) - (r - s))
-            store(0, i, each(curl, load_b(0, i), y_next(ez), ez, z_next(ey), ey))
-            store(1, i, each(curl, load_b(1, i), z_next(ex), ex, ez_far, ez))
-            store(2, i, each(curl, load_b(2, i), ey_far, ey, y_next(ex), ex))
-            done(i)
-
-    update(
-        emf_f,
-        time_step / 0.5,
-        lambda c, i: slab(b_f, c, i, 0, CB),
-        lambda c, i, value: put_fine_slab(out_f, c, i, value),
-        lambda i: None,
-    )
-    results = [
-        pltpu.make_async_copy(out_f.at[pl.ds(b * PITCH, 96)], new_f.at[b], sems.at[0])
-        for b in range(FB)
-    ]
-    for copy in results:
-        copy.start()
 
     load_patch.wait()
     planes = {(d, t): pair(patch, (d * 2 + t) * CB) for d in range(3) for t in range(2)}
     bits = [m.astype(jnp.int32) for m in pair(masks, 0)]
     hits = [[((m >> d) & 1).astype(F32) for m in bits] for d in range(3)]
-    for i in range(EDGE):
+    ready = {}
+
+    def corrected(i):
         now = {c: slab(emf_c, c, i, 0, CB) for c in range(3)}
         if i == 0:
             for t, c in enumerate(TANGENT[0]):
@@ -514,23 +498,43 @@
         for t, c in enumerate(TANGENT[2]):
             value = [pltpu.roll(p, turn, 1) for p in planes[2, t]]
             now[c] = each(jnp.where, there, value, now[c])
+        return now
+
+    def load(c, i):
+        if i not in ready:
+            ready[i] = corrected(i)
+        return ready[i][c]
+
+    curls(load, curl_c)
+
+
+def update_kernel(
+    top, curl_c, curl_f, b_c, b_f, far_pairs,
+    new_c, new_f, picked, chosen,
+    out_c, out_f, pairs, sems,
+):
+    load = pltpu.make_async_copy(far_pairs, pairs, sems.at[2])
+    load.start()
+    time_step = 0.2 / top[0:1, 2:3]
+    results = []
+    step = lambda factor: lambda b, c: b - factor * c
+    for i in range(EDGE):
         for c in range(3):
-            put_slab(emf, c, i, 0, CB, now[c])
-
-    def send_chunk(i):
+            value = each(step(time_step), slab(b_c, c, i, 0, CB), slab(curl_c, c, i, 0, CB))
+            put_slab(out_c, c, i, 0, CB, value)
         if i % 4 == 3:
             part = pl.ds((i - 3) * WIDE, 4 * WIDE)
             copy = pltpu.make_async_copy(out_c.at[:, :, part], new_c.at[:, :, part], sems.at[1])
             copy.start()
             results.append(copy)
-
-    update(
-        emf,
-        time_step,
-        lambda c, i: slab(b_c, c, i, 0, CB),
-        lambda c, i, value: put_slab(out_c, c, i, 0, CB, value),
-        send_chunk,
-    )
+    for i in range(EDGE):
+        for c in range(3):
+            value = each(step(time_step / 0.5), slab(b_f, c, i, 0, CB), slab(curl_f, c, i, 0, CB))
+            put_fine_slab(out_f, c, i, value)
+    for b in range(FB):
+        copy = pltpu.make_async_copy(out_f.at[pl.ds(b * PITCH, 96)], new_f.at[b], sems.at[0])
+        copy.start()
+        results.append(copy)
     faces = (
         fine_slab(out_f, 0, 0),
         face_row_wise(lambda i: fine_slab(out_f, 1, i)[0]),
@@ -633,11 +637,18 @@
     for other in others:
         top = jnp.maximum(top, other)
     returned = lax.all_to_all(back, BLOCKS, 0, 0, tiled=True)
+    curl_c, curl_f = call(
+        curl_kernel,
+        [FIELD, FIELD],
+        near(emf_c) + far(patch) + near(masks, emf_f),
+        [pltpu.VMEM(FACES, F32), sems((1,))],
+        {0: 0, 3: 1},
+    )
     new_c, new_f, picked, chosen = call(
         update_kernel,
         [("hbm", FIELD), ("hbm", (FB, 96, 128)), (PAIRS, WIDE), (PAIRS, 128)],
-        near(top, emf_c) + far(patch) + near(masks, emf_f, b_c, b_f) + far(rows),
-        [field, field, pitched, small, pltpu.VMEM(FACES, F32), sems((4,))],
+        near(top, curl_c, curl_f, b_c, b_f) + far(rows),
+        [field, pitched, small, sems((3,))],
     )
     (jump,) = call(
         third_kernel,

time: 51 us -> 51 us (level)
  waiting for transfers between devices: 14.3 us -> 13.6 us
  Pallas kernels: 13.5 us -> 14.2 us
    all_to_all x1, waiting for transfers between devices: 7.46 us -> 6.77 us  [on_device(): returned = lax.all_to_all(back, BLOCKS, 0, 0, tiled=True)]
    pallas_call x5 -> x6, Pallas kernels: 13.5 us -> 14.2 us  [call(): pl.pallas_call(kernel, out_shape=[pltpu.HBM(out[1], F32) if is_far else p...]
  transfers between devices with their start and end apart: 5 -> 5, of which waited for: 2 -> 2; matrix products, arithmetic and copies ran while one was open for 0% -> 0% of each run, Pallas kernels for 11% -> 13%
where the time goes in v4:
time: 51 us; the launch traced here: 50.7 us
  starting transfers between devices  22.1 us (43%)
  Pallas kernels  14.2 us (28%)
  waiting for transfers between devices  13.6 us (27%)
  between operations  0.72 us (1%)
    pallas_call x6, Pallas kernels, call(): pl.pallas_call(kernel, out_shape=[pltpu.HBM(out[1], F32) if is_far else p...  14.2 us
    all_to_all x1, starting transfers between devices, on_device(): got = lax.all_to_all(send, BLOCKS, 0, 0, tiled=True)  13 us
    all_to_all x1, waiting for transfers between devices, on_device(): got = lax.all_to_all(send, BLOCKS, 0, 0, tiled=True)  6.86 us
    all_to_all x1, waiting for transfers between devices, on_device(): returned = lax.all_to_all(back, BLOCKS, 0, 0, tiled=True)  6.77 us
    all_to_all x1, starting transfers between devices, on_device(): returned = lax.all_to_all(back, BLOCKS, 0, 0, tiled=True)  5.27 us
    ppermute x3, starting transfers between devices, on_device(): lax.ppermute(top, 'gz', [(i, (i + k) % count) for i in range(count)])  3.85 us
  transfers between devices with their start and end apart: 5, of which 2 were waited for; matrix products, arithmetic and copies ran while one was open for 0% of the time, Pallas kernels for 13%

profile of v4, /device:TPU:1, one launch (start us, length us, event | category | flops | bytes accessed | tf_op | source)
XLA Modules:
  0.0 50.7 jit_solution(16995407562373987790)
XLA Ops:
  0.6 4.6 %shard_map.76 = (f32[64,1,384]{2,1,0:T(1,128)}, f32[3,16,4096]{2,1,0:T(8,128)S(1)}, f32[3,16,4096]{2,1,0:T(8,128)S(1)}) custom-call(f32[3,16,4096]{2,1,0:T(8,128)} %bitcast.14, f32[3,16,4096]{2,1,0:T(8,128)} %bitcast.16, f32[12,96,128]{2,1,0:T(8,128)} %bitcast.18, f32[12,96,128]{2,1,0:T(8,128)} %bitcast.19, s32[6,1,32]{2,1,0:T(1,128)} %bitcast.21), custom_call_target="tpu_custom_call" | custom-call | tf_op jit(solution)/shard_map/pallas_call | solution.py:584
  5.2 13.0 %all-to-all-start = ((f32[64,1,384]{2,1,0:T(1,128)}), f32[64,1,384]{2,1,0:T(1,128)S(1)}, u32[]{:S(2)}, u32[]{:S(2)}) async-start(f32[64,1,384]{2,1,0:T(1,128)} %get-tuple-element.25), calls=%async_computation | async-start | bytes 196608 | tf_op jit(solution)/shard_map/all_to_all | solution.py:623
  18.2 3.3 %shard_map.77 = (f32[3,16,4096]{2,1,0:T(8,128)S(1)}, f32[96,256]{1,0:T(8,128)S(1)}, f32[48,256]{1,0:T(8,128)S(1)}, f32[3,16,4096]{2,1,0:T(8,128)S(1)}) custom-call(f32[3,16,4096]{2,1,0:T(8,128)} %bitcast.15, f32[3,16,4096]{2,1,0:T(8,128)} %bitcast.17), custom_call_target="tpu_custom_call" | custom-call | tf_op jit(solution)/shard_map/pallas_call | solution.py:584
  21.5 6.9 %all-to-all-done.got = f32[64,1,384]{2,1,0:T(1,128)S(1)} async-done(((f32[64,1,384]{2,1,0:T(1,128)}), f32[64,1,384]{2,1,0:T(1,128)S(1)}, u32[]{:S(2)}, u32[]{:S(2)}) %all-to-all-start) | async-done | bytes 98336 | tf_op jit(solution)/shard_map/all_to_all | solution.py:623
  28.4 2.2 %shard_map.78 = (f32[64,1,256]{2,1,0:T(1,128)}, f32[96,256]{1,0:T(8,128)}, f32[16,256]{1,0:T(8,128)S(1)}, f32[1,128]{1,0:T(1,128)S(1)}) custom-call(f32[64,1,384]{2,1,0:T(1,128)S(1)} %all-to-all-done.got, f32[96,256]{1,0:T(8,128)S(1)} %get-tuple-element.31.planes, f32[48,256]{1,0:T(8,128)S(1)} %get-tuple-element.32.quads_b), custom_call_target="tpu_custom_call" | custom-call | tf_op jit(solution)/shard_map/pallas_call | solution.py:584
  30.6 2.8 %collective-permute-start.2 = (f32[1,128]{1,0:T(1,128)S(1)}, f32[1,128]{1,0:T(1,128)S(1)}, u32[]{:S(2)}, u32[]{:S(2)}) collective-permute-start(f32[1,128]{1,0:T(1,128)S(1)} %get-tuple-element.33), channel_id=1, source_target_pairs={{0,3},{1,0},{2,1},{3,2},{4,7},{5,4},{6,5},{7,6},{8,11},{9,8},{10,9... | collective-permute-start | bytes 1544 | tf_op jit(solution)/shard_map/ppermute | solution.py:636
  33.4 0.3 collective-permute-start.1
  33.8 0.7 %collective-permute-start = (f32[1,128]{1,0:T(1,128)S(1)}, f32[1,128]{1,0:T(1,128)S(1)}, u32[]{:S(2)}, u32[]{:S(2)}) collective-permute-start(f32[1,128]{1,0:T(1,128)S(1)} %get-tuple-element.33), channel_id=1, source_target_pairs={{0,1},{1,2},{2,3},{3,0},{4,5},{5,6},{6,7},{7,4},{8,9},{9,10},{10,1... | collective-permute-start | bytes 1544 | tf_op jit(solution)/shard_map/ppermute | solution.py:636
  34.5 5.3 %all-to-all-start.1 = ((f32[64,1,256]{2,1,0:T(1,128)}), f32[64,1,256]{2,1,0:T(1,128)S(1)}, u32[]{:S(2)}, u32[]{:S(2)}) async-start(f32[64,1,256]{2,1,0:T(1,128)} %get-tuple-element.44), calls=%async_computation.1 | async-start | bytes 131072 | tf_op jit(solution)/shard_map/all_to_all | solution.py:639
  39.7 1.8 %shard_map.79 = (f32[3,16,4096]{2,1,0:T(8,128)S(1)}, f32[3,16,4096]{2,1,0:T(8,128)S(1)}) custom-call(f32[3,16,4096]{2,1,0:T(8,128)S(1)} %get-tuple-element.34.emf_c, f32[96,256]{1,0:T(8,128)} %get-tuple-element.35.far_patch, f32[16,256]{1,0:T(8,128)S(1)} %get-tuple-element.36.masks, ...), custom_call_target="tpu_custom_call", output_to_operand_aliasing={{0}: (0, {}), {1}: (3, {})} | custom-call | tf_op jit(solution)/shard_map/pallas_call | solution.py:584
  41.5 0.0 collective-permute-done.2
  41.6 0.0 collective-permute-done.1
  41.6 0.0 collective-permute-done
  41.6 1.3 %shard_map.80 = (f32[3,16,4096]{2,1,0:T(8,128)}, f32[12,96,128]{2,1,0:T(8,128)}, f32[32,256]{1,0:T(8,128)S(1)}, f32[32,128]{1,0:T(8,128)S(1)}) custom-call(f32[1,128]{1,0:T(1,128)S(1)} %maximum_maximum_fusion.top, f32[3,16,4096]{2,1,0:T(8,128)S(1)} %get-tuple-element.38.curl_c, f32[3,16,4096]{2,1,0:T(8,128)S(1)} %get-tuple-element.39.curl_f, ...), custom_call_target="tpu_custom_call" | custom-call | tf_op jit(solution)/shard_map/pallas_call | solution.py:584
  42.9 6.8 %all-to-all-done.1.got = f32[64,1,256]{2,1,0:T(1,128)S(1)} async-done(((f32[64,1,256]{2,1,0:T(1,128)}), f32[64,1,256]{2,1,0:T(1,128)S(1)}, u32[]{:S(2)}, u32[]{:S(2)}) %all-to-all-start.1) | async-done | bytes 65568 | tf_op jit(solution)/shard_map/all_to_all | solution.py:639
  49.6 1.0 %shard_map.81 = f32[32,256]{1,0:T(8,128)} custom-call(f32[64,1,256]{2,1,0:T(1,128)S(1)} %all-to-all-done.1.got, f32[1,128]{1,0:T(1,128)S(1)} %maximum_maximum_fusion.top, f32[32,256]{1,0:T(8,128)S(1)} %get-tuple-element.45.picked, f32[32,128]{1,0:T(8,128)S(1)} %get-tuple-element.46.chosen), custom_call_target="tpu_custom_call" | custom-call | tf_op jit(solution)/shard_map/pallas_call | solution.py:584
  (1 shorter events, 0.0 us)
Async XLA Ops:
  5.2 23.2 %all-to-all-start = ((f32[64,1,384]{2,1,0:T(1,128)}), f32[64,1,384]{2,1,0:T(1,128)S(1)}, u32[]{:S(2)}, u32[]{:S(2)}) async-start(f32[64,1,384]{2,1,0:T(1,128)} %get-tuple-element.25), calls=%async_computation | async-start | bytes 196608 | tf_op jit(solution)/shard_map/all_to_all | solution.py:623
  30.6 10.9 %collective-permute-start.2 = (f32[1,128]{1,0:T(1,128)S(1)}, f32[1,128]{1,0:T(1,128)S(1)}, u32[]{:S(2)}, u32[]{:S(2)}) collective-permute-start(f32[1,128]{1,0:T(1,128)S(1)} %get-tuple-element.33), channel_id=1, source_target_pairs={{0,3},{1,0},{2,1},{3,2},{4,7},{5,4},{6,5},{7,6},{8,11},{9,8},{10,9... | collective-permute-start | bytes 1544 | tf_op jit(solution)/shard_map/ppermute | solution.py:636
  33.4 8.1 %collective-permute-start.1 = (f32[1,128]{1,0:T(1,128)S(1)}, f32[1,128]{1,0:T(1,128)S(1)}, u32[]{:S(2)}, u32[]{:S(2)}) collective-permute-start(f32[1,128]{1,0:T(1,128)S(1)} %get-tuple-element.33), channel_id=1, source_target_pairs={{0,2},{1,3},{2,0},{3,1},{4,6},{5,7},{6,4},{7,5},{8,10},{9,11},{10,... | collective-permute-start | bytes 1544 | tf_op jit(solution)/shard_map/ppermute | solution.py:636
  33.8 7.8 %collective-permute-start = (f32[1,128]{1,0:T(1,128)S(1)}, f32[1,128]{1,0:T(1,128)S(1)}, u32[]{:S(2)}, u32[]{:S(2)}) collective-permute-start(f32[1,128]{1,0:T(1,128)S(1)} %get-tuple-element.33), channel_id=1, source_target_pairs={{0,1},{1,2},{2,3},{3,0},{4,5},{5,6},{6,7},{7,4},{8,9},{9,10},{10,1... | collective-permute-start | bytes 1544 | tf_op jit(solution)/shard_map/ppermute | solution.py:636
  34.5 15.2 %all-to-all-start.1 = ((f32[64,1,256]{2,1,0:T(1,128)}), f32[64,1,256]{2,1,0:T(1,128)S(1)}, u32[]{:S(2)}, u32[]{:S(2)}) async-start(f32[64,1,256]{2,1,0:T(1,128)} %get-tuple-element.44), calls=%async_computation.1 | async-start | bytes 131072 | tf_op jit(solution)/shard_map/all_to_all | solution.py:639

commit v5 on v4

--- a/solution.py
+++ b/solution.py
@@ -19,6 +19,7 @@
 F32 = jnp.float32
 BF16 = jnp.bfloat16
 TANGENT = ((1, 2), (0, 2), (0, 1))
+CHUNK = 16
 
 
 def grid_of(rows, cols):
@@ -91,21 +92,10 @@
     return lax.broadcasted_iota(jnp.int32, value.shape, 1)
 
 
-def y_prev(p):
-    a, b = pltpu.roll(p[0], 16, 1), pltpu.roll(p[1], 16, 1)
-    edge = lanes_of(a) < 16
-    return jnp.where(edge, b, a), jnp.where(edge, a, b)
-
-
 def y_next(p):
     a, b = pltpu.roll(p[0], 112, 1), pltpu.roll(p[1], 112, 1)
     edge = lanes_of(a) >= 112
     return jnp.where(edge, b, a), jnp.where(edge, a, b)
-
-
-def z_prev(p):
-    edge = (lanes_of(p[0]) & 15) == 0
-    return tuple(jnp.where(edge, pltpu.roll(x, 113, 1), pltpu.roll(x, 1, 1)) for x in p)
 
 
 def z_next(p):
@@ -193,20 +183,55 @@
     return first, second, source
 
 
-def edges(cell, emf):
-    last = [slab(cell, c, EDGE - 1, 0, CB) for c in range(3)]
-    now = last
-    add = lambda a, b: a + b
-    quarter = lambda a, b: 0.25 * (a + b)
-    for i in reversed(range(EDGE)):
-        prior = [slab(cell, c, i - 1, 0, CB) for c in range(3)] if i else last
-        sum_x = each(add, now[0], y_prev(now[0]))
-        sum_y = each(add, now[1], prior[1])
-        sum_z = each(add, now[2], prior[2])
-        put_slab(emf, 0, i, 0, CB, each(quarter, sum_x, z_prev(sum_x)))
-        put_slab(emf, 1, i, 0, CB, each(quarter, sum_y, z_prev(sum_y)))
-        put_slab(emf, 2, i, 0, CB, each(quarter, sum_z, y_prev(sum_z)))
-        now = prior
+def lane_maps():
+    at, to = grid_of(WIDE, WIDE)
+    z_back = (to & ~15) | ((to - 1) & 15)
+    z_on = (to & ~15) | ((to + 1) & 15)
+    return at, to, (to - 16) & 255, (to + 16) & 255, z_back, z_on
+
+
+def corner_matrices():
+    at, to, y_back, _, z_back, _ = lane_maps()
+    same, y, z = at == to, at == y_back, at == z_back
+    both = at == ((z_back - 16) & 255)
+    return as_matrix(same | y | z | both, 0.25), as_matrix(same | z, 0.25), as_matrix(same | y, 0.25)
+
+
+def ahead_matrices():
+    at, to, _, y_on, _, z_on = lane_maps()
+    own = jnp.where(at == to, 1.0, 0.0)
+    return tuple((jnp.where(at == on, 1.0, 0.0) - own).astype(BF16) for on in (y_on, z_on))
+
+
+def stacked(load, c, slabs):
+    return jnp.concatenate([jnp.concatenate(load(c, i % EDGE), axis=1) for i in slabs], axis=0)
+
+
+def put_stacked(ref, c, slabs, value):
+    for k, i in enumerate(slabs):
+        part = value[k * CB : (k + 1) * CB]
+        put_slab(ref, c, i, 0, CB, (part[:, 0:128], part[:, 128:256]))
+
+
+def edges(cell, emf, corners):
+    load = lambda c, i: slab(cell, c, i, 0, CB)
+    for start in range(0, EDGE, CHUNK):
+        here, prior = range(start, start + CHUNK), range(start - 1, start - 1 + CHUNK)
+        put_stacked(emf, 0, here, mm_left(stacked(load, 0, here), corners[0]))
+        for c in (1, 2):
+            both = stacked(load, c, here) + stacked(load, c, prior)
+            put_stacked(emf, c, here, mm_left(both, corners[c]))
+
+
+def curls(emf, curl, aheads):
+    load = lambda c, i: slab(emf, c, i, 0, CB)
+    ahead_y, ahead_z = aheads
+    for start in range(0, EDGE, CHUNK):
+        here, far = range(start, start + CHUNK), range(start + 1, start + 1 + CHUNK)
+        ex, ey, ez = (stacked(load, c, here) for c in range(3))
+        put_stacked(curl, 0, here, mm_left(ez, ahead_y) - mm_left(ey, ahead_z))
+        put_stacked(curl, 1, here, mm_left(ex, ahead_z) - (stacked(load, 2, far) - ez))
+        put_stacked(curl, 2, here, (stacked(load, 1, far) - ey) - mm_left(ex, ahead_y))
 
 
 def face_of(ref, along, d):
@@ -261,7 +286,7 @@
 def first_kernel(
     cb, cv, fb, fv, far_pairs,
     send, emf_f, b_f,
-    b_c, v_c, pitched_b, v_f, pairs, out, sems,
+    b_c, v_c, pitched_b, v_f, cell_f, pairs, out, held_corners, held_restrict, sems,
 ):
     fine_copies = fetch_fine(fb, pitched_b, sems.at[0]) + fetch_fine(fv, v_f, sems.at[1])
     coarse_copies = coarse_parts(cb, cv, b_c, v_c, sems.at[pl.ds(2, 4)])
@@ -282,6 +307,12 @@
         picks.append(mm(chosen.astype(BF16), source.astype(BF16), nt).astype(BF16))
         meta = jnp.where(lane == k, jnp.sum(chosen * key, axis=1, keepdims=True), meta)
 
+    corners = corner_matrices()
+    for k in range(3):
+        held_corners[k] = corners[k]
+    restrict = [restrict_matrix(False), restrict_matrix(True)]
+    for k in range(2):
+        held_restrict[k] = restrict[k]
     for copy in fine_copies:
         copy.wait()
     held = {}
@@ -295,10 +326,10 @@
     top_fine = top_coarse = jnp.zeros((CB, 128), F32)
     for i in range(EDGE):
         centre, velocity = centres(fine_b, i), [fine_slab(v_f, c, i) for c in range(3)]
-        put_cell(emf_f, i, centre, velocity)
+        put_cell(cell_f, i, centre, velocity)
         top_fine = jnp.maximum(top_fine, speeds(centre, velocity))
-    edges(emf_f, emf_f)
-    restrict = [restrict_matrix(False), restrict_matrix(True)]
+    edges(cell_f, emf_f, held_corners)
+    restrict = held_restrict
     rows = []
     for d in range(3):
         planes = [face_of(emf_f, along, d) for along in TANGENT[d]]
@@ -327,16 +358,20 @@
     meta_copy.wait()
 
 
-def coarse_kernel(cb, cv, emf, planes, quads, b_c, v_c, sems):
+def coarse_kernel(cb, cv, emf_f, emf, planes, quads, b_c, curl_f, v_c, cell, held, sems):
     copies = coarse_parts(cb, cv, b_c, v_c, sems)
     for copy in sum(copies, []):
         copy.start()
+    corners, aheads = corner_matrices(), ahead_matrices()
+    curls(emf_f, held, aheads)
+    for c in range(3):
+        curl_f[c] = held[c]
     load_b, load_v = (lambda c, i, ref=ref: slab(ref, c, i, 0, CB) for ref in (b_c, v_c))
     for i in range(EDGE):
         wait_part(copies, i)
         centre = centres(load_b, i)
-        put_cell(emf, i, centre, [load_v(c, i) for c in range(3)])
-    edges(emf, emf)
+        put_cell(cell, i, centre, [load_v(c, i) for c in range(3)])
+    edges(cell, emf, corners)
     for d in range(3):
         for t in range(2):
             at = (d * 2 + t) * CB
@@ -456,23 +491,9 @@
         copy.wait()
 
 
-def curls(load, curl):
-    first = [load(c, 0) for c in range(3)]
-    now = first
-    turn = lambda p, q, r, s: (p - q) - (r - s)
-    for i in range(EDGE):
-        far = [load(c, i + 1) for c in range(3)] if i + 1 < EDGE else first
-        ex, ey, ez = now
-        put_slab(curl, 0, i, 0, CB, each(turn, y_next(ez), ez, z_next(ey), ey))
-        put_slab(curl, 1, i, 0, CB, each(turn, z_next(ex), ex, far[2], ez))
-        put_slab(curl, 2, i, 0, CB, each(turn, far[1], ey, y_next(ex), ex))
-        now = far
-
-
-def curl_kernel(emf_c, far_patch, masks, emf_f, curl_c, curl_f, patch, sems):
+def curl_kernel(emf_c, far_patch, masks, curl_c, patch, held, sems):
     load_patch = pltpu.make_async_copy(far_patch, patch, sems.at[0])
     load_patch.start()
-    curls(lambda c, i: slab(emf_f, c, i, 0, CB), curl_f)
     lane = lax.broadcasted_iota(jnp.int32, (CB, 128), 1)
 
     def pair(ref, first):
@@ -482,9 +503,7 @@
     planes = {(d, t): pair(patch, (d * 2 + t) * CB) for d in range(3) for t in range(2)}
     bits = [m.astype(jnp.int32) for m in pair(masks, 0)]
     hits = [[((m >> d) & 1).astype(F32) for m in bits] for d in range(3)]
-    ready = {}
-
-    def corrected(i):
+    for i in range(EDGE):
         now = {c: slab(emf_c, c, i, 0, CB) for c in range(3)}
         if i == 0:
             for t, c in enumerate(TANGENT[0]):
@@ -498,14 +517,9 @@
         for t, c in enumerate(TANGENT[2]):
             value = [pltpu.roll(p, turn, 1) for p in planes[2, t]]
             now[c] = each(jnp.where, there, value, now[c])
-        return now
-
-    def load(c, i):
-        if i not in ready:
-            ready[i] = corrected(i)
-        return ready[i][c]
-
-    curls(load, curl_c)
+        for c in range(3):
+            put_slab(held, c, i, 0, CB, now[c])
+    curls(held, curl_c, ahead_matrices())
 
 
 def update_kernel(
@@ -618,13 +632,30 @@
         first_kernel,
         [("hbm", (PEERS, 1, 384)), FIELD, FIELD],
         far(cb, cv, fb, fv, rows),
-        [field, field, pitched, pitched, small, pltpu.VMEM((PEERS, 1, 384), F32), sems((9,))],
+        [
+            field,
+            field,
+            pitched,
+            pitched,
+            field,
+            small,
+            pltpu.VMEM((PEERS, 1, 384), F32),
+            pltpu.VMEM((3, WIDE, WIDE), BF16),
+            pltpu.VMEM((2, 2 * WIDE, 128), BF16),
+            sems((9,)),
+        ],
     )
     got = lax.all_to_all(send, BLOCKS, 0, 0, tiled=True)
-    emf_c, planes, quads, b_c = call(
-        coarse_kernel, [FIELD, FACES, (3 * CB, WIDE), FIELD], far(cb, cv), [field, sems((4,))]
-    )
-    got, emf_c, planes, quads, b_c = lax.optimization_barrier((got, emf_c, planes, quads, b_c))
+    emf_c, planes, quads, b_c, curl_f = call(
+        coarse_kernel,
+        [FIELD, FACES, (3 * CB, WIDE), FIELD, FIELD],
+        far(cb, cv) + near(emf_f),
+        [field, field, field, sems((4,))],
+        {2: 4},
+    )
+    got, emf_c, planes, quads, b_c, curl_f = lax.optimization_barrier(
+        (got, emf_c, planes, quads, b_c, curl_f)
+    )
     back, patch, masks, top = call(
         answer_kernel,
         [("hbm", (PEERS, 1, 256)), ("hbm", FACES), (CB, WIDE), (1, 128)],
@@ -637,12 +668,12 @@
     for other in others:
         top = jnp.maximum(top, other)
     returned = lax.all_to_all(back, BLOCKS, 0, 0, tiled=True)
-    curl_c, curl_f = call(
+    (curl_c,) = call(
         curl_kernel,
-        [FIELD, FIELD],
-        near(emf_c) + far(patch) + near(masks, emf_f),
-        [pltpu.VMEM(FACES, F32), sems((1,))],
-        {0: 0, 3: 1},
+        [FIELD],
+        near(emf_c) + far(patch) + near(masks),
+        [pltpu.VMEM(FACES, F32), field, sems((1,))],
+        {0: 0},
     )
     new_c, new_f, picked, chosen = call(
         update_kernel,

time: 51 us -> 50.3 us (0.986)
  Pallas kernels: 14.2 us -> 12.3 us
  waiting for transfers between devices: 13.6 us -> 14.9 us
    pallas_call x6, Pallas kernels: 14.2 us -> 12.3 us  [call(): pl.pallas_call(kernel, out_shape=[pltpu.HBM(out[1], F32) if is_far else p...]
    all_to_all x1, waiting for transfers between devices: 6.86 us -> 7.86 us  [on_device(): got = lax.all_to_all(send, BLOCKS, 0, 0, tiled=True)]
  transfers between devices with their start and end apart: 5 -> 5, of which waited for: 2 -> 2; matrix products, arithmetic and copies ran while one was open for 0% -> 0% of each run, Pallas kernels for 13% -> 10%
where the time goes in v5:
time: 50.3 us; the launch traced here: 50 us
  starting transfers between devices  22.1 us (44%)
  waiting for transfers between devices  14.9 us (30%)
  Pallas kernels  12.3 us (24%)
  between operations  0.72 us (1%)
    all_to_all x1, starting transfers between devices, on_device(): got = lax.all_to_all(send, BLOCKS, 0, 0, tiled=True)  13 us
    pallas_call x6, Pallas kernels, call(): pl.pallas_call(kernel, out_shape=[pltpu.HBM(out[1], F32) if is_far else p...  12.3 us
    all_to_all x1, waiting for transfers between devices, on_device(): got = lax.all_to_all(send, BLOCKS, 0, 0, tiled=True)  7.86 us
    all_to_all x1, waiting for transfers between devices, on_device(): returned = lax.all_to_all(back, BLOCKS, 0, 0, tiled=True)  7.02 us
    all_to_all x1, starting transfers between devices, on_device(): returned = lax.all_to_all(back, BLOCKS, 0, 0, tiled=True)  5.24 us
    ppermute x3, starting transfers between devices, on_device(): lax.ppermute(top, 'gz', [(i, (i + k) % count) for i in range(count)])  3.85 us
  transfers between devices with their start and end apart: 5, of which 2 were waited for; matrix products, arithmetic and copies ran while one was open for 0% of the time, Pallas kernels for 10%

profile of v5, /device:TPU:1, one launch (start us, length us, event | category | flops | bytes accessed | tf_op | source)
XLA Modules:
  0.0 50.0 jit_solution(452908093240153407)
XLA Ops:
  0.6 3.9 %shard_map.76 = (f32[64,1,384]{2,1,0:T(1,128)}, f32[3,16,4096]{2,1,0:T(8,128)S(1)}, f32[3,16,4096]{2,1,0:T(8,128)S(1)}) custom-call(f32[3,16,4096]{2,1,0:T(8,128)} %bitcast.14, f32[3,16,4096]{2,1,0:T(8,128)} %bitcast.16, f32[12,96,128]{2,1,0:T(8,128)} %bitcast.18, f32[12,96,128]{2,1,0:T(8,128)} %bitcast.19, s32[6,1,32]{2,1,0:T(1,128)} %bitcast.21), custom_call_target="tpu_custom_call" | custom-call | tf_op jit(solution)/shard_map/pallas_call | solution.py:598
  4.6 13.0 %all-to-all-start = ((f32[64,1,384]{2,1,0:T(1,128)}), f32[64,1,384]{2,1,0:T(1,128)S(1)}, u32[]{:S(2)}, u32[]{:S(2)}) async-start(f32[64,1,384]{2,1,0:T(1,128)} %get-tuple-element.25), calls=%async_computation | async-start | bytes 196608 | tf_op jit(solution)/shard_map/all_to_all | solution.py:648
  17.6 2.3 %shard_map.77 = (f32[3,16,4096]{2,1,0:T(8,128)S(1)}, f32[96,256]{1,0:T(8,128)S(1)}, f32[48,256]{1,0:T(8,128)S(1)}, f32[3,16,4096]{2,1,0:T(8,128)S(1)}, f32[3,16,4096]{2,1,0:T(8,128)S(1)}) custom-call(f32[3,16,4096]{2,1,0:T(8,128)} %bitcast.15, f32[3,16,4096]{2,1,0:T(8,128)} %bitcast.17, ...), custom_call_target="tpu_custom_call", output_to_operand_aliasing={{4}: (2, {})} | custom-call | tf_op jit(solution)/shard_map/pallas_call | solution.py:598
  19.9 7.9 %all-to-all-done.got = f32[64,1,384]{2,1,0:T(1,128)S(1)} async-done(((f32[64,1,384]{2,1,0:T(1,128)}), f32[64,1,384]{2,1,0:T(1,128)S(1)}, u32[]{:S(2)}, u32[]{:S(2)}) %all-to-all-start) | async-done | bytes 98336 | tf_op jit(solution)/shard_map/all_to_all | solution.py:648
  27.7 2.2 %shard_map.78 = (f32[64,1,256]{2,1,0:T(1,128)}, f32[96,256]{1,0:T(8,128)}, f32[16,256]{1,0:T(8,128)S(1)}, f32[1,128]{1,0:T(1,128)S(1)}) custom-call(f32[64,1,384]{2,1,0:T(1,128)S(1)} %all-to-all-done.got, f32[96,256]{1,0:T(8,128)S(1)} %get-tuple-element.33.planes, f32[48,256]{1,0:T(8,128)S(1)} %get-tuple-element.34.quads_b), custom_call_target="tpu_custom_call" | custom-call | tf_op jit(solution)/shard_map/pallas_call | solution.py:598
  30.0 2.8 %collective-permute-start.2 = (f32[1,128]{1,0:T(1,128)S(1)}, f32[1,128]{1,0:T(1,128)S(1)}, u32[]{:S(2)}, u32[]{:S(2)}) collective-permute-start(f32[1,128]{1,0:T(1,128)S(1)} %get-tuple-element.35), channel_id=1, source_target_pairs={{0,3},{1,0},{2,1},{3,2},{4,7},{5,4},{6,5},{7,6},{8,11},{9,8},{10,9... | collective-permute-start | bytes 1544 | tf_op jit(solution)/shard_map/ppermute | solution.py:667
  32.8 0.3 collective-permute-start.1
  33.1 0.7 %collective-permute-start = (f32[1,128]{1,0:T(1,128)S(1)}, f32[1,128]{1,0:T(1,128)S(1)}, u32[]{:S(2)}, u32[]{:S(2)}) collective-permute-start(f32[1,128]{1,0:T(1,128)S(1)} %get-tuple-element.35), channel_id=1, source_target_pairs={{0,1},{1,2},{2,3},{3,0},{4,5},{5,6},{6,7},{7,4},{8,9},{9,10},{10,1... | collective-permute-start | bytes 1544 | tf_op jit(solution)/shard_map/ppermute | solution.py:667
  33.8 5.2 %all-to-all-start.1 = ((f32[64,1,256]{2,1,0:T(1,128)}), f32[64,1,256]{2,1,0:T(1,128)S(1)}, u32[]{:S(2)}, u32[]{:S(2)}) async-start(f32[64,1,256]{2,1,0:T(1,128)} %get-tuple-element.44), calls=%async_computation.1 | async-start | bytes 131072 | tf_op jit(solution)/shard_map/all_to_all | solution.py:670
  39.1 1.6 %shard_map.79.curl_c = f32[3,16,4096]{2,1,0:T(8,128)S(1)} custom-call(f32[3,16,4096]{2,1,0:T(8,128)S(1)} %get-tuple-element.36.emf_c, f32[96,256]{1,0:T(8,128)} %get-tuple-element.37.far_patch, f32[16,256]{1,0:T(8,128)S(1)} %get-tuple-element.38.masks), custom_call_target="tpu_custom_call", output_to_operand_aliasing={{}: (0, {})} | custom-call | tf_op jit(solution)/shard_map/pallas_call | solution.py:598
  40.6 0.0 collective-permute-done.2
  40.6 0.0 collective-permute-done.1
  40.7 0.0 collective-permute-done
  40.7 1.3 %shard_map.80 = (f32[3,16,4096]{2,1,0:T(8,128)}, f32[12,96,128]{2,1,0:T(8,128)}, f32[32,256]{1,0:T(8,128)S(1)}, f32[32,128]{1,0:T(8,128)S(1)}) custom-call(f32[1,128]{1,0:T(1,128)S(1)} %maximum_maximum_fusion.top, f32[3,16,4096]{2,1,0:T(8,128)S(1)} %shard_map.79.curl_c, f32[3,16,4096]{2,1,0:T(8,128)S(1)} %get-tuple-element.39.curl_f, ...), custom_call_target="tpu_custom_call" | custom-call | tf_op jit(solution)/shard_map/pallas_call | solution.py:598
  41.9 7.0 %all-to-all-done.1.got = f32[64,1,256]{2,1,0:T(1,128)S(1)} async-done(((f32[64,1,256]{2,1,0:T(1,128)}), f32[64,1,256]{2,1,0:T(1,128)S(1)}, u32[]{:S(2)}, u32[]{:S(2)}) %all-to-all-start.1) | async-done | bytes 65568 | tf_op jit(solution)/shard_map/all_to_all | solution.py:670
  49.0 1.0 %shard_map.81 = f32[32,256]{1,0:T(8,128)} custom-call(f32[64,1,256]{2,1,0:T(1,128)S(1)} %all-to-all-done.1.got, f32[1,128]{1,0:T(1,128)S(1)} %maximum_maximum_fusion.top, f32[32,256]{1,0:T(8,128)S(1)} %get-tuple-element.45.picked, f32[32,128]{1,0:T(8,128)S(1)} %get-tuple-element.46.chosen), custom_call_target="tpu_custom_call" | custom-call | tf_op jit(solution)/shard_map/pallas_call | solution.py:598
  (1 shorter events, 0.0 us)
Async XLA Ops:
  4.6 23.2 %all-to-all-start = ((f32[64,1,384]{2,1,0:T(1,128)}), f32[64,1,384]{2,1,0:T(1,128)S(1)}, u32[]{:S(2)}, u32[]{:S(2)}) async-start(f32[64,1,384]{2,1,0:T(1,128)} %get-tuple-element.25), calls=%async_computation | async-start | bytes 196608 | tf_op jit(solution)/shard_map/all_to_all | solution.py:648
  30.0 10.7 %collective-permute-start.2 = (f32[1,128]{1,0:T(1,128)S(1)}, f32[1,128]{1,0:T(1,128)S(1)}, u32[]{:S(2)}, u32[]{:S(2)}) collective-permute-start(f32[1,128]{1,0:T(1,128)S(1)} %get-tuple-element.35), channel_id=1, source_target_pairs={{0,3},{1,0},{2,1},{3,2},{4,7},{5,4},{6,5},{7,6},{8,11},{9,8},{10,9... | collective-permute-start | bytes 1544 | tf_op jit(solution)/shard_map/ppermute | solution.py:667
  32.8 7.9 %collective-permute-start.1 = (f32[1,128]{1,0:T(1,128)S(1)}, f32[1,128]{1,0:T(1,128)S(1)}, u32[]{:S(2)}, u32[]{:S(2)}) collective-permute-start(f32[1,128]{1,0:T(1,128)S(1)} %get-tuple-element.35), channel_id=1, source_target_pairs={{0,2},{1,3},{2,0},{3,1},{4,6},{5,7},{6,4},{7,5},{8,10},{9,11},{10,... | collective-permute-start | bytes 1544 | tf_op jit(solution)/shard_map/ppermute | solution.py:667
  33.1 7.5 %collective-permute-start = (f32[1,128]{1,0:T(1,128)S(1)}, f32[1,128]{1,0:T(1,128)S(1)}, u32[]{:S(2)}, u32[]{:S(2)}) collective-permute-start(f32[1,128]{1,0:T(1,128)S(1)} %get-tuple-element.35), channel_id=1, source_target_pairs={{0,1},{1,2},{2,3},{3,0},{4,5},{5,6},{6,7},{7,4},{8,9},{9,10},{10,1... | collective-permute-start | bytes 1544 | tf_op jit(solution)/shard_map/ppermute | solution.py:667
  33.8 15.1 %all-to-all-start.1 = ((f32[64,1,256]{2,1,0:T(1,128)}), f32[64,1,256]{2,1,0:T(1,128)S(1)}, u32[]{:S(2)}, u32[]{:S(2)}) async-start(f32[64,1,256]{2,1,0:T(1,128)} %get-tuple-element.44), calls=%async_computation.1 | async-start | bytes 131072 | tf_op jit(solution)/shard_map/all_to_all | solution.py:670

commit v6 on v5

--- a/solution.py
+++ b/solution.py
@@ -291,7 +291,7 @@
     fine_copies = fetch_fine(fb, pitched_b, sems.at[0]) + fetch_fine(fv, v_f, sems.at[1])
     coarse_copies = coarse_parts(cb, cv, b_c, v_c, sems.at[pl.ds(2, 4)])
     pairs_copy = pltpu.make_async_copy(far_pairs, pairs, sems.at[6])
-    for copy in [pairs_copy, *fine_copies, *sum(coarse_copies, [])]:
+    for copy in [pairs_copy, *fine_copies]:
         copy.start()
     idle = pl.ds(FB * PITCH, (CB - FB) * PITCH)
     pitched_b[idle, :] = jnp.zeros(((CB - FB) * PITCH, 128), F32)
@@ -307,6 +307,8 @@
         picks.append(mm(chosen.astype(BF16), source.astype(BF16), nt).astype(BF16))
         meta = jnp.where(lane == k, jnp.sum(chosen * key, axis=1, keepdims=True), meta)
 
+    for copy in sum(coarse_copies, []):
+        copy.start()
     corners = corner_matrices()
     for k in range(3):
         held_corners[k] = corners[k]
@@ -328,6 +330,8 @@
         centre, velocity = centres(fine_b, i), [fine_slab(v_f, c, i) for c in range(3)]
         put_cell(cell_f, i, centre, velocity)
         top_fine = jnp.maximum(top_fine, speeds(centre, velocity))
+    for copy in sum(coarse_copies, []):
+        copy.wait()
     edges(cell_f, emf_f, held_corners)
     restrict = held_restrict
     rows = []
@@ -338,24 +342,15 @@
     rows = jnp.concatenate(rows, axis=0)
     for k in range(2):
         out[:, 0, k * 128 : (k + 1) * 128] = mm_right(picks[k], rows)
-    rows_copy = pltpu.make_async_copy(
-        out.at[:, :, pl.ds(0, 256)], send.at[:, :, pl.ds(0, 256)], sems.at[7]
-    )
-    rows_copy.start()
-
     for i in range(EDGE):
-        wait_part(coarse_copies, i)
         centre = centres(lambda c, k: slab(b_c, c, k, 0, CB), i)
         top_coarse = jnp.maximum(top_coarse, speeds(centre, [slab(v_c, c, i, 0, CB) for c in range(3)]))
     top = jnp.max(jnp.maximum(top_fine, top_coarse), axis=0, keepdims=True)
     top = jnp.broadcast_to(jnp.max(top, axis=1, keepdims=True), (PEERS, 128))
     out[:, 0, 256:384] = jnp.where(lane < 2, meta, top)
-    meta_copy = pltpu.make_async_copy(
-        out.at[:, :, pl.ds(256, 128)], send.at[:, :, pl.ds(256, 128)], sems.at[8]
-    )
-    meta_copy.start()
-    rows_copy.wait()
-    meta_copy.wait()
+    send_copy = pltpu.make_async_copy(out, send, sems.at[7])
+    send_copy.start()
+    send_copy.wait()
 
 
 def coarse_kernel(cb, cv, emf_f, emf, planes, quads, b_c, curl_f, v_c, cell, held, sems):

time: 50.3 us -> 50.2 us (level)
  no operation moved by 1% of the time
where the time goes in v6:
time: 50.2 us; the launch traced here: 49.9 us
  starting transfers between devices  22.1 us (44%)
  waiting for transfers between devices  14.9 us (30%)
  Pallas kernels  12.2 us (24%)
  between operations  0.72 us (1%)
    all_to_all x1, starting transfers between devices, on_device(): got = lax.all_to_all(send, BLOCKS, 0, 0, tiled=True)  13 us
    pallas_call x6, Pallas kernels, call(): pl.pallas_call(kernel, out_shape=[pltpu.HBM(out[1], F32) if is_far else p...  12.2 us
    all_to_all x1, waiting for transfers between devices, on_device(): got = lax.all_to_all(send, BLOCKS, 0, 0, tiled=True)  7.85 us
    all_to_all x1, waiting for transfers between devices, on_device(): returned = lax.all_to_all(back, BLOCKS, 0, 0, tiled=True)  7.02 us
    all_to_all x1, starting transfers between devices, on_device(): returned = lax.all_to_all(back, BLOCKS, 0, 0, tiled=True)  5.24 us
    ppermute x3, starting transfers between devices, on_device(): lax.ppermute(top, 'gz', [(i, (i + k) % count) for i in range(count)])  3.87 us
  transfers between devices with their start and end apart: 5, of which 2 were waited for; matrix products, arithmetic and copies ran while one was open for 0% of the time, Pallas kernels for 10%

profile of v6, /device:TPU:1, one launch (start us, length us, event | category | flops | bytes accessed | tf_op | source)
XLA Modules:
  0.0 49.9 jit_solution(17350650547285686981)
XLA Ops:
  0.6 3.8 %shard_map.76 = (f32[64,1,384]{2,1,0:T(1,128)}, f32[3,16,4096]{2,1,0:T(8,128)S(1)}, f32[3,16,4096]{2,1,0:T(8,128)S(1)}) custom-call(f32[3,16,4096]{2,1,0:T(8,128)} %bitcast.14, f32[3,16,4096]{2,1,0:T(8,128)} %bitcast.16, f32[12,96,128]{2,1,0:T(8,128)} %bitcast.18, f32[12,96,128]{2,1,0:T(8,128)} %bitcast.19, s32[6,1,32]{2,1,0:T(1,128)} %bitcast.21), custom_call_target="tpu_custom_call" | custom-call | tf_op jit(solution)/shard_map/pallas_call | solution.py:593
  4.4 13.0 %all-to-all-start = ((f32[64,1,384]{2,1,0:T(1,128)}), f32[64,1,384]{2,1,0:T(1,128)S(1)}, u32[]{:S(2)}, u32[]{:S(2)}) async-start(f32[64,1,384]{2,1,0:T(1,128)} %get-tuple-element.25), calls=%async_computation | async-start | bytes 196608 | tf_op jit(solution)/shard_map/all_to_all | solution.py:643
  17.4 2.3 %shard_map.77 = (f32[3,16,4096]{2,1,0:T(8,128)S(1)}, f32[96,256]{1,0:T(8,128)S(1)}, f32[48,256]{1,0:T(8,128)S(1)}, f32[3,16,4096]{2,1,0:T(8,128)S(1)}, f32[3,16,4096]{2,1,0:T(8,128)S(1)}) custom-call(f32[3,16,4096]{2,1,0:T(8,128)} %bitcast.15, f32[3,16,4096]{2,1,0:T(8,128)} %bitcast.17, ...), custom_call_target="tpu_custom_call", output_to_operand_aliasing={{4}: (2, {})} | custom-call | tf_op jit(solution)/shard_map/pallas_call | solution.py:593
  19.7 7.9 %all-to-all-done.got = f32[64,1,384]{2,1,0:T(1,128)S(1)} async-done(((f32[64,1,384]{2,1,0:T(1,128)}), f32[64,1,384]{2,1,0:T(1,128)S(1)}, u32[]{:S(2)}, u32[]{:S(2)}) %all-to-all-start) | async-done | bytes 98336 | tf_op jit(solution)/shard_map/all_to_all | solution.py:643
  27.6 2.2 %shard_map.78 = (f32[64,1,256]{2,1,0:T(1,128)}, f32[96,256]{1,0:T(8,128)}, f32[16,256]{1,0:T(8,128)S(1)}, f32[1,128]{1,0:T(1,128)S(1)}) custom-call(f32[64,1,384]{2,1,0:T(1,128)S(1)} %all-to-all-done.got, f32[96,256]{1,0:T(8,128)S(1)} %get-tuple-element.33.planes, f32[48,256]{1,0:T(8,128)S(1)} %get-tuple-element.34.quads_b), custom_call_target="tpu_custom_call" | custom-call | tf_op jit(solution)/shard_map/pallas_call | solution.py:593
  29.8 2.8 %collective-permute-start.2 = (f32[1,128]{1,0:T(1,128)S(1)}, f32[1,128]{1,0:T(1,128)S(1)}, u32[]{:S(2)}, u32[]{:S(2)}) collective-permute-start(f32[1,128]{1,0:T(1,128)S(1)} %get-tuple-element.35), channel_id=1, source_target_pairs={{0,3},{1,0},{2,1},{3,2},{4,7},{5,4},{6,5},{7,6},{8,11},{9,8},{10,9... | collective-permute-start | bytes 1544 | tf_op jit(solution)/shard_map/ppermute | solution.py:662
  32.7 0.4 collective-permute-start.1
  33.0 0.7 %collective-permute-start = (f32[1,128]{1,0:T(1,128)S(1)}, f32[1,128]{1,0:T(1,128)S(1)}, u32[]{:S(2)}, u32[]{:S(2)}) collective-permute-start(f32[1,128]{1,0:T(1,128)S(1)} %get-tuple-element.35), channel_id=1, source_target_pairs={{0,1},{1,2},{2,3},{3,0},{4,5},{5,6},{6,7},{7,4},{8,9},{9,10},{10,1... | collective-permute-start | bytes 1544 | tf_op jit(solution)/shard_map/ppermute | solution.py:662
  33.7 5.2 %all-to-all-start.1 = ((f32[64,1,256]{2,1,0:T(1,128)}), f32[64,1,256]{2,1,0:T(1,128)S(1)}, u32[]{:S(2)}, u32[]{:S(2)}) async-start(f32[64,1,256]{2,1,0:T(1,128)} %get-tuple-element.44), calls=%async_computation.1 | async-start | bytes 131072 | tf_op jit(solution)/shard_map/all_to_all | solution.py:665
  38.9 1.6 %shard_map.79.curl_c = f32[3,16,4096]{2,1,0:T(8,128)S(1)} custom-call(f32[3,16,4096]{2,1,0:T(8,128)S(1)} %get-tuple-element.36.emf_c, f32[96,256]{1,0:T(8,128)} %get-tuple-element.37.far_patch, f32[16,256]{1,0:T(8,128)S(1)} %get-tuple-element.38.masks), custom_call_target="tpu_custom_call", output_to_operand_aliasing={{}: (0, {})} | custom-call | tf_op jit(solution)/shard_map/pallas_call | solution.py:593
  40.5 0.0 collective-permute-done.2
  40.5 0.0 collective-permute-done.1
  40.5 0.0 collective-permute-done
  40.6 1.3 %shard_map.80 = (f32[3,16,4096]{2,1,0:T(8,128)}, f32[12,96,128]{2,1,0:T(8,128)}, f32[32,256]{1,0:T(8,128)S(1)}, f32[32,128]{1,0:T(8,128)S(1)}) custom-call(f32[1,128]{1,0:T(1,128)S(1)} %maximum_maximum_fusion.top, f32[3,16,4096]{2,1,0:T(8,128)S(1)} %shard_map.79.curl_c, f32[3,16,4096]{2,1,0:T(8,128)S(1)} %get-tuple-element.39.curl_f, ...), custom_call_target="tpu_custom_call" | custom-call | tf_op jit(solution)/shard_map/pallas_call | solution.py:593
  41.8 7.0 %all-to-all-done.1.got = f32[64,1,256]{2,1,0:T(1,128)S(1)} async-done(((f32[64,1,256]{2,1,0:T(1,128)}), f32[64,1,256]{2,1,0:T(1,128)S(1)}, u32[]{:S(2)}, u32[]{:S(2)}) %all-to-all-start.1) | async-done | bytes 65568 | tf_op jit(solution)/shard_map/all_to_all | solution.py:665
  48.8 1.0 %shard_map.81 = f32[32,256]{1,0:T(8,128)} custom-call(f32[64,1,256]{2,1,0:T(1,128)S(1)} %all-to-all-done.1.got, f32[1,128]{1,0:T(1,128)S(1)} %maximum_maximum_fusion.top, f32[32,256]{1,0:T(8,128)S(1)} %get-tuple-element.45.picked, f32[32,128]{1,0:T(8,128)S(1)} %get-tuple-element.46.chosen), custom_call_target="tpu_custom_call" | custom-call | tf_op jit(solution)/shard_map/pallas_call | solution.py:593
  (1 shorter events, 0.0 us)
Async XLA Ops:
  4.4 23.1 %all-to-all-start = ((f32[64,1,384]{2,1,0:T(1,128)}), f32[64,1,384]{2,1,0:T(1,128)S(1)}, u32[]{:S(2)}, u32[]{:S(2)}) async-start(f32[64,1,384]{2,1,0:T(1,128)} %get-tuple-element.25), calls=%async_computation | async-start | bytes 196608 | tf_op jit(solution)/shard_map/all_to_all | solution.py:643
  29.8 10.7 %collective-permute-start.2 = (f32[1,128]{1,0:T(1,128)S(1)}, f32[1,128]{1,0:T(1,128)S(1)}, u32[]{:S(2)}, u32[]{:S(2)}) collective-permute-start(f32[1,128]{1,0:T(1,128)S(1)} %get-tuple-element.35), channel_id=1, source_target_pairs={{0,3},{1,0},{2,1},{3,2},{4,7},{5,4},{6,5},{7,6},{8,11},{9,8},{10,9... | collective-permute-start | bytes 1544 | tf_op jit(solution)/shard_map/ppermute | solution.py:662
  32.7 7.9 %collective-permute-start.1 = (f32[1,128]{1,0:T(1,128)S(1)}, f32[1,128]{1,0:T(1,128)S(1)}, u32[]{:S(2)}, u32[]{:S(2)}) collective-permute-start(f32[1,128]{1,0:T(1,128)S(1)} %get-tuple-element.35), channel_id=1, source_target_pairs={{0,2},{1,3},{2,0},{3,1},{4,6},{5,7},{6,4},{7,5},{8,10},{9,11},{10,... | collective-permute-start | bytes 1544 | tf_op jit(solution)/shard_map/ppermute | solution.py:662
  33.0 7.5 %collective-permute-start = (f32[1,128]{1,0:T(1,128)S(1)}, f32[1,128]{1,0:T(1,128)S(1)}, u32[]{:S(2)}, u32[]{:S(2)}) collective-permute-start(f32[1,128]{1,0:T(1,128)S(1)} %get-tuple-element.35), channel_id=1, source_target_pairs={{0,1},{1,2},{2,3},{3,0},{4,5},{5,6},{6,7},{7,4},{8,9},{9,10},{10,1... | collective-permute-start | bytes 1544 | tf_op jit(solution)/shard_map/ppermute | solution.py:662
  33.7 15.1 %all-to-all-start.1 = ((f32[64,1,256]{2,1,0:T(1,128)}), f32[64,1,256]{2,1,0:T(1,128)S(1)}, u32[]{:S(2)}, u32[]{:S(2)}) async-start(f32[64,1,256]{2,1,0:T(1,128)} %get-tuple-element.44), calls=%async_computation.1 | async-start | bytes 131072 | tf_op jit(solution)/shard_map/all_to_all | solution.py:665
